TPU v7x, 256 devices: a whole 4x4x8 slice. The times are simulated.
256 devices in a mesh: img: 16 (over y, x), row: 16 (over z, core).
Axes of the slice: x: 4, y: 4, z: 8, core: 2. Of those that a mesh axis runs over, the one named last changes fastest.
Arguments:
- latent: bfloat16 [1024, 128, 512], P(('img', 'row')), parts along dimension 0, may hold values from -8 to 8
- attn_gain: float32 [512], replicated, may hold values from 0.5 to 1.5
- attn_shift: float32 [512], replicated, may hold values from -3 to 3
- w_query: bfloat16 [512, 512], replicated, may hold values from -2 to 2
- w_key: bfloat16 [512, 512], replicated, may hold values from -2 to 2
- w_value: bfloat16 [512, 512], replicated, may hold values from -0.25 to 0.25
- w_out: bfloat16 [512, 512], replicated, may hold values from -0.25 to 0.25
- conv_gain: float32 [512], replicated, may hold values from 0.5 to 1.5
- conv_shift: float32 [512], replicated, may hold values from -3 to 3
- w_conv: bfloat16 [3, 3, 512, 512], replicated, may hold values from -0.09375 to 0.09375
- conv_bias: float32 [512], replicated, may hold values from -3 to 3
Outputs:
- encoded: bfloat16 [1024, 128, 512], P(('img', 'row')), parts along dimension 0
There are 16 independent parts, one for each index of `img`. A program takes and returns all parts, laid end to end along the dimension named above; an argument that names none is the same for every part. Nothing has to cross between parts.
All inputs are finite; a program needn't handle non-finite values.
Results may differ from a plain program's by a relative error of at most 0.011.
Values may be sent and summed in bfloat16 or wider, within the bound.
No kernel may reach another device: no remote copies, remote signals or barrier semaphores. Data moves between devices by JAX's collectives and lax.ppermute only.
A program may use at most 128 MiB of HBM per device.

v0:
```python
import jax
import jax.numpy as jnp
from jax import lax
from jax.sharding import PartitionSpec as P

C = 512
GROUPS = 32
W = 128


epsilon = 1e-06


def copy_for_each(shard, axis):
    copies = jnp.broadcast_to(shard, (lax.axis_size(axis), *shard.shape))
    return lax.all_to_all(copies, axis, split_axis=0, concat_axis=0, tiled=True)


def taken_together(shard, axis):
    return copy_for_each(shard, axis).sum(axis=0)


def together(arrays, axis):
    line, at, done = (jnp.concatenate([a.reshape(-1) for a in arrays]), 0, [])
    total = taken_together(line, axis)
    for a in arrays:
        done.append(total[at : at + a.size].reshape(a.shape))
        at += a.size
    return tuple(done)


def with_halo(cells, sides, width):
    for axis, dim in sides:
        count = lax.axis_size(axis)
        ends = count - 1
        head = lax.slice_in_dim(cells, 0, width, axis=dim)
        tail = lax.slice_in_dim(cells, cells.shape[dim] - width, cells.shape[dim], axis=dim)
        cells = jnp.concatenate(
            [
                lax.ppermute(tail, axis, [(i, (i + 1) % count) for i in range(ends)]),
                cells,
                lax.ppermute(head, axis, [((i + 1) % count, i) for i in range(ends)]),
            ],
            axis=dim,
        )
    return cells


def group_stats(grouped, count):
    first, second = together(
        (jnp.sum(grouped, axis=(0, 2)), jnp.sum(grouped * grouped, axis=(0, 2))), "row"
    )
    centre = first / count
    spread = second / count - centre * centre
    return (centre, spread)


def group_norm(field, gain, shift):
    grouped = field.reshape(field.shape[0], GROUPS, C // GROUPS)
    count = field.shape[0] * lax.axis_size("row") * (C // GROUPS)
    centre, spread = group_stats(grouped, count)
    normed = (grouped - centre[None, :, None]) * lax.rsqrt(spread + epsilon)[None, :, None]
    return normed.reshape(field.shape) * gain + shift


def attend(carry, key_piece, value_piece, queries):
    maxima, denominator, accumulated = carry
    scaling = 1.0 / jnp.sqrt(jnp.float32(C))
    scores = (
        jnp.einsum("qc,kc->qk", queries, key_piece, preferred_element_type=jnp.float32) * scaling
    )
    newest = jnp.maximum(maxima, jnp.max(scores, axis=1))
    expo = jnp.exp(scores - newest[:, None])
    denominator = jnp.sum(expo, axis=1)
    accumulated = jnp.dot(
        expo.astype(jnp.bfloat16), value_piece, preferred_element_type=jnp.float32
    )
    return (newest, denominator, accumulated)


def local(
    latent,
    attn_gain,
    attn_shift,
    w_query,
    w_key,
    w_value,
    w_out,
    conv_gain,
    conv_shift,
    w_conv,
    conv_bias,
):
    local_rows = latent.shape[0]
    positions = latent.reshape(local_rows * W, C)
    normed = group_norm(positions.astype(jnp.float32), attn_gain, attn_shift).astype(jnp.bfloat16)
    queries = jnp.dot(normed, w_query, preferred_element_type=jnp.float32).astype(jnp.bfloat16)
    count_rows = positions.shape[0]
    start_carry = (
        jnp.full((count_rows,), -1e30, jnp.float32),
        jnp.zeros((count_rows,), jnp.float32),
        jnp.zeros((count_rows, C), jnp.float32),
    )
    piece = lax.all_gather(normed, "row", axis=0, tiled=True)
    key_piece = jnp.dot(piece, w_key, preferred_element_type=jnp.float32).astype(jnp.bfloat16)
    value_piece = jnp.dot(piece, w_value, preferred_element_type=jnp.float32).astype(jnp.bfloat16)
    maxima, denominator, accumulated = attend(start_carry, key_piece, value_piece, queries)
    attended = (accumulated / denominator[:, None]).astype(jnp.bfloat16)
    hidden = (
        positions.astype(jnp.float32) + jnp.dot(attended, w_out, preferred_element_type=jnp.float32)
    ).astype(jnp.bfloat16)
    activated = jax.nn.silu(group_norm(hidden.astype(jnp.float32), conv_gain, conv_shift)).astype(
        jnp.bfloat16
    )
    activated = activated.reshape(local_rows, W, C)
    bordered = with_halo(activated, (("row", 0),), 1)
    padded = jnp.pad(bordered, ((0, 0), (1, 1), (0, 0)))
    convolved = jnp.zeros((local_rows * W, C), jnp.float32)
    for row_tap in range(3):
        for col_tap in range(3):
            window = padded[row_tap : row_tap + local_rows, col_tap : col_tap + W].reshape(
                local_rows * W, C
            )
            convolved = convolved + jnp.dot(
                window, w_conv[row_tap, col_tap], preferred_element_type=jnp.float32
            )
    encoded = hidden.astype(jnp.float32) + (convolved + conv_bias)
    return encoded.astype(jnp.bfloat16).reshape(local_rows, W, C)


def solution(mesh):
    in_specs = (P(("img", "row"), None, None), P(), P(), P(), P(), P(), P(), P(), P(), P(), P())
    out_specs = P(("img", "row"), None, None)
    return jax.shard_map(local, mesh=mesh, in_specs=in_specs, out_specs=out_specs, check_vma=False)
```

profile of v0, /device:TPU:1, one launch (start us, length us, event | category | flops | bytes accessed | tf_op | source)
XLA Modules:
  0.0 157.1 jit_solution(7887998248014053439)
XLA Ops:
  6.5 1.3 convert_reduce_fusion.1
  8.0 0.1 reduce_sum.75
  8.1 0.1 reduce_sum.96
  8.3 16.8 %all_to_all.12 = f32[16,1,64]{2,1,0:T(1,128)S(1)} all-to-all(f32[16,1,64]{2,1,0:T(1,128)S(1)} %broadcast_in_dim.6), channel_id=1, replica_groups=mesh['img'=16,'row'=16] {'row'}, dimensions={0} | all-to-all | bytes 8192 | tf_op jit(solution)/shard_map/all_to_all | solution.py:16
  25.3 0.1 sub.41
  25.5 2.1 %fusion.31 = bf16[512,512]{1,0:T(8,128)(2,1)} fusion(bf16[4,128,512]{2,1,0:T(8,128)(2,1)} %param.11, f32[512]{0:T(512)} %param.13, f32[512]{0:T(512)} %param.12, f32[512]{0:T(512)S(1)} %mul.69, f32[512]{0:T(512)S(1)} %sub.41), kind=kLoop, calls=%fused_computation.46 | loop fusion | flops 1572864 | bytes 1056768 | tf_op jit(solution)/shard_map/convert_element_type | solution.py:96
  27.6 1.6 %convolution_convert_fusion.2 = bf16[512,512]{1,0:T(8,128)(2,1)S(1)} fusion(bf16[512,512]{1,0:T(8,128)(2,1)} %fusion.31, bf16[512,512]{1,0:T(8,128)(2,1)} %param.14), kind=kOutput, calls=%fused_computation.28 | convolution fusion | flops 268697600 | bytes 1572864 | tf_op jit(solution)/shard_map/dot_general | solution.py:97
  29.2 51.1 %all-gather.2.cloned.1.call-done = bf16[8192,512]{1,0:T(8,128)(2,1)} async-done(((bf16[512,512]{1,0:T(8,128)(2,1)}), bf16[8192,512]{1,0:T(8,128)(2,1)}) %all-gather.2.cloned.1.call-update) | async-done | bytes 8388624 | tf_op jit(solution)/shard_map/all_gather | solution.py:104
  80.4 14.5 %multiply_reduce_fusion = (f32[512]{0:T(512)S(1)}, f32[512,8192]{1,0:T(8,128)}) fusion(bf16[512,512]{1,0:T(8,128)(2,1)S(1)} %convolution_convert_fusion.2, bf16[8192,512]{1,0:T(8,128)(2,1)} %all-gather.2.cloned.1.call-done, bf16[512,512]{1,0:T(8,128)(2,1)S(1)} %copy-done), kind=kOutput, calls=%fused_computation.1 | convolution fusion | flops 8602517504 | bytes 26216448 | tf_op jit(solution)/shard_map/qc,kc->qk/dot_general | solution.py:70
  94.9 8.7 %fusion = f32[512]{0:T(512)S(1)} fusion(f32[512,8192]{1,0:T(8,128)} %get-tuple-element.24, f32[512]{0:T(512)S(1)} %broadcast_maximum_fusion), kind=kLoop, calls=%fused_computation.2 | loop fusion | flops 12582400 | bytes 16781312 | tf_op jit(solution)/shard_map/reduce_sum | solution.py:74
  103.6 17.2 %fusion.15 = bf16[512,512]{1,0:T(8,128)(2,1)S(1)} fusion(bf16[8192,512]{1,0:T(8,128)(2,1)} %all-gather.2.cloned.1.call-done, bf16[512,512]{1,0:T(8,128)(2,1)S(1)} %copy-done.5, f32[512,8192]{1,0:T(8,128)} %get-tuple-element.24, f32[512]{0:T(512)S(1)} %broadcast_maximum_fusion, f32[512]{0:T(512)S(1)} %fusion), kind=kOutput, calls=%fused_computation.31 | convolution fusion | flops 8607236096 | bytes 26218496 | tf_op jit(solution)/shard_map/dot_general | solution.py:75
  120.8 0.5 convert_reduce_fusion
  121.4 0.3 reduce_sum.101
  121.8 0.1 reduce_sum.104
  122.0 11.4 %all_to_all.13 = f32[16,1,64]{2,1,0:T(1,128)S(1)} all-to-all(f32[16,1,64]{2,1,0:T(1,128)S(1)} %broadcast_in_dim.8), channel_id=1, replica_groups=mesh['img'=16,'row'=16] {'row'}, dimensions={0} | all-to-all | bytes 8192 | tf_op jit(solution)/shard_map/all_to_all | solution.py:16
  133.8 0.4 fusion.27
  134.2 2.7 %collective-permute-start = (bf16[1,128,512]{2,1,0:T(8,128)(2,1)S(1)}, bf16[1,128,512]{2,1,0:T(8,128)(2,1)S(1)}, u32[]{:S(2)}, u32[]{:S(2)}) collective-permute-start(bf16[1,128,512]{2,1,0:T(8,128)(2,1)S(1)} %get-tuple-element.17), channel_id=1, source_target_pairs={{0,1},{1,2},{2,3},{3,4},{4,5},{5,6},{6,7},{7,8},{8,9},{9,10},{10,1... | collective-permute-start | bytes 393224 | tf_op jit(solution)/shard_map/ppermute | solution.py:40
  137.0 1.9 %collective-permute-start.1 = (bf16[1,128,512]{2,1,0:T(8,128)(2,1)S(1)}, bf16[1,128,512]{2,1,0:T(8,128)(2,1)S(1)}, u32[]{:S(2)}, u32[]{:S(2)}) collective-permute-start(bf16[1,128,512]{2,1,0:T(8,128)(2,1)S(1)} %get-tuple-element.18), channel_id=1, source_target_pairs={{1,0},{2,1},{3,2},{4,3},{5,4},{6,5},{7,6},{8,7},{9,8},{10,9},{11,1... | collective-permute-start | bytes 393224 | tf_op jit(solution)/shard_map/ppermute | solution.py:42
  138.9 4.3 %collective-permute-done.1 = bf16[1,128,512]{2,1,0:T(8,128)(2,1)S(1)} collective-permute-done((bf16[1,128,512]{2,1,0:T(8,128)(2,1)S(1)}, bf16[1,128,512]{2,1,0:T(8,128)(2,1)S(1)}, u32[]{:S(2)}, u32[]{:S(2)}) %collective-permute-start.1) | collective-permute-done | bytes 131104 | tf_op jit(solution)/shard_map/ppermute | solution.py:42
  143.3 0.2 fusion.36
  143.5 0.4 fusion.58
  143.9 1.7 %fusion.46 = f32[512,512]{1,0:T(8,128)S(1)} fusion(bf16[512,512]{1,0:T(8,128)(2,1)S(1)} %bitcast.82, bf16[3,3,512,512]{3,2,1,0:T(8,128)(2,1)} %param.20), kind=kOutput, calls=%fused_computation.65 | convolution fusion | flops 268435456 | bytes 2097152 | tf_op jit(solution)/shard_map/dot_general | solution.py:124
  145.6 0.1 pad_maximum_fusion
  145.7 0.1 slice-done.1
  145.8 0.4 convolution_add_fusion.6
  146.3 0.4 convolution_add_fusion.5
  146.7 0.4 convolution_add_fusion.4
  147.2 0.4 convolution_add_fusion.3
  147.6 0.4 fusion.37
  148.1 0.4 convolution_add_fusion.2
  148.5 0.4 convolution_add_fusion.1
  149.0 1.3 fusion.10
  (42 shorter events, 1.3 us)
Async XLA Ops:
  6.5 73.8 %copy-start = (bf16[512,512]{1,0:T(8,128)(2,1)S(1)}, bf16[512,512]{1,0:T(8,128)(2,1)}, u32[]{:S(2)}) copy-start(bf16[512,512]{1,0:T(8,128)(2,1)} %param.15) | copy-start | bytes 1572868
  6.5 73.8 %all-gather.2.cloned.1.call-start = ((), (), s32[]{:S(2)}) async-start(), calls=%async_computation.2 | async-start | bytes 8912896 | tf_op jit(solution)/shard_map/all_gather | solution.py:104
  94.9 8.7 %copy-start.5 = (bf16[512,512]{1,0:T(8,128)(2,1)S(1)}, bf16[512,512]{1,0:T(8,128)(2,1)}, u32[]{:S(2)}) copy-start(bf16[512,512]{1,0:T(8,128)(2,1)} %param.16) | copy-start | bytes 1572868
  103.6 17.2 %copy-start.1 = (bf16[4,128,512]{2,1,0:T(8,128)(2,1)S(1)}, bf16[4,128,512]{2,1,0:T(8,128)(2,1)}, u32[]{:S(2)}) copy-start(bf16[4,128,512]{2,1,0:T(8,128)(2,1)} %param.11) | copy-start | bytes 1572868
  103.6 17.2 %copy-start.6 = (bf16[512,512]{1,0:T(8,128)(2,1)S(1)}, bf16[512,512]{1,0:T(8,128)(2,1)}, u32[]{:S(2)}) copy-start(bf16[512,512]{1,0:T(8,128)(2,1)} %param.17) | copy-start | bytes 1572868
  103.6 30.2 %copy-start.2 = (f32[512]{0:T(512)S(1)}, f32[512]{0:T(512)}, u32[]{:S(2)}) copy-start(f32[512]{0:T(512)} %param.19) | copy-start | bytes 6148
  103.6 30.2 %copy-start.3 = (f32[512]{0:T(512)S(1)}, f32[512]{0:T(512)}, u32[]{:S(2)}) copy-start(f32[512]{0:T(512)} %param.18) | copy-start | bytes 6148
  120.8 24.9 %slice-start = ((s8[4718592]{0:T(1024)(128)(4,1)}), s8[524288]{0:T(1024)(128)(4,1)S(1)}, s32[]{:S(2)}) async-start(s8[4718592]{0:T(1024)(128)(4,1)} %bitcast.74), calls=%async_computation.3 | async-start | bytes 1048576
  134.2 4.7 %collective-permute-start = (bf16[1,128,512]{2,1,0:T(8,128)(2,1)S(1)}, bf16[1,128,512]{2,1,0:T(8,128)(2,1)S(1)}, u32[]{:S(2)}, u32[]{:S(2)}) collective-permute-start(bf16[1,128,512]{2,1,0:T(8,128)(2,1)S(1)} %get-tuple-element.17), channel_id=1, source_target_pairs={{0,1},{1,2},{2,3},{3,4},{4,5},{5,6},{6,7},{7,8},{8,9},{9,10},{10,1... | collective-permute-start | bytes 393224 | tf_op jit(solution)/shard_map/ppermute | solution.py:40
  137.0 6.3 %collective-permute-start.1 = (bf16[1,128,512]{2,1,0:T(8,128)(2,1)S(1)}, bf16[1,128,512]{2,1,0:T(8,128)(2,1)S(1)}, u32[]{:S(2)}, u32[]{:S(2)}) collective-permute-start(bf16[1,128,512]{2,1,0:T(8,128)(2,1)S(1)} %get-tuple-element.18), channel_id=1, source_target_pairs={{1,0},{2,1},{3,2},{4,3},{5,4},{6,5},{7,6},{8,7},{9,8},{10,9},{11,1... | collective-permute-start | bytes 393224 | tf_op jit(solution)/shard_map/ppermute | solution.py:42
  143.5 2.3 %slice-start.1 = ((s8[4718592]{0:T(1024)(128)(4,1)}), s8[4194304]{0:T(1024)(128)(4,1)S(1)}, s32[]{:S(2)}) async-start(s8[4718592]{0:T(1024)(128)(4,1)} %bitcast.74), calls=%async_computation.4 | async-start | bytes 8388608
  146.3 2.7 %copy-start.4 = (f32[512]{0:T(512)S(1)}, f32[512]{0:T(512)}, u32[]{:S(2)}) copy-start(f32[512]{0:T(512)} %param.21) | copy-start | bytes 6148
Sparse Core Ops, SparseCore 0:
  27.7 52.6 all-gather.1
where the time goes:
time: 157 us
  waiting for transfers between devices  55.5 us (35%)
  matrix products  39.9 us (25%)
  blocking collectives  28.2 us (18%)
  other arithmetic  13.7 us (9%)
  between operations  13.6 us (9%)
  starting transfers between devices  4.64 us (3%)
    all_gather x1, waiting for transfers between devices, local(): piece = lax.all_gather(normed, 'row', axis=0, tiled=True)  51.1 us
    all_to_all x2, blocking collectives, copy_for_each(): return lax.all_to_all(copies, axis, split_axis=0, concat_axis=0, tiled=True)  28.2 us
    dot_general x1, matrix products, attend(): jnp.dot(expo.astype(jnp.bfloat16), value_piece, preferred_element_type=jn...  17.2 us
    dot_general x1, matrix products, attend(): jnp.einsum('qc,kc->qk', queries, key_piece, preferred_element_type=jnp.fl...  14.5 us
    reduce_sum x1, other arithmetic, attend(): denominator = jnp.sum(expo, axis=1)  8.68 us
    dot_general x9, matrix products, local(): jnp.dot(window, w_conv[row_tap, col_tap], preferred_element_type=jnp.floa...  6.07 us
    ppermute x1, waiting for transfers between devices, with_halo(): lax.ppermute(head, axis, [((i + 1) % count, i) for i in range(ends)])  4.35 us
  transfers between devices with their start and end apart: 3, of which 2 were waited for; matrix products, arithmetic and copies ran while one was open for 1% of the time, Pallas kernels for 0%

commit v1 on v0

v1 whole, which is shorter than its diff:
```python
import jax
import jax.numpy as jnp
from jax import lax
from jax.experimental import pallas as pl
from jax.experimental.pallas import tpu as pltpu
from jax.sharding import PartitionSpec as P

C = 512
GROUPS = 32
W = 128
LANES = 128
EPS = 1e-06
LOG2E = 1.4426950408889634
VMEM = pl.BlockSpec(memory_space=pltpu.VMEM)
SMEM = pl.BlockSpec(memory_space=pltpu.SMEM)
F32 = jnp.float32
BF16 = jnp.bfloat16
MIB = 1024 * 1024


def call(kernel, outs, specs, args, flops, vmem_mib=16, scratch=(), aliases=None):
    moved = sum(a.size * a.dtype.itemsize for a in args)
    return pl.pallas_call(
        kernel,
        out_shape=outs,
        in_specs=specs,
        out_specs=jax.tree.map(lambda _: VMEM, outs),
        scratch_shapes=list(scratch),
        input_output_aliases=aliases or {},
        cost_estimate=pl.CostEstimate(flops=flops, bytes_accessed=moved, transcendentals=0),
        compiler_params=pltpu.CompilerParams(vmem_limit_bytes=vmem_mib * MIB),
    )(*args)


def group_sum(v):
    lane = lax.broadcasted_iota(jnp.int32, v.shape, 1)
    for k in (1, 2, 4, 8):
        up = pltpu.roll(v, k, 1)
        down = pltpu.roll(v, C - k, 1)
        v = v + jnp.where((lane & k) != 0, up, down)
    return v


def write_stats(field, out_ref):
    rows = field.shape[0]
    share = C // GROUPS
    mean = group_sum(jnp.broadcast_to(jnp.sum(field, 0, keepdims=True), (8, C))) * (
        1.0 / (rows * share)
    )
    offset = field - mean[0:1]
    spread = group_sum(jnp.broadcast_to(jnp.sum(offset * offset, 0, keepdims=True), (8, C)))
    for i in range(C // LANES):
        cut = slice(i * LANES, (i + 1) * LANES)
        out_ref[i : i + 1, :] = mean[0:1, cut]
        out_ref[i + 4 : i + 5, :] = spread[0:1, cut]


def affine(stats, gain, shift, rows):
    count = stats.shape[0]
    local = rows * (C // GROUPS)
    means = stats[:, 0:4, :]
    mean = jnp.sum(means, 0) * (1.0 / count)
    offset = means - mean[None]
    total = jnp.sum(stats[:, 4:8, :], 0) + local * jnp.sum(offset * offset, 0)
    inverse = lax.rsqrt(total * (1.0 / (local * count)) + EPS)
    flat = lambda v: jnp.concatenate([v[i : i + 1] for i in range(4)], axis=1)
    scale = flat(inverse) * gain
    return scale, shift - flat(mean) * scale


def stats_kernel(x_ref, out_ref):
    write_stats(x_ref[...].astype(F32), out_ref)


def query_kernel(x_ref, stats_ref, gain_ref, shift_ref, wqk_ref, q_ref, coef_ref):
    scale, shift = affine(stats_ref[...], gain_ref[...], shift_ref[...], x_ref.shape[0])
    coef_ref[0:1, :] = scale
    coef_ref[1:2, :] = shift
    normed = (x_ref[...].astype(F32) * scale + shift).astype(BF16)
    q = jnp.dot(normed, wqk_ref[...], preferred_element_type=F32)
    q_ref[...] = (q * (scale * (LOG2E / C**0.5))).astype(BF16)


BLOCK = 256


def attend_kernel(first, last, own_ref, other_ref, ka_ref, kb_ref, *refs):
    if first:
        state, outs = None, refs
    else:
        state, outs = refs[:3], refs[3:]
    half = own_ref.shape[0]
    blocks = 2 * half // BLOCK
    keys = [ka_ref, kb_ref]

    def scores(i):
        src = own_ref if i * BLOCK < half else other_ref
        at = (i * BLOCK) % half
        q = src[at : at + BLOCK, :]
        return [
            lax.dot_general(q, k[...], (((1,), (1,)), ((), ())), preferred_element_type=F32)
            for k in keys
        ]

    ahead = scores(0)
    for i in range(blocks):
        s = ahead
        if i + 1 < blocks:
            ahead = scores(i + 1)
        at = slice(i * BLOCK, (i + 1) * BLOCK)
        tiles = [t[:, j : j + LANES] for t in s for j in range(0, t.shape[1], LANES)]
        top = tiles[0]
        for t in tiles[1:]:
            top = jnp.maximum(top, t)
        top = jnp.broadcast_to(jnp.max(top, axis=1, keepdims=True), (BLOCK, LANES))
        if not first:
            before = state[1][at, :]
            top = jnp.maximum(before, top)
        part = None
        acc = None
        n = 0
        for t, k in zip(s, keys):
            width = t.shape[1] // LANES
            probs = []
            for _ in range(width):
                p = jnp.exp2(tiles[n] - top).astype(BF16)
                probs.append(p)
                p32 = p.astype(F32)
                part = p32 if part is None else part + p32
                n += 1
            d = jnp.dot(jnp.concatenate(probs, axis=1), k[...], preferred_element_type=F32)
            acc = d if acc is None else acc + d
        if not first:
            fade = jnp.exp2(before - top)
            part = part + state[2][at, :] * fade
            acc = acc + state[0][at, :] * jnp.concatenate([fade] * (C // LANES), axis=1)
        if last:
            o = outs[0] if i * BLOCK < half else outs[1]
            to = slice((i * BLOCK) % half, (i * BLOCK) % half + BLOCK)
            o[to, 0:C] = acc
            total = jnp.broadcast_to(jnp.sum(part, axis=1, keepdims=True), (BLOCK, LANES))
            lane = lax.broadcasted_iota(jnp.int32, (BLOCK, LANES), 1)
            o[to, C : C + LANES] = jnp.where(lane < 64, top, total)
        else:
            outs[0][at, :] = acc
            outs[1][at, :] = top
            outs[2][at, :] = part


def attend(own, other, ka, kb, state, last):
    half = own.shape[0]
    first = state is None
    if last:
        outs = [jax.ShapeDtypeStruct((half, C + LANES), F32)] * 2
    else:
        outs = [
            jax.ShapeDtypeStruct((2 * half, C), F32),
            jax.ShapeDtypeStruct((2 * half, LANES), F32),
            jax.ShapeDtypeStruct((2 * half, LANES), F32),
        ]
    args = [own, other, ka, kb] + ([] if first else list(state))
    aliases = {} if first or last else {4: 0, 5: 1, 6: 2}

    def kernel(*refs):
        attend_kernel(first, last, *refs)

    flops = 4 * 2 * half * C * (ka.shape[0] + kb.shape[0])
    return call(kernel, outs, [VMEM] * len(args), args, flops, 20, aliases=aliases)


def output_kernel(a_ref, b_ref, x_ref, coef_ref, wvo_ref, hidden_ref, stats_ref):
    one = slice(C, C + 1)
    two = slice(C + LANES - 1, C + LANES)
    ma, mb = a_ref[:, one], b_ref[:, one]
    m = jnp.maximum(ma, mb)
    wa, wb = jnp.exp2(ma - m), jnp.exp2(mb - m)
    inverse = 1.0 / (a_ref[:, two] * wa + b_ref[:, two] * wb)
    mixed = a_ref[:, 0:C] * (wa * inverse) + b_ref[:, 0:C] * (wb * inverse)
    normed = (mixed * coef_ref[0:1, :] + coef_ref[1:2, :]).astype(BF16)
    hidden = x_ref[...].astype(F32) + jnp.dot(normed, wvo_ref[...], preferred_element_type=F32)
    hidden = hidden.astype(BF16)
    hidden_ref[...] = hidden
    write_stats(hidden.astype(F32), stats_ref)


def conv_kernel(
    flags_ref, h_ref, top_ref, bottom_ref, stats_ref, gain_ref, shift_ref, w_ref, bias_ref,
    out_ref, left_ref, mid_ref, right_ref,
):
    rows = h_ref.shape[0]
    scale, shift = affine(stats_ref[...], gain_ref[...], shift_ref[...], rows)

    def activate(f, at, keep):
        v = f.astype(F32) * scale + shift
        v = v / (1.0 + jnp.exp(-v))
        if keep is not None:
            v = jnp.where(keep, v, 0.0)
        column = lax.broadcasted_iota(jnp.int32, v.shape, 0) % W
        mid_ref[at : at + W, :] = v.astype(BF16)
        before = jnp.where(column == 0, 0.0, pltpu.roll(v, 1, 0))
        left_ref[at : at + W, :] = before.astype(BF16)
        after = jnp.where(column == W - 1, 0.0, pltpu.roll(v, W - 1, 0))
        right_ref[at : at + W, :] = after.astype(BF16)

    activate(top_ref[...], 0, flags_ref[0] > 0)
    for r in range(rows // W):
        activate(h_ref[r * W : (r + 1) * W, :], (r + 1) * W, None)
    activate(bottom_ref[...], rows + W, flags_ref[1] > 0)
    for r in range(0, rows, BLOCK):
        for n in range(0, C, BLOCK):
            total = None
            for dy in range(3):
                for dx, src in enumerate((left_ref, mid_ref, right_ref)):
                    d = jnp.dot(
                        src[r + dy * W : r + dy * W + BLOCK, :],
                        w_ref[3 * dy + dx, :, n : n + BLOCK],
                        preferred_element_type=F32,
                    )
                    total = d if total is None else total + d
            base = h_ref[r : r + BLOCK, n : n + BLOCK].astype(F32)
            out_ref[r : r + BLOCK, n : n + BLOCK] = (
                base + (total + bias_ref[:, n : n + BLOCK])
            ).astype(BF16)


def everyone(tile):
    count = lax.axis_size("row")
    copies = jnp.broadcast_to(tile, (count, *tile.shape))
    return lax.all_to_all(copies, "row", split_axis=0, concat_axis=0, tiled=True)


def local(
    latent, attn_gain, attn_shift, w_query, w_key, w_value, w_out,
    conv_gain, conv_shift, w_conv, conv_bias,
):
    count = lax.axis_size("row")
    chips = count // 2
    rows = latent.shape[0] * W
    half = rows // 2
    x = latent.reshape(rows, C)
    line = lambda v: v.reshape(1, C)
    swap = [(i, i ^ 1) for i in range(count)]
    turn = lambda d: [(i, ((i // 2 + d) % chips) * 2 + i % 2) for i in range(count)]

    a, b = x[:half], x[half:]
    up, down = [a, b], [a, b]
    pairs = [(a, b)]
    for step in range(1, chips // 2 + 1):
        if step < chips // 2:
            for h in range(2):
                up[h] = lax.ppermute(up[h], "row", turn(1))
                down[h] = lax.ppermute(down[h], "row", turn(-1))
                pairs.append((up[h], down[h]))
        else:
            pairs.append(
                (lax.ppermute(up[0], "row", turn(1)), lax.ppermute(down[1], "row", turn(-1)))
            )

    tile = jax.ShapeDtypeStruct((8, LANES), F32)
    wqk = lax.dot_general(
        w_query, w_key, (((1,), (1,)), ((), ())), preferred_element_type=F32
    ).astype(BF16)
    wvo = jnp.dot(w_value, w_out, preferred_element_type=F32).astype(BF16)
    stats = everyone(call(stats_kernel, tile, [VMEM], [x], 4 * rows * C))
    query, coef = call(
        query_kernel,
        [jax.ShapeDtypeStruct((rows, C), BF16), jax.ShapeDtypeStruct((8, C), F32)],
        [VMEM] * 5,
        [x, stats, line(attn_gain), line(attn_shift), wqk],
        2 * rows * C * C,
    )
    other = lax.ppermute(query, "row", swap)
    state = None
    for n, (ka, kb) in enumerate(pairs):
        state = attend(query, other, ka, kb, state, n == len(pairs) - 1)
    mine, theirs = state
    met = lax.ppermute(theirs, "row", swap)
    hidden, tile2 = call(
        output_kernel,
        [jax.ShapeDtypeStruct((rows, C), BF16), tile],
        [VMEM] * 5,
        [mine, met, x, coef, wvo],
        2 * rows * C * C,
    )
    top = lax.ppermute(hidden[rows - W :], "row", [(i, i + 1) for i in range(count - 1)])
    bottom = lax.ppermute(hidden[:W], "row", [(i + 1, i) for i in range(count - 1)])
    stats2 = everyone(tile2)
    me = lax.axis_index("row")
    flags = jnp.stack([me > 0, me < count - 1]).astype(jnp.int32)
    encoded = call(
        conv_kernel,
        jax.ShapeDtypeStruct((rows, C), BF16),
        [SMEM] + [VMEM] * 8,
        [
            flags, hidden, top, bottom, stats2, line(conv_gain), line(conv_shift),
            w_conv.reshape(9, C, C), line(conv_bias),
        ],
        18 * rows * C * C,
        scratch=[pltpu.VMEM((rows + 2 * W, C), BF16)] * 3,
    )
    return encoded.reshape(latent.shape)


def solution(mesh):
    in_specs = (P(("img", "row"), None, None), P(), P(), P(), P(), P(), P(), P(), P(), P(), P())
    out_specs = P(("img", "row"), None, None)
    return jax.shard_map(local, mesh=mesh, in_specs=in_specs, out_specs=out_specs, check_vma=False)
```

time: 157 us -> 93.9 us (0.60)
  matrix products: 39.9 us -> 1.94 us
  starting transfers between devices: 4.64 us -> 41.9 us
  waiting for transfers between devices: 55.5 us -> 24.3 us
  blocking collectives: 28.2 us -> 0 us
  Pallas kernels: 0 us -> 19.1 us
  other arithmetic: 13.7 us -> 0.07 us
  between operations: 13.6 us -> 0.24 us
  local copies, waits for them, and re-layouts: 1.52 us -> 5.89 us
    all_gather x1 -> x0, waiting for transfers between devices: 51.1 us -> none  [local(): piece = lax.all_gather(normed, 'row', axis=0, tiled=True)]
    dot_general x13 -> x2, matrix products: 39.9 us -> 1.94 us  [the longest x1 1.51 us: local(): lax.dot_general(w_query, w_key, (((1,), (1,)), ((), ())), preferred_eleme...]
    all_to_all x2 -> x0, blocking collectives: 28.2 us -> none  [copy_for_each(): return lax.all_to_all(copies, axis, split_axis=0, concat_axis=0, tiled=True)]
    ppermute x2 -> x18, starting transfers between devices: 4.64 us -> 28.2 us  [the longest x6 13.9 us: local(): down[h] = lax.ppermute(down[h], 'row', turn(-1))]
    pallas_call x0 -> x12, Pallas kernels: none -> 19.1 us  [call(): pl.pallas_call(kernel, out_shape=outs, in_specs=specs, out_specs=jax.tree...]
    all_to_all x0 -> x2, waiting for transfers between devices: none -> 13.9 us  [everyone(): lax.all_to_all(copies, 'row', split_axis=0, concat_axis=0, tiled=True)]
    all_to_all x0 -> x2, starting transfers between devices: none -> 13.8 us  [everyone(): lax.all_to_all(copies, 'row', split_axis=0, concat_axis=0, tiled=True)]
    reduce_sum x8 -> x0, other arithmetic: 10.6 us -> none  [the longest x1 8.68 us: attend(): denominator = jnp.sum(expo, axis=1)]
  transfers between devices with their start and end apart: 3 -> 20, of which waited for: 2 -> 6; matrix products, arithmetic and copies ran while one was open for 1% -> 4% of each run, Pallas kernels for 0% -> 13%
where the time goes in v1:
time: 93.9 us; the launch traced here: 93.5 us
  starting transfers between devices  41.9 us (45%)
  waiting for transfers between devices  24.3 us (26%)
  Pallas kernels  19.1 us (20%)
  local copies, waits for them, and re-layouts  5.89 us (6%)
  matrix products  1.94 us (2%)
    pallas_call x12, Pallas kernels, call(): pl.pallas_call(kernel, out_shape=outs, in_specs=specs, out_specs=jax.tree...  19.1 us
    all_to_all x2, waiting for transfers between devices, everyone(): lax.all_to_all(copies, 'row', split_axis=0, concat_axis=0, tiled=True)  13.9 us
    ppermute x6, starting transfers between devices, local(): down[h] = lax.ppermute(down[h], 'row', turn(-1))  13.9 us
    all_to_all x2, starting transfers between devices, everyone(): lax.all_to_all(copies, 'row', split_axis=0, concat_axis=0, tiled=True)  13.8 us
    ppermute x6, waiting for transfers between devices, local(): up[h] = lax.ppermute(up[h], 'row', turn(1))  4.54 us
    ppermute x6, starting transfers between devices, local(): up[h] = lax.ppermute(up[h], 'row', turn(1))  4.36 us
    ppermute x6, waiting for transfers between devices, local(): down[h] = lax.ppermute(down[h], 'row', turn(-1))  3.63 us
    unnamed x22, local copies, waits for them, and re-layouts  3.41 us
  transfers between devices with their start and end apart: 20, of which 6 were waited for; matrix products, arithmetic and copies ran while one was open for 4% of the time, Pallas kernels for 13%

profile of v1, /device:TPU:1, one launch (start us, length us, event | category | flops | bytes accessed | tf_op | source)
XLA Modules:
  0.0 93.5 jit_solution(5075506604129375804)
XLA Ops:
  0.0 1.2 %fusion.1 = (bf16[2,128,512]{2,1,0:T(8,128)(2,1)S(1)}, bf16[2,128,512]{2,1,0:T(8,128)(2,1)S(1)}) fusion(bf16[4,128,512]{2,1,0:T(8,128)(2,1)} %param.11), kind=kLoop, calls=%fused_computation.4 | loop fusion | bytes 1048576 | tf_op jit(solution)/shard_map/slice | solution.py:245
  1.2 2.5 %collective-permute-start.1 = (bf16[256,512]{1,0:T(8,128)(2,1)S(1)}, bf16[256,512]{1,0:T(8,128)(2,1)S(1)}, u32[]{:S(2)}, u32[]{:S(2)}) collective-permute-start(bf16[256,512]{1,0:T(8,128)(2,1)S(1)} %bitcast.22), channel_id=1, source_target_pairs={{0,2},{1,3},{2,4},{3,5},{4,6},{5,7},{6,8},{7,9},{8,10},{9,11},{10,... | collective-permute-start | bytes 786440 | tf_op jit(solution)/shard_map/ppermute | solution.py:251
  3.7 4.0 %collective-permute-start.12 = (bf16[256,512]{1,0:T(8,128)(2,1)S(1)}, bf16[256,512]{1,0:T(8,128)(2,1)S(1)}, u32[]{:S(2)}, u32[]{:S(2)}) collective-permute-start(bf16[256,512]{1,0:T(8,128)(2,1)S(1)} %bitcast.23), channel_id=1, source_target_pairs={{0,14},{1,15},{2,0},{3,1},{4,2},{5,3},{6,4},{7,5},{8,6},{9,7},{10,... | collective-permute-start | bytes 786440 | tf_op jit(solution)/shard_map/ppermute | solution.py:252
  7.7 1.4 %collective-permute-start.5 = (bf16[256,512]{1,0:T(8,128)(2,1)S(1)}, bf16[256,512]{1,0:T(8,128)(2,1)S(1)}, u32[]{:S(2)}, u32[]{:S(2)}) collective-permute-start(bf16[256,512]{1,0:T(8,128)(2,1)S(1)} %bitcast.19), channel_id=1, source_target_pairs={{0,14},{1,15},{2,0},{3,1},{4,2},{5,3},{6,4},{7,5},{8,6},{9,7},{10,... | collective-permute-start | bytes 786440 | tf_op jit(solution)/shard_map/ppermute | solution.py:252
  11.8 7.3 %all-to-all-start = ((f32[16,8,128]{2,1,0:T(8,128)}), f32[16,8,128]{2,1,0:T(8,128)S(1)}, u32[]{:S(2)}, u32[]{:S(2)}) async-start(f32[16,8,128]{2,1,0:T(8,128)} %broadcast_in_dim.6), calls=%async_computation | async-start | bytes 131072 | tf_op jit(solution)/shard_map/all_to_all | solution.py:229
  19.1 1.5 %convolution_convert_fusion.1.wqk_ref = bf16[512,512]{1,0:T(8,128)(2,1)S(1)} fusion(bf16[512,512]{1,0:T(8,128)(2,1)S(1)} %copy-done, bf16[512,512]{1,0:T(8,128)(2,1)} %param.15), kind=kOutput, calls=%fused_computation.1 | convolution fusion | flops 268697600 | bytes 1572864 | tf_op jit(solution)/shard_map/dot_general | solution.py:260
  20.6 6.2 %all-to-all-done.stats_ref = f32[16,8,128]{2,1,0:T(8,128)S(1)} async-done(((f32[16,8,128]{2,1,0:T(8,128)}), f32[16,8,128]{2,1,0:T(8,128)S(1)}, u32[]{:S(2)}, u32[]{:S(2)}) %all-to-all-start) | async-done | bytes 65568 | tf_op jit(solution)/shard_map/all_to_all | solution.py:229
  27.9 2.3 %collective-permute-start.13 = (bf16[256,512]{1,0:T(8,128)(2,1)S(1)}, bf16[256,512]{1,0:T(8,128)(2,1)S(1)}, u32[]{:S(2)}, u32[]{:S(2)}) collective-permute-start(bf16[256,512]{1,0:T(8,128)(2,1)S(1)} %collective-permute-done.12.refs_3_), channel_id=1, source_target_pairs={{0,14},{1,15},{2,0},{3,1},{4,2},{5,3},{6,4},{7,5},{8,6},{9,7},{10,... | collective-permute-start | bytes 786440 | tf_op jit(solution)/shard_map/ppermute | solution.py:252
  30.3 1.4 %collective-permute-start.10 = (bf16[256,512]{1,0:T(8,128)(2,1)S(1)}, bf16[256,512]{1,0:T(8,128)(2,1)S(1)}, u32[]{:S(2)}, u32[]{:S(2)}) collective-permute-start(bf16[256,512]{1,0:T(8,128)(2,1)S(1)} %collective-permute-done.9.refs_2_), channel_id=1, source_target_pairs={{0,2},{1,3},{2,4},{3,5},{4,6},{5,7},{6,8},{7,9},{8,10},{9,11},{10,... | collective-permute-start | bytes 786440 | tf_op jit(solution)/shard_map/ppermute | solution.py:251
  31.7 4.5 %collective-permute-done.2.refs_2_ = bf16[256,512]{1,0:T(8,128)(2,1)S(1)} collective-permute-done((bf16[256,512]{1,0:T(8,128)(2,1)S(1)}, bf16[256,512]{1,0:T(8,128)(2,1)S(1)}, u32[]{:S(2)}, u32[]{:S(2)}) %collective-permute-start.2) | collective-permute-done | bytes 262176 | tf_op jit(solution)/shard_map/ppermute | solution.py:251
  36.2 2.7 %collective-permute-start.14 = (bf16[256,512]{1,0:T(8,128)(2,1)S(1)}, bf16[256,512]{1,0:T(8,128)(2,1)S(1)}, u32[]{:S(2)}, u32[]{:S(2)}) collective-permute-start(bf16[256,512]{1,0:T(8,128)(2,1)S(1)} %collective-permute-done.13.refs_3_), channel_id=1, source_target_pairs={{0,14},{1,15},{2,0},{3,1},{4,2},{5,3},{6,4},{7,5},{8,6},{9,7},{10,... | collective-permute-start | bytes 786440 | tf_op jit(solution)/shard_map/ppermute | solution.py:252
  38.9 1.9 %collective-permute-done.6.refs_3_ = bf16[256,512]{1,0:T(8,128)(2,1)S(1)} collective-permute-done((bf16[256,512]{1,0:T(8,128)(2,1)S(1)}, bf16[256,512]{1,0:T(8,128)(2,1)S(1)}, u32[]{:S(2)}, u32[]{:S(2)}) %collective-permute-start.6) | collective-permute-done | bytes 262176 | tf_op jit(solution)/shard_map/ppermute | solution.py:252
  40.9 3.4 %collective-permute-start.7 = (bf16[256,512]{1,0:T(8,128)(2,1)S(1)}, bf16[256,512]{1,0:T(8,128)(2,1)S(1)}, u32[]{:S(2)}, u32[]{:S(2)}) collective-permute-start(bf16[256,512]{1,0:T(8,128)(2,1)S(1)} %collective-permute-done.6.refs_3_), channel_id=1, source_target_pairs={{0,14},{1,15},{2,0},{3,1},{4,2},{5,3},{6,4},{7,5},{8,6},{9,7},{10,... | collective-permute-start | bytes 786440 | tf_op jit(solution)/shard_map/ppermute | solution.py:252
  44.3 1.3 %shard_map.111 = (f32[1024,512]{1,0:T(8,128)S(1)}, f32[1024,128]{1,0:T(8,128)S(1)}, f32[1024,128]{1,0:T(8,128)S(1)}) custom-call(bf16[512,512]{1,0:T(8,128)(2,1)S(1)} %get-tuple-element.32.refs_0_, bf16[512,512]{1,0:T(8,128)(2,1)S(1)} %collective-permute-done.refs_1_, bf16[256,512]{1,0:T(8,128)(2,1)S(1)} %bitcast.24, bf16[256,512]{1,0:T(8,128)(2,1)S(1)} %bitcast.21), custom_call_target="tpu_custom_call" | custom-call | flops 1073741824 | bytes 1572864 | tf_op jit(solution)/shard_map/pallas_call | solution.py:23
  45.6 1.6 %shard_map.112 = (f32[1024,512]{1,0:T(8,128)S(1)}, f32[1024,128]{1,0:T(8,128)S(1)}, f32[1024,128]{1,0:T(8,128)S(1)}) custom-call(bf16[512,512]{1,0:T(8,128)(2,1)S(1)} %get-tuple-element.32.refs_0_, bf16[512,512]{1,0:T(8,128)(2,1)S(1)} %collective-permute-done.refs_1_, ...), custom_call_target="tpu_custom_call", output_to_operand_aliasing={{0}: (4, {}), {1}: (5, {}), {2}: (6, {})} | custom-call | flops 1073741824 | bytes 4718592 | tf_op jit(solution)/shard_map/pallas_call | solution.py:23
  47.1 1.6 %shard_map.113 = (f32[1024,512]{1,0:T(8,128)S(1)}, f32[1024,128]{1,0:T(8,128)S(1)}, f32[1024,128]{1,0:T(8,128)S(1)}) custom-call(bf16[512,512]{1,0:T(8,128)(2,1)S(1)} %get-tuple-element.32.refs_0_, bf16[512,512]{1,0:T(8,128)(2,1)S(1)} %collective-permute-done.refs_1_, ...), custom_call_target="tpu_custom_call", output_to_operand_aliasing={{0}: (4, {}), {1}: (5, {}), {2}: (6, {})} | custom-call | flops 1073741824 | bytes 4718592 | tf_op jit(solution)/shard_map/pallas_call | solution.py:23
  48.7 1.6 %shard_map.114 = (f32[1024,512]{1,0:T(8,128)S(1)}, f32[1024,128]{1,0:T(8,128)S(1)}, f32[1024,128]{1,0:T(8,128)S(1)}) custom-call(bf16[512,512]{1,0:T(8,128)(2,1)S(1)} %get-tuple-element.32.refs_0_, bf16[512,512]{1,0:T(8,128)(2,1)S(1)} %collective-permute-done.refs_1_, ...), custom_call_target="tpu_custom_call", output_to_operand_aliasing={{0}: (4, {}), {1}: (5, {}), {2}: (6, {})} | custom-call | flops 1073741824 | bytes 4718592 | tf_op jit(solution)/shard_map/pallas_call | solution.py:23
  50.4 1.7 %collective-permute-done.7.refs_3_ = bf16[256,512]{1,0:T(8,128)(2,1)S(1)} collective-permute-done((bf16[256,512]{1,0:T(8,128)(2,1)S(1)}, bf16[256,512]{1,0:T(8,128)(2,1)S(1)}, u32[]{:S(2)}, u32[]{:S(2)}) %collective-permute-start.7) | collective-permute-done | bytes 262176 | tf_op jit(solution)/shard_map/ppermute | solution.py:252
  52.1 3.4 %collective-permute-start.8 = (bf16[256,512]{1,0:T(8,128)(2,1)S(1)}, bf16[256,512]{1,0:T(8,128)(2,1)S(1)}, u32[]{:S(2)}, u32[]{:S(2)}) collective-permute-start(bf16[256,512]{1,0:T(8,128)(2,1)S(1)} %collective-permute-done.7.refs_3_), channel_id=1, source_target_pairs={{0,14},{1,15},{2,0},{3,1},{4,2},{5,3},{6,4},{7,5},{8,6},{9,7},{10,... | collective-permute-start | bytes 786440 | tf_op jit(solution)/shard_map/ppermute | solution.py:256
  55.5 1.6 %shard_map.115 = (f32[1024,512]{1,0:T(8,128)S(1)}, f32[1024,128]{1,0:T(8,128)S(1)}, f32[1024,128]{1,0:T(8,128)S(1)}) custom-call(bf16[512,512]{1,0:T(8,128)(2,1)S(1)} %get-tuple-element.32.refs_0_, bf16[512,512]{1,0:T(8,128)(2,1)S(1)} %collective-permute-done.refs_1_, ...), custom_call_target="tpu_custom_call", output_to_operand_aliasing={{0}: (4, {}), {1}: (5, {}), {2}: (6, {})} | custom-call | flops 1073741824 | bytes 4718592 | tf_op jit(solution)/shard_map/pallas_call | solution.py:23
  57.1 1.6 %shard_map.116 = (f32[1024,512]{1,0:T(8,128)S(1)}, f32[1024,128]{1,0:T(8,128)S(1)}, f32[1024,128]{1,0:T(8,128)S(1)}) custom-call(bf16[512,512]{1,0:T(8,128)(2,1)S(1)} %get-tuple-element.32.refs_0_, bf16[512,512]{1,0:T(8,128)(2,1)S(1)} %collective-permute-done.refs_1_, ...), custom_call_target="tpu_custom_call", output_to_operand_aliasing={{0}: (4, {}), {1}: (5, {}), {2}: (6, {})} | custom-call | flops 1073741824 | bytes 4718592 | tf_op jit(solution)/shard_map/pallas_call | solution.py:23
  58.7 1.6 %shard_map.117 = (f32[1024,512]{1,0:T(8,128)S(1)}, f32[1024,128]{1,0:T(8,128)S(1)}, f32[1024,128]{1,0:T(8,128)S(1)}) custom-call(bf16[512,512]{1,0:T(8,128)(2,1)S(1)} %get-tuple-element.32.refs_0_, bf16[512,512]{1,0:T(8,128)(2,1)S(1)} %collective-permute-done.refs_1_, ...), custom_call_target="tpu_custom_call", output_to_operand_aliasing={{0}: (4, {}), {1}: (5, {}), {2}: (6, {})} | custom-call | flops 1073741824 | bytes 4718592 | tf_op jit(solution)/shard_map/pallas_call | solution.py:23
  60.3 1.4 %shard_map.118 = (f32[512,640]{1,0:T(8,128)S(1)}, f32[512,640]{1,0:T(8,128)S(1)}) custom-call(bf16[512,512]{1,0:T(8,128)(2,1)S(1)} %get-tuple-element.32.refs_0_, bf16[512,512]{1,0:T(8,128)(2,1)S(1)} %collective-permute-done.refs_1_, bf16[256,512]{1,0:T(8,128)(2,1)S(1)} %collective-permute-done.4.refs_2_, ...), custom_call_target="tpu_custom_call" | custom-call | flops 1073741824 | bytes 4718592 | tf_op jit(solution)/shard_map/pallas_call | solution.py:23
  61.7 1.9 %collective-permute-start.15 = (f32[512,640]{1,0:T(8,128)S(1)}, f32[512,640]{1,0:T(8,128)S(1)}, u32[]{:S(2)}, u32[]{:S(2)}) collective-permute-start(f32[512,640]{1,0:T(8,128)S(1)} %get-tuple-element.55), channel_id=1, source_target_pairs={{0,1},{1,0},{2,3},{3,2},{4,5},{5,4},{6,7},{7,6},{8,9},{9,8},{10,11... | collective-permute-start | bytes 3932168 | tf_op jit(solution)/shard_map/ppermute | solution.py:277
  64.1 2.2 %collective-permute-done.15.b_ref = f32[512,640]{1,0:T(8,128)S(1)} collective-permute-done((f32[512,640]{1,0:T(8,128)S(1)}, f32[512,640]{1,0:T(8,128)S(1)}, u32[]{:S(2)}, u32[]{:S(2)}) %collective-permute-start.15) | collective-permute-done | bytes 1310752 | tf_op jit(solution)/shard_map/ppermute | solution.py:277
  66.3 1.6 %shard_map.119 = (bf16[512,512]{1,0:T(8,128)(2,1)S(1)}, f32[8,128]{1,0:T(8,128)S(1)}) custom-call(f32[512,640]{1,0:T(8,128)S(1)} %get-tuple-element.54.a_ref, f32[512,640]{1,0:T(8,128)S(1)} %collective-permute-done.15.b_ref, bf16[512,512]{1,0:T(8,128)(2,1)S(1)} %bitcast.18, f32[8,512]{1,0:T(8,128)S(1)} %get-tuple-element.56.coef_ref, ...), custom_call_target="tpu_custom_call" | custom-call | flops 268435456 | bytes 3686400 | tf_op jit(solution)/shard_map/pallas_call | solution.py:23
  67.9 1.9 %collective-permute-start.16 = (bf16[128,512]{1,0:T(8,128)(2,1)S(1)}, bf16[128,512]{1,0:T(8,128)(2,1)S(1)}, u32[]{:S(2)}, u32[]{:S(2)}) collective-permute-start(bf16[128,512]{1,0:T(8,128)(2,1)S(1)} %get-tuple-element.60), channel_id=1, source_target_pairs={{0,1},{1,2},{2,3},{3,4},{4,5},{5,6},{6,7},{7,8},{8,9},{9,10},{10,1... | collective-permute-start | bytes 393224 | tf_op jit(solution)/shard_map/ppermute | solution.py:285
  69.8 2.4 %collective-permute-start.17 = (bf16[128,512]{1,0:T(8,128)(2,1)S(1)}, bf16[128,512]{1,0:T(8,128)(2,1)S(1)}, u32[]{:S(2)}, u32[]{:S(2)}) collective-permute-start(bf16[128,512]{1,0:T(8,128)(2,1)S(1)} %get-tuple-element.59), channel_id=1, source_target_pairs={{1,0},{2,1},{3,2},{4,3},{5,4},{6,5},{7,6},{8,7},{9,8},{10,9},{11,1... | collective-permute-start | bytes 393224 | tf_op jit(solution)/shard_map/ppermute | solution.py:286
  72.9 6.5 %all-to-all-start.1 = ((f32[16,8,128]{2,1,0:T(8,128)}), f32[16,8,128]{2,1,0:T(8,128)S(1)}, u32[]{:S(2)}, u32[]{:S(2)}) async-start(f32[16,8,128]{2,1,0:T(8,128)} %broadcast_in_dim.7), calls=%async_computation.1 | async-start | bytes 131072 | tf_op jit(solution)/shard_map/all_to_all | solution.py:229
  79.4 7.7 %all-to-all-done.1.stats_ref = f32[16,8,128]{2,1,0:T(8,128)S(1)} async-done(((f32[16,8,128]{2,1,0:T(8,128)}), f32[16,8,128]{2,1,0:T(8,128)S(1)}, u32[]{:S(2)}, u32[]{:S(2)}) %all-to-all-start.1) | async-done | bytes 65568 | tf_op jit(solution)/shard_map/all_to_all | solution.py:229
  87.2 2.3 %copy-done.5 = bf16[3,3,512,512]{3,2,1,0:T(8,128)(2,1)S(1)} copy-done((bf16[3,3,512,512]{3,2,1,0:T(8,128)(2,1)S(1)}, bf16[3,3,512,512]{3,2,1,0:T(8,128)(2,1)}, u32[]{:S(2)}) %copy-start.5) | copy-done | bytes 4718616
  89.5 4.0 %shard_map.120 = bf16[512,512]{1,0:T(8,128)(2,1)} custom-call(s32[2]{0:T(128)S(1)} %add_convert_fusion.flags_ref, bf16[512,512]{1,0:T(8,128)(2,1)S(1)} %get-tuple-element.57.h_ref, bf16[128,512]{1,0:T(8,128)(2,1)S(1)} %collective-permute-done.16.top_ref, bf16[128,512]{1,0:T(8,128)(2,1)S(1)} %collective-permute-done.17.bottom_ref, ...), custom_call_target="tpu_custom_call" | custom-call | flops 2415919104 | bytes 5576712 | tf_op jit(solution)/shard_map/pallas_call | solution.py:23
  (49 shorter events, 5.1 us)
Async XLA Ops:
  0.0 19.1 %copy-start = (bf16[512,512]{1,0:T(8,128)(2,1)S(1)}, bf16[512,512]{1,0:T(8,128)(2,1)}, u32[]{:S(2)}) copy-start(bf16[512,512]{1,0:T(8,128)(2,1)} %param.14) | copy-start | bytes 1572868
  0.0 26.8 %copy-start.2 = (bf16[4,128,512]{2,1,0:T(8,128)(2,1)S(1)}, bf16[4,128,512]{2,1,0:T(8,128)(2,1)}, u32[]{:S(2)}) copy-start(bf16[4,128,512]{2,1,0:T(8,128)(2,1)} %param.11) | copy-start | bytes 1572868
  0.0 26.8 %copy-start.3 = (f32[512]{0:T(512)S(1)}, f32[512]{0:T(512)}, u32[]{:S(2)}) copy-start(f32[512]{0:T(512)} %param.12) | copy-start | bytes 6148
  0.0 26.8 %copy-start.4 = (f32[512]{0:T(512)S(1)}, f32[512]{0:T(512)}, u32[]{:S(2)}) copy-start(f32[512]{0:T(512)} %param.13) | copy-start | bytes 6148
  1.2 26.4 %collective-permute-start.1 = (bf16[256,512]{1,0:T(8,128)(2,1)S(1)}, bf16[256,512]{1,0:T(8,128)(2,1)S(1)}, u32[]{:S(2)}, u32[]{:S(2)}) collective-permute-start(bf16[256,512]{1,0:T(8,128)(2,1)S(1)} %bitcast.22), channel_id=1, source_target_pairs={{0,2},{1,3},{2,4},{3,5},{4,6},{5,7},{6,8},{7,9},{8,10},{9,11},{10,... | collective-permute-start | bytes 786440 | tf_op jit(solution)/shard_map/ppermute | solution.py:251
  3.7 24.2 %collective-permute-start.12 = (bf16[256,512]{1,0:T(8,128)(2,1)S(1)}, bf16[256,512]{1,0:T(8,128)(2,1)S(1)}, u32[]{:S(2)}, u32[]{:S(2)}) collective-permute-start(bf16[256,512]{1,0:T(8,128)(2,1)S(1)} %bitcast.23), channel_id=1, source_target_pairs={{0,14},{1,15},{2,0},{3,1},{4,2},{5,3},{6,4},{7,5},{8,6},{9,7},{10,... | collective-permute-start | bytes 786440 | tf_op jit(solution)/shard_map/ppermute | solution.py:252
  7.7 22.5 %collective-permute-start.5 = (bf16[256,512]{1,0:T(8,128)(2,1)S(1)}, bf16[256,512]{1,0:T(8,128)(2,1)S(1)}, u32[]{:S(2)}, u32[]{:S(2)}) collective-permute-start(bf16[256,512]{1,0:T(8,128)(2,1)S(1)} %bitcast.19), channel_id=1, source_target_pairs={{0,14},{1,15},{2,0},{3,1},{4,2},{5,3},{6,4},{7,5},{8,6},{9,7},{10,... | collective-permute-start | bytes 786440 | tf_op jit(solution)/shard_map/ppermute | solution.py:252
  9.1 21.2 %collective-permute-start.9 = (bf16[256,512]{1,0:T(8,128)(2,1)S(1)}, bf16[256,512]{1,0:T(8,128)(2,1)S(1)}, u32[]{:S(2)}, u32[]{:S(2)}) collective-permute-start(bf16[256,512]{1,0:T(8,128)(2,1)S(1)} %bitcast.20), channel_id=1, source_target_pairs={{0,2},{1,3},{2,4},{3,5},{4,6},{5,7},{6,8},{7,9},{8,10},{9,11},{10,... | collective-permute-start | bytes 786440 | tf_op jit(solution)/shard_map/ppermute | solution.py:251
  9.2 1.0 %copy-start.1 = (bf16[4,128,512]{2,1,0:T(8,128)(2,1)S(1)}, bf16[4,128,512]{2,1,0:T(8,128)(2,1)}, u32[]{:S(2)}) copy-start(bf16[4,128,512]{2,1,0:T(8,128)(2,1)} %param.11) | copy-start | bytes 1572868
  11.8 15.1 %all-to-all-start = ((f32[16,8,128]{2,1,0:T(8,128)}), f32[16,8,128]{2,1,0:T(8,128)S(1)}, u32[]{:S(2)}, u32[]{:S(2)}) async-start(f32[16,8,128]{2,1,0:T(8,128)} %broadcast_in_dim.6), calls=%async_computation | async-start | bytes 131072 | tf_op jit(solution)/shard_map/all_to_all | solution.py:229
  27.3 16.9 %collective-permute-start = (bf16[512,512]{1,0:T(8,128)(2,1)S(1)}, bf16[512,512]{1,0:T(8,128)(2,1)S(1)}, u32[]{:S(2)}, u32[]{:S(2)}) collective-permute-start(bf16[512,512]{1,0:T(8,128)(2,1)S(1)} %get-tuple-element.32.refs_0_), channel_id=1, source_target_pairs={{0,1},{1,0},{2,3},{3,2},{4,5},{5,4},{6,7},{7,6},{8,9},{9,8},{10,11... | collective-permute-start | bytes 1572872 | tf_op jit(solution)/shard_map/ppermute | solution.py:272
  27.5 8.7 %collective-permute-start.2 = (bf16[256,512]{1,0:T(8,128)(2,1)S(1)}, bf16[256,512]{1,0:T(8,128)(2,1)S(1)}, u32[]{:S(2)}, u32[]{:S(2)}) collective-permute-start(bf16[256,512]{1,0:T(8,128)(2,1)S(1)} %collective-permute-done.1.refs_2_), channel_id=1, source_target_pairs={{0,2},{1,3},{2,4},{3,5},{4,6},{5,7},{6,8},{7,9},{8,10},{9,11},{10,... | collective-permute-start | bytes 786440 | tf_op jit(solution)/shard_map/ppermute | solution.py:251
  27.9 8.3 %collective-permute-start.13 = (bf16[256,512]{1,0:T(8,128)(2,1)S(1)}, bf16[256,512]{1,0:T(8,128)(2,1)S(1)}, u32[]{:S(2)}, u32[]{:S(2)}) collective-permute-start(bf16[256,512]{1,0:T(8,128)(2,1)S(1)} %collective-permute-done.12.refs_3_), channel_id=1, source_target_pairs={{0,14},{1,15},{2,0},{3,1},{4,2},{5,3},{6,4},{7,5},{8,6},{9,7},{10,... | collective-permute-start | bytes 786440 | tf_op jit(solution)/shard_map/ppermute | solution.py:252
  30.2 10.6 %collective-permute-start.6 = (bf16[256,512]{1,0:T(8,128)(2,1)S(1)}, bf16[256,512]{1,0:T(8,128)(2,1)S(1)}, u32[]{:S(2)}, u32[]{:S(2)}) collective-permute-start(bf16[256,512]{1,0:T(8,128)(2,1)S(1)} %collective-permute-done.5.refs_3_), channel_id=1, source_target_pairs={{0,14},{1,15},{2,0},{3,1},{4,2},{5,3},{6,4},{7,5},{8,6},{9,7},{10,... | collective-permute-start | bytes 786440 | tf_op jit(solution)/shard_map/ppermute | solution.py:252
  30.3 13.9 %collective-permute-start.10 = (bf16[256,512]{1,0:T(8,128)(2,1)S(1)}, bf16[256,512]{1,0:T(8,128)(2,1)S(1)}, u32[]{:S(2)}, u32[]{:S(2)}) collective-permute-start(bf16[256,512]{1,0:T(8,128)(2,1)S(1)} %collective-permute-done.9.refs_2_), channel_id=1, source_target_pairs={{0,2},{1,3},{2,4},{3,5},{4,6},{5,7},{6,8},{7,9},{8,10},{9,11},{10,... | collective-permute-start | bytes 786440 | tf_op jit(solution)/shard_map/ppermute | solution.py:251
  36.2 14.1 %collective-permute-start.3 = (bf16[256,512]{1,0:T(8,128)(2,1)S(1)}, bf16[256,512]{1,0:T(8,128)(2,1)S(1)}, u32[]{:S(2)}, u32[]{:S(2)}) collective-permute-start(bf16[256,512]{1,0:T(8,128)(2,1)S(1)} %collective-permute-done.2.refs_2_), channel_id=1, source_target_pairs={{0,2},{1,3},{2,4},{3,5},{4,6},{5,7},{6,8},{7,9},{8,10},{9,11},{10,... | collective-permute-start | bytes 786440 | tf_op jit(solution)/shard_map/ppermute | solution.py:251
  36.2 20.8 %collective-permute-start.14 = (bf16[256,512]{1,0:T(8,128)(2,1)S(1)}, bf16[256,512]{1,0:T(8,128)(2,1)S(1)}, u32[]{:S(2)}, u32[]{:S(2)}) collective-permute-start(bf16[256,512]{1,0:T(8,128)(2,1)S(1)} %collective-permute-done.13.refs_3_), channel_id=1, source_target_pairs={{0,14},{1,15},{2,0},{3,1},{4,2},{5,3},{6,4},{7,5},{8,6},{9,7},{10,... | collective-permute-start | bytes 786440 | tf_op jit(solution)/shard_map/ppermute | solution.py:252
  40.9 11.2 %collective-permute-start.7 = (bf16[256,512]{1,0:T(8,128)(2,1)S(1)}, bf16[256,512]{1,0:T(8,128)(2,1)S(1)}, u32[]{:S(2)}, u32[]{:S(2)}) collective-permute-start(bf16[256,512]{1,0:T(8,128)(2,1)S(1)} %collective-permute-done.6.refs_3_), channel_id=1, source_target_pairs={{0,14},{1,15},{2,0},{3,1},{4,2},{5,3},{6,4},{7,5},{8,6},{9,7},{10,... | collective-permute-start | bytes 786440 | tf_op jit(solution)/shard_map/ppermute | solution.py:252
  44.3 14.4 %collective-permute-start.11 = (bf16[256,512]{1,0:T(8,128)(2,1)S(1)}, bf16[256,512]{1,0:T(8,128)(2,1)S(1)}, u32[]{:S(2)}, u32[]{:S(2)}) collective-permute-start(bf16[256,512]{1,0:T(8,128)(2,1)S(1)} %collective-permute-done.10.refs_2_), channel_id=1, source_target_pairs={{0,2},{1,3},{2,4},{3,5},{4,6},{5,7},{6,8},{7,9},{8,10},{9,11},{10,... | collective-permute-start | bytes 786440 | tf_op jit(solution)/shard_map/ppermute | solution.py:251
  50.3 9.9 %collective-permute-start.4 = (bf16[256,512]{1,0:T(8,128)(2,1)S(1)}, bf16[256,512]{1,0:T(8,128)(2,1)S(1)}, u32[]{:S(2)}, u32[]{:S(2)}) collective-permute-start(bf16[256,512]{1,0:T(8,128)(2,1)S(1)} %collective-permute-done.3.refs_2_), channel_id=1, source_target_pairs={{0,2},{1,3},{2,4},{3,5},{4,6},{5,7},{6,8},{7,9},{8,10},{9,11},{10,... | collective-permute-start | bytes 786440 | tf_op jit(solution)/shard_map/ppermute | solution.py:256
  52.1 8.2 %collective-permute-start.8 = (bf16[256,512]{1,0:T(8,128)(2,1)S(1)}, bf16[256,512]{1,0:T(8,128)(2,1)S(1)}, u32[]{:S(2)}, u32[]{:S(2)}) collective-permute-start(bf16[256,512]{1,0:T(8,128)(2,1)S(1)} %collective-permute-done.7.refs_3_), channel_id=1, source_target_pairs={{0,14},{1,15},{2,0},{3,1},{4,2},{5,3},{6,4},{7,5},{8,6},{9,7},{10,... | collective-permute-start | bytes 786440 | tf_op jit(solution)/shard_map/ppermute | solution.py:256
  60.3 3.3 %copy-start.9 = (bf16[512,512]{1,0:T(8,128)(2,1)S(1)}, bf16[512,512]{1,0:T(8,128)(2,1)}, u32[]{:S(2)}) copy-start(bf16[512,512]{1,0:T(8,128)(2,1)} %param.16) | copy-start | bytes 1572868
  60.3 3.3 %copy-start.10 = (bf16[512,512]{1,0:T(8,128)(2,1)S(1)}, bf16[512,512]{1,0:T(8,128)(2,1)}, u32[]{:S(2)}) copy-start(bf16[512,512]{1,0:T(8,128)(2,1)} %param.17) | copy-start | bytes 1572868
  61.7 4.6 %collective-permute-start.15 = (f32[512,640]{1,0:T(8,128)S(1)}, f32[512,640]{1,0:T(8,128)S(1)}, u32[]{:S(2)}, u32[]{:S(2)}) collective-permute-start(f32[512,640]{1,0:T(8,128)S(1)} %get-tuple-element.55), channel_id=1, source_target_pairs={{0,1},{1,0},{2,3},{3,2},{4,5},{5,4},{6,7},{7,6},{8,9},{9,8},{10,11... | collective-permute-start | bytes 3932168 | tf_op jit(solution)/shard_map/ppermute | solution.py:277
  66.3 20.9 %copy-start.6 = (f32[512]{0:T(512)S(1)}, f32[512]{0:T(512)}, u32[]{:S(2)}) copy-start(f32[512]{0:T(512)} %param.18) | copy-start | bytes 6148
  66.3 20.9 %copy-start.7 = (f32[512]{0:T(512)S(1)}, f32[512]{0:T(512)}, u32[]{:S(2)}) copy-start(f32[512]{0:T(512)} %param.19) | copy-start | bytes 6148
  66.3 20.9 %copy-start.8 = (f32[512]{0:T(512)S(1)}, f32[512]{0:T(512)}, u32[]{:S(2)}) copy-start(f32[512]{0:T(512)} %param.21) | copy-start | bytes 6148
  67.9 19.2 %collective-permute-start.16 = (bf16[128,512]{1,0:T(8,128)(2,1)S(1)}, bf16[128,512]{1,0:T(8,128)(2,1)S(1)}, u32[]{:S(2)}, u32[]{:S(2)}) collective-permute-start(bf16[128,512]{1,0:T(8,128)(2,1)S(1)} %get-tuple-element.60), channel_id=1, source_target_pairs={{0,1},{1,2},{2,3},{3,4},{4,5},{5,6},{6,7},{7,8},{8,9},{9,10},{10,1... | collective-permute-start | bytes 393224 | tf_op jit(solution)/shard_map/ppermute | solution.py:285
  69.8 17.3 %collective-permute-start.17 = (bf16[128,512]{1,0:T(8,128)(2,1)S(1)}, bf16[128,512]{1,0:T(8,128)(2,1)S(1)}, u32[]{:S(2)}, u32[]{:S(2)}) collective-permute-start(bf16[128,512]{1,0:T(8,128)(2,1)S(1)} %get-tuple-element.59), channel_id=1, source_target_pairs={{1,0},{2,1},{3,2},{4,3},{5,4},{6,5},{7,6},{8,7},{9,8},{10,9},{11,1... | collective-permute-start | bytes 393224 | tf_op jit(solution)/shard_map/ppermute | solution.py:286
  72.9 14.3 %all-to-all-start.1 = ((f32[16,8,128]{2,1,0:T(8,128)}), f32[16,8,128]{2,1,0:T(8,128)S(1)}, u32[]{:S(2)}, u32[]{:S(2)}) async-start(f32[16,8,128]{2,1,0:T(8,128)} %broadcast_in_dim.7), calls=%async_computation.1 | async-start | bytes 131072 | tf_op jit(solution)/shard_map/all_to_all | solution.py:229
  87.2 2.3 %copy-start.5 = (bf16[3,3,512,512]{3,2,1,0:T(8,128)(2,1)S(1)}, bf16[3,3,512,512]{3,2,1,0:T(8,128)(2,1)}, u32[]{:S(2)}) copy-start(bf16[3,3,512,512]{3,2,1,0:T(8,128)(2,1)} %param.20) | copy-start | bytes 14155780

commit v2 on v1

v2 whole, which is shorter than its diff:
```python
import jax
import jax.numpy as jnp
from jax import lax
from jax.experimental import pallas as pl
from jax.experimental.pallas import tpu as pltpu
from jax.sharding import PartitionSpec as P


C = 512
GROUPS = 32
W = 128
LANES = 128
EPS = 1e-06
LOG2E = 1.4426950408889634
VMEM = pl.BlockSpec(memory_space=pltpu.VMEM)
SMEM = pl.BlockSpec(memory_space=pltpu.SMEM)
F32 = jnp.float32
BF16 = jnp.bfloat16
MIB = 1024 * 1024
AHEAD = 20_000_000_000


def call(kernel, outs, specs, args, flops, vmem_mib=16, scratch=(), aliases=None):
    moved = sum(a.size * a.dtype.itemsize for a in args)
    return pl.pallas_call(
        kernel,
        out_shape=outs,
        in_specs=specs,
        out_specs=jax.tree.map(lambda _: VMEM, outs),
        scratch_shapes=list(scratch),
        input_output_aliases=aliases or {},
        cost_estimate=pl.CostEstimate(flops=flops, bytes_accessed=moved, transcendentals=0),
        compiler_params=pltpu.CompilerParams(vmem_limit_bytes=vmem_mib * MIB),
    )(*args)


def group_sum(v):
    lane = lax.broadcasted_iota(jnp.int32, v.shape, 1)
    for k in (1, 2, 4, 8):
        up = pltpu.roll(v, k, 1)
        down = pltpu.roll(v, C - k, 1)
        v = v + jnp.where((lane & k) != 0, up, down)
    return v


def write_stats(field, out_ref):
    rows = field.shape[0]
    share = C // GROUPS
    mean = group_sum(jnp.broadcast_to(jnp.sum(field, 0, keepdims=True), (8, C))) * (
        1.0 / (rows * share)
    )
    offset = field - mean[0:1]
    spread = group_sum(jnp.broadcast_to(jnp.sum(offset * offset, 0, keepdims=True), (8, C)))
    for i in range(C // LANES):
        cut = slice(i * LANES, (i + 1) * LANES)
        out_ref[i : i + 1, :] = mean[0:1, cut]
        out_ref[i + 4 : i + 5, :] = spread[0:1, cut]


def affine(stats, gain, shift, rows):
    count = stats.shape[0]
    local = rows * (C // GROUPS)
    means = stats[:, 0:4, :]
    mean = jnp.sum(means, 0) * (1.0 / count)
    offset = means - mean[None]
    total = jnp.sum(stats[:, 4:8, :], 0) + local * jnp.sum(offset * offset, 0)
    inverse = lax.rsqrt(total * (1.0 / (local * count)) + EPS)
    flat = lambda v: jnp.concatenate([v[i : i + 1] for i in range(4)], axis=1)
    scale = flat(inverse) * gain
    return scale, shift - flat(mean) * scale


def stats_kernel(x_ref, out_ref):
    write_stats(x_ref[...].astype(F32), out_ref)


def fold_kernel(transposed, left_ref, right_ref, *refs):
    dims = (((1,), (1 if transposed else 0,)), ((), ()))
    product = lax.dot_general(left_ref[...], right_ref[...], dims, preferred_element_type=F32)
    refs[-1][...] = product.astype(BF16)


def fold(left, right, transposed, *early):
    def kernel(*refs):
        fold_kernel(transposed, *refs)

    args = [left, right, *early]
    out = jax.ShapeDtypeStruct((C, C), BF16)
    return call(kernel, out, [VMEM] * len(args), args, AHEAD, 8)


def query_kernel(x_ref, stats_ref, gain_ref, shift_ref, wqk_ref, q_ref, coef_ref):
    scale, shift = affine(stats_ref[...], gain_ref[...], shift_ref[...], x_ref.shape[0])
    coef_ref[0:1, :] = scale
    coef_ref[1:2, :] = shift
    normed = (x_ref[...].astype(F32) * scale + shift).astype(BF16)
    q = jnp.dot(normed, wqk_ref[...], preferred_element_type=F32)
    q_ref[...] = (q * (scale * (LOG2E / C**0.5))).astype(BF16)


BLOCK = 256


def scores_of(q, keys):
    return [
        lax.dot_general(q, k[...], (((1,), (1,)), ((), ())), preferred_element_type=F32)
        for k in keys
    ]


def wide(v):
    return jnp.concatenate([v] * (C // LANES), axis=1)


def absorb(scores, keys, state):
    tiles = [t[:, j : j + LANES] for t in scores for j in range(0, t.shape[1], LANES)]
    top = tiles[0]
    for t in tiles[1:]:
        top = jnp.maximum(top, t)
    top = jnp.broadcast_to(jnp.max(top, axis=1, keepdims=True), top.shape)
    if state is not None:
        acc0, before, part0 = state
        top = jnp.maximum(before, top)
    part = None
    acc = None
    n = 0
    for t, k in zip(scores, keys):
        probs = []
        for _ in range(t.shape[1] // LANES):
            p = jnp.exp2(tiles[n] - top).astype(BF16)
            probs.append(p)
            p32 = p.astype(F32)
            part = p32 if part is None else part + p32
            n += 1
        d = jnp.dot(jnp.concatenate(probs, axis=1), k[...], preferred_element_type=F32)
        acc = d if acc is None else acc + d
    if state is not None:
        fade = jnp.exp2(before - top)
        part = part + part0 * fade
        acc = acc + acc0 * wide(fade)
    return acc, top, part


def pack(ref, at, acc, top, part):
    ref[at, 0:C] = acc
    total = jnp.broadcast_to(jnp.sum(part, axis=1, keepdims=True), top.shape)
    lane = lax.broadcasted_iota(jnp.int32, top.shape, 1)
    ref[at, C : C + LANES] = jnp.where(lane < LANES // 2, top, total)


def attend_kernel(n_q, n_k, first, packed, *refs):
    queries, keys, refs = refs[:n_q], refs[n_q : n_q + n_k], refs[n_q + n_k :]
    if not first:
        states, refs = [refs[3 * i : 3 * i + 3] for i in range(n_q)], refs[3 * n_q :]
    work = [
        (i, slice(at, at + BLOCK)) for i in range(n_q) for at in range(0, queries[i].shape[0], BLOCK)
    ]
    ahead = scores_of(queries[0][work[0][1], :], keys)
    for n, (i, at) in enumerate(work):
        now = ahead
        if n + 1 < len(work):
            j, to = work[n + 1]
            ahead = scores_of(queries[j][to, :], keys)
        state = None if first else tuple(r[at, :] for r in states[i])
        result = absorb(now, keys, state)
        if packed and i == 1:
            pack(refs[3], at, *result)
        else:
            for ref, v in zip(refs[3 * i : 3 * i + 3], result):
                ref[at, :] = v


def attend(queries, keys, state, packed=False):
    half = queries[0].shape[0]
    first = state is None
    n_q, n_k = len(queries), len(keys)
    one = [
        jax.ShapeDtypeStruct((half, C), F32),
        jax.ShapeDtypeStruct((half, LANES), F32),
        jax.ShapeDtypeStruct((half, LANES), F32),
    ]
    outs = one * n_q
    if packed:
        outs = one + [jax.ShapeDtypeStruct((half, C + LANES), F32)]
    args = [*queries, *keys] + ([] if first else list(state))
    aliases = {} if first else {n_q + n_k + i: i for i in range(3 if packed else 3 * n_q)}

    def kernel(*refs):
        attend_kernel(n_q, n_k, first, packed, *refs)

    flops = 4 * n_q * half * C * sum(k.shape[0] for k in keys)
    return call(kernel, outs, [VMEM] * len(args), args, flops, 20, aliases=aliases)


def output_kernel(
    flags_ref, q_ref, key_ref, acc_ref, top_ref, part_ref, met_ref, x_ref, coef_ref, wvo_ref,
    hidden_ref, stats_ref, inside_ref, outside_ref,
):
    keys = [key_ref]
    rows = q_ref.shape[0]
    ahead = scores_of(q_ref[0:BLOCK, :], keys)
    for r in range(0, rows, BLOCK):
        at = slice(r, r + BLOCK)
        now = ahead
        if r + BLOCK < rows:
            ahead = scores_of(q_ref[r + BLOCK : r + 2 * BLOCK, :], keys)
        acc, top, part = absorb(now, keys, (acc_ref[at, :], top_ref[at, :], part_ref[at, :]))
        total = jnp.broadcast_to(jnp.sum(part, axis=1, keepdims=True), top.shape)
        edge = met_ref[at, C : C + LANES]
        other = jnp.broadcast_to(edge[:, 0:1], top.shape)
        other_total = jnp.broadcast_to(edge[:, LANES - 1 : LANES], top.shape)
        most = jnp.maximum(top, other)
        wa, wb = jnp.exp2(top - most), jnp.exp2(other - most)
        inverse = 1.0 / (total * wa + other_total * wb)
        mixed = acc * wide(wa * inverse) + met_ref[at, 0:C] * wide(wb * inverse)
        normed = (mixed * coef_ref[0:1, :] + coef_ref[1:2, :]).astype(BF16)
        hidden = x_ref[at, :].astype(F32) + jnp.dot(
            normed, wvo_ref[...], preferred_element_type=F32
        )
        hidden_ref[at, :] = hidden.astype(BF16)
    first = hidden_ref[0:W, :]
    last = hidden_ref[rows - W : rows, :]
    even = flags_ref[2] > 0
    inside_ref[...] = jnp.where(even, last, first)
    outside_ref[...] = jnp.where(even, first, last)
    write_stats(hidden_ref[...].astype(F32), stats_ref)


def conv_kernel(
    flags_ref, h_ref, inside_ref, outside_ref, stats_ref, gain_ref, shift_ref, w_ref, bias_ref,
    out_ref, left_ref, mid_ref, right_ref,
):
    rows = h_ref.shape[0]
    scale, shift = affine(stats_ref[...], gain_ref[...], shift_ref[...], rows)

    def activate(f, at, keep):
        v = f.astype(F32) * scale + shift
        v = v / (1.0 + jnp.exp(-v))
        if keep is not None:
            v = jnp.where(keep, v, 0.0)
        column = lax.broadcasted_iota(jnp.int32, v.shape, 0) % W
        mid_ref[at : at + W, :] = v.astype(BF16)
        before = jnp.where(column == 0, 0.0, pltpu.roll(v, 1, 0))
        left_ref[at : at + W, :] = before.astype(BF16)
        after = jnp.where(column == W - 1, 0.0, pltpu.roll(v, W - 1, 0))
        right_ref[at : at + W, :] = after.astype(BF16)

    even = flags_ref[2] > 0
    activate(jnp.where(even, outside_ref[...], inside_ref[...]), 0, flags_ref[0] > 0)
    for r in range(rows // W):
        activate(h_ref[r * W : (r + 1) * W, :], (r + 1) * W, None)
    bottom = jnp.where(even, inside_ref[...], outside_ref[...])
    activate(bottom, rows + W, flags_ref[1] > 0)
    for r in range(0, rows, BLOCK):
        for n in range(0, C, BLOCK):
            total = None
            for dy in range(3):
                for dx, src in enumerate((left_ref, mid_ref, right_ref)):
                    d = jnp.dot(
                        src[r + dy * W : r + dy * W + BLOCK, :],
                        w_ref[3 * dy + dx, :, n : n + BLOCK],
                        preferred_element_type=F32,
                    )
                    total = d if total is None else total + d
            base = h_ref[r : r + BLOCK, n : n + BLOCK].astype(F32)
            out_ref[r : r + BLOCK, n : n + BLOCK] = (
                base + (total + bias_ref[:, n : n + BLOCK])
            ).astype(BF16)


def everyone(tile):
    count = lax.axis_size("row")
    copies = jnp.broadcast_to(tile, (count, *tile.shape))
    return lax.all_to_all(copies, "row", split_axis=0, concat_axis=0, tiled=True)


def local(
    latent, attn_gain, attn_shift, w_query, w_key, w_value, w_out,
    conv_gain, conv_shift, w_conv, conv_bias,
):
    count = lax.axis_size("row")
    chips = count // 2
    rows = latent.shape[0] * W
    me = lax.axis_index("row")
    flags = jnp.stack([me > 0, me < count - 1, me % 2 == 0]).astype(jnp.int32)
    latent, flags = lax.optimization_barrier((latent, flags))
    x = latent.reshape(rows, C)
    line = lambda v: v.reshape(1, C)
    swap = [(i, i ^ 1) for i in range(count)]
    ring = [(i, ((i // 2 + 1 - 2 * (i % 2)) % chips) * 2 + i % 2) for i in range(count)]

    move = lambda v, to: lax.ppermute(v, "row", to)
    tile = jax.ShapeDtypeStruct((8, LANES), F32)
    stats = call(stats_kernel, tile, [VMEM], [x], AHEAD)
    wqk = fold(w_query, w_key, True)
    taps = w_conv.reshape(9, C, C)
    wvo = fold(w_value, w_out, False, taps)
    near, far = x, move(x, swap)
    pieces = [x]
    for step in range(1, chips // 2 + 1):
        near = move(near, ring)
        pieces.append(near)
        if step < chips // 2:
            far = move(far, ring)
            pieces.append(far)

    stats = everyone(stats)
    query, coef = call(
        query_kernel,
        [jax.ShapeDtypeStruct((rows, C), BF16), jax.ShapeDtypeStruct((8, C), F32)],
        [VMEM] * 5,
        [x, stats, line(attn_gain), line(attn_shift), wqk],
        2 * rows * C * C,
    )
    other = move(query, swap)
    state = None
    *early, late = pieces
    for n, key in enumerate(early):
        state = attend([query, other], [key], state, n == len(early) - 1)
    *mine, theirs = state
    met = move(theirs, swap)
    across = move(late, swap)
    mine = attend([query], [late], mine)
    edge = jax.ShapeDtypeStruct((W, C), BF16)
    hidden, tile2, inside, outside = call(
        output_kernel,
        [jax.ShapeDtypeStruct((rows, C), BF16), tile, edge, edge],
        [SMEM] + [VMEM] * 9,
        [flags, query, across, *mine, met, x, coef, wvo],
        6 * rows * C * C,
        20,
    )
    between = [(i, i + 1) for i in range(1, count - 1, 2)]
    inside = move(inside, swap)
    outside = move(outside, between + [(b, a) for a, b in between])
    stats2 = everyone(tile2)
    encoded = call(
        conv_kernel,
        jax.ShapeDtypeStruct((rows, C), BF16),
        [SMEM] + [VMEM] * 8,
        [
            flags, hidden, inside, outside, stats2, line(conv_gain), line(conv_shift),
            taps, line(conv_bias),
        ],
        18 * rows * C * C,
        scratch=[pltpu.VMEM((rows + 2 * W, C), BF16)] * 3,
    )
    return encoded.reshape(latent.shape)


def solution(mesh):
    in_specs = (P(("img", "row"), None, None), P(), P(), P(), P(), P(), P(), P(), P(), P(), P())
    out_specs = P(("img", "row"), None, None)
    return jax.shard_map(local, mesh=mesh, in_specs=in_specs, out_specs=out_specs, check_vma=False)
```

time: 93.9 us -> 82.6 us (0.88)
  blocking collectives: 0 us -> 15.8 us
  starting transfers between devices: 41.9 us -> 28.7 us
  waiting for transfers between devices: 24.3 us -> 13.6 us
  local copies, waits for them, and re-layouts: 5.89 us -> 2.84 us
  matrix products: 1.94 us -> 0 us
  Pallas kernels: 19.1 us -> 21 us
    all_to_all x0 -> x1, blocking collectives: none -> 15.8 us  [everyone(): lax.all_to_all(copies, 'row', split_axis=0, concat_axis=0, tiled=True)]
    all_to_all x2 -> x1, waiting for transfers between devices: 13.9 us -> 2.38 us  [everyone(): lax.all_to_all(copies, 'row', split_axis=0, concat_axis=0, tiled=True)]
    all_to_all x2 -> x1, starting transfers between devices: 13.8 us -> 4.68 us  [everyone(): lax.all_to_all(copies, 'row', split_axis=0, concat_axis=0, tiled=True)]
    ppermute x18 -> x13, starting transfers between devices: 28.2 us -> 24.1 us  [local(): move = lambda v, to: lax.ppermute(v, 'row', to)]
    dot_general x2 -> x0, matrix products: 1.94 us -> none  [the longest x1 1.51 us: local(): lax.dot_general(w_query, w_key, (((1,), (1,)), ((), ())), preferred_eleme...]
    pallas_call x12 -> x14, Pallas kernels: 19.1 us -> 21 us  [call(): pl.pallas_call(kernel, out_shape=outs, in_specs=specs, out_specs=jax.tree...]
    unnamed x22 -> x26, local copies, waits for them, and re-layouts: 3.41 us -> 2.17 us
    slice x2 -> x0, local copies, waits for them, and re-layouts: 1.17 us -> none  [the longest x1 1.15 us: local(): a, b = (x[:half], x[half:])]
  transfers between devices with their start and end apart: 20 -> 14, of which waited for: 6 -> 6; matrix products, arithmetic and copies ran while one was open for 4% -> 1% of each run, Pallas kernels for 13% -> 17%
where the time goes in v2:
time: 82.6 us; the launch traced here: 82.3 us
  starting transfers between devices  28.7 us (35%)
  Pallas kernels  21 us (25%)
  blocking collectives  15.8 us (19%)
  waiting for transfers between devices  13.6 us (16%)
  local copies, waits for them, and re-layouts  2.84 us (3%)
    ppermute x13, starting transfers between devices, local(): move = lambda v, to: lax.ppermute(v, 'row', to)  24.1 us
    pallas_call x14, Pallas kernels, call(): pl.pallas_call(kernel, out_shape=outs, in_specs=specs, out_specs=jax.tree...  21 us
    all_to_all x1, blocking collectives, everyone(): lax.all_to_all(copies, 'row', split_axis=0, concat_axis=0, tiled=True)  15.8 us
    ppermute x13, waiting for transfers between devices, local(): move = lambda v, to: lax.ppermute(v, 'row', to)  11.2 us
    all_to_all x1, starting transfers between devices, everyone(): lax.all_to_all(copies, 'row', split_axis=0, concat_axis=0, tiled=True)  4.68 us
    all_to_all x1, waiting for transfers between devices, everyone(): lax.all_to_all(copies, 'row', split_axis=0, concat_axis=0, tiled=True)  2.38 us
    unnamed x26, local copies, waits for them, and re-layouts  2.17 us
  transfers between devices with their start and end apart: 14, of which 6 were waited for; matrix products, arithmetic and copies ran while one was open for 1% of the time, Pallas kernels for 17%

profile of v2, /device:TPU:1, one launch (start us, length us, event | category | flops | bytes accessed | tf_op | source)
XLA Modules:
  0.0 82.3 jit_solution(18110048450243917871)
XLA Ops:
  0.1 6.4 %collective-permute-start = (bf16[512,512]{1,0:T(8,128)(2,1)}, bf16[512,512]{1,0:T(8,128)(2,1)S(1)}, u32[]{:S(2)}, u32[]{:S(2)}) collective-permute-start(bf16[512,512]{1,0:T(8,128)(2,1)} %bitcast.11), channel_id=1, source_target_pairs={{0,2},{1,15},{2,4},{3,1},{4,6},{5,3},{6,8},{7,5},{8,10},{9,7},{10,... | collective-permute-start | bytes 1572872 | tf_op jit(solution)/shard_map/ppermute | solution.py:292
  6.5 1.1 %copy-done = bf16[4,128,512]{2,1,0:T(8,128)(2,1)S(1)} copy-done((bf16[4,128,512]{2,1,0:T(8,128)(2,1)S(1)}, bf16[4,128,512]{2,1,0:T(8,128)(2,1)}, u32[]{:S(2)}) %copy-start) | copy-done | bytes 524312
  7.6 0.9 %shard_map.109 = f32[8,128]{1,0:T(8,128)S(1)} custom-call(bf16[512,512]{1,0:T(8,128)(2,1)S(1)} %bitcast.13), custom_call_target="tpu_custom_call" | custom-call | flops 20000000000 | bytes 524288 | tf_op jit(solution)/shard_map/pallas_call | solution.py:25
  8.4 0.7 broadcast_in_dim.6
  9.1 4.7 %all-to-all-start = ((f32[16,8,128]{2,1,0:T(8,128)}), f32[16,8,128]{2,1,0:T(8,128)S(1)}, u32[]{:S(2)}, u32[]{:S(2)}) async-start(f32[16,8,128]{2,1,0:T(8,128)} %broadcast_in_dim.6), calls=%async_computation | async-start | bytes 131072 | tf_op jit(solution)/shard_map/all_to_all | solution.py:274
  13.8 2.6 %collective-permute-start.7 = (bf16[512,512]{1,0:T(8,128)(2,1)}, bf16[512,512]{1,0:T(8,128)(2,1)S(1)}, u32[]{:S(2)}, u32[]{:S(2)}) collective-permute-start(bf16[512,512]{1,0:T(8,128)(2,1)} %collective-permute-done.6), channel_id=1, source_target_pairs={{0,2},{1,15},{2,4},{3,1},{4,6},{5,3},{6,8},{7,5},{8,10},{9,7},{10,... | collective-permute-start | bytes 1572872 | tf_op jit(solution)/shard_map/ppermute | solution.py:292
  16.5 1.2 %collective-permute-start.1 = (bf16[512,512]{1,0:T(8,128)(2,1)S(1)}, bf16[512,512]{1,0:T(8,128)(2,1)S(1)}, u32[]{:S(2)}, u32[]{:S(2)}) collective-permute-start(bf16[512,512]{1,0:T(8,128)(2,1)S(1)} %collective-permute-done.refs_2_), channel_id=1, source_target_pairs={{0,2},{1,15},{2,4},{3,1},{4,6},{5,3},{6,8},{7,5},{8,10},{9,7},{10,... | collective-permute-start | bytes 1572872 | tf_op jit(solution)/shard_map/ppermute | solution.py:292
  17.6 1.0 %copy-done.5 = bf16[512,512]{1,0:T(8,128)(2,1)S(1)} copy-done((bf16[512,512]{1,0:T(8,128)(2,1)S(1)}, bf16[512,512]{1,0:T(8,128)(2,1)}, u32[]{:S(2)}) %copy-start.5) | copy-done | bytes 524312
  19.2 2.4 %all-to-all-done.stats_ref = f32[16,8,128]{2,1,0:T(8,128)S(1)} async-done(((f32[16,8,128]{2,1,0:T(8,128)}), f32[16,8,128]{2,1,0:T(8,128)S(1)}, u32[]{:S(2)}, u32[]{:S(2)}) %all-to-all-start) | async-done | bytes 65568 | tf_op jit(solution)/shard_map/all_to_all | solution.py:274
  21.5 0.5 shard_map.111
  22.1 1.5 %collective-permute-done.7.refs_2_ = bf16[512,512]{1,0:T(8,128)(2,1)S(1)} collective-permute-done((bf16[512,512]{1,0:T(8,128)(2,1)}, bf16[512,512]{1,0:T(8,128)(2,1)S(1)}, u32[]{:S(2)}, u32[]{:S(2)}) %collective-permute-start.7) | collective-permute-done | bytes 524320 | tf_op jit(solution)/shard_map/ppermute | solution.py:292
  23.6 2.5 %collective-permute-start.8 = (bf16[512,512]{1,0:T(8,128)(2,1)S(1)}, bf16[512,512]{1,0:T(8,128)(2,1)S(1)}, u32[]{:S(2)}, u32[]{:S(2)}) collective-permute-start(bf16[512,512]{1,0:T(8,128)(2,1)S(1)} %collective-permute-done.7.refs_2_), channel_id=1, source_target_pairs={{0,2},{1,15},{2,4},{3,1},{4,6},{5,3},{6,8},{7,5},{8,10},{9,7},{10,... | collective-permute-start | bytes 1572872 | tf_op jit(solution)/shard_map/ppermute | solution.py:292
  26.1 3.1 %collective-permute-done.1.refs_2_ = bf16[512,512]{1,0:T(8,128)(2,1)S(1)} collective-permute-done((bf16[512,512]{1,0:T(8,128)(2,1)S(1)}, bf16[512,512]{1,0:T(8,128)(2,1)S(1)}, u32[]{:S(2)}, u32[]{:S(2)}) %collective-permute-start.1) | collective-permute-done | bytes 524320 | tf_op jit(solution)/shard_map/ppermute | solution.py:292
  29.2 2.5 %collective-permute-start.2 = (bf16[512,512]{1,0:T(8,128)(2,1)S(1)}, bf16[512,512]{1,0:T(8,128)(2,1)S(1)}, u32[]{:S(2)}, u32[]{:S(2)}) collective-permute-start(bf16[512,512]{1,0:T(8,128)(2,1)S(1)} %collective-permute-done.1.refs_2_), channel_id=1, source_target_pairs={{0,2},{1,15},{2,4},{3,1},{4,6},{5,3},{6,8},{7,5},{8,10},{9,7},{10,... | collective-permute-start | bytes 1572872 | tf_op jit(solution)/shard_map/ppermute | solution.py:292
  31.7 3.1 %collective-permute-done.8.refs_2_ = bf16[512,512]{1,0:T(8,128)(2,1)S(1)} collective-permute-done((bf16[512,512]{1,0:T(8,128)(2,1)S(1)}, bf16[512,512]{1,0:T(8,128)(2,1)S(1)}, u32[]{:S(2)}, u32[]{:S(2)}) %collective-permute-start.8) | collective-permute-done | bytes 524320 | tf_op jit(solution)/shard_map/ppermute | solution.py:292
  34.8 2.5 %collective-permute-start.9 = (bf16[512,512]{1,0:T(8,128)(2,1)S(1)}, bf16[512,512]{1,0:T(8,128)(2,1)S(1)}, u32[]{:S(2)}, u32[]{:S(2)}) collective-permute-start(bf16[512,512]{1,0:T(8,128)(2,1)S(1)} %collective-permute-done.8.refs_2_), channel_id=1, source_target_pairs={{0,2},{1,15},{2,4},{3,1},{4,6},{5,3},{6,8},{7,5},{8,10},{9,7},{10,... | collective-permute-start | bytes 1572872 | tf_op jit(solution)/shard_map/ppermute | solution.py:292
  37.4 1.3 %shard_map.112 = (f32[512,512]{1,0:T(8,128)S(1)}, f32[512,128]{1,0:T(8,128)S(1)}, f32[512,128]{1,0:T(8,128)S(1)}, f32[512,512]{1,0:T(8,128)S(1)}, f32[512,128]{1,0:T(8,128)S(1)}, /*index=5*/f32[512,128]{1,0:T(8,128)S(1)}) custom-call(bf16[512,512]{1,0:T(8,128)(2,1)S(1)} %get-tuple-element.58.refs_0_.q_ref, ...), custom_call_target="tpu_custom_call" | custom-call | flops 1073741824 | bytes 1572864 | tf_op jit(solution)/shard_map/pallas_call | solution.py:25
  38.7 1.8 %collective-permute-done.2.refs_2_ = bf16[512,512]{1,0:T(8,128)(2,1)S(1)} collective-permute-done((bf16[512,512]{1,0:T(8,128)(2,1)S(1)}, bf16[512,512]{1,0:T(8,128)(2,1)S(1)}, u32[]{:S(2)}, u32[]{:S(2)}) %collective-permute-start.2) | collective-permute-done | bytes 524320 | tf_op jit(solution)/shard_map/ppermute | solution.py:292
  40.4 2.5 %collective-permute-start.3 = (bf16[512,512]{1,0:T(8,128)(2,1)S(1)}, bf16[512,512]{1,0:T(8,128)(2,1)S(1)}, u32[]{:S(2)}, u32[]{:S(2)}) collective-permute-start(bf16[512,512]{1,0:T(8,128)(2,1)S(1)} %collective-permute-done.2.refs_2_), channel_id=1, source_target_pairs={{0,2},{1,15},{2,4},{3,1},{4,6},{5,3},{6,8},{7,5},{8,10},{9,7},{10,... | collective-permute-start | bytes 1572872 | tf_op jit(solution)/shard_map/ppermute | solution.py:292
  43.0 1.6 %shard_map.113 = (f32[512,512]{1,0:T(8,128)S(1)}, f32[512,128]{1,0:T(8,128)S(1)}, f32[512,128]{1,0:T(8,128)S(1)}, f32[512,512]{1,0:T(8,128)S(1)}, f32[512,128]{1,0:T(8,128)S(1)}, /*index=5*/f32[512,128]{1,0:T(8,128)S(1)}) custom-call(bf16[512,512]{1,0:T(8,128)(2,1)S(1)} %get-tuple-element., ...), custom_call_target="tpu_custom_call", output_to_operand_aliasing={{0}: (3, {}), {1}: (4, {}), {2}: (5, {}), {3}: (6, {}), {4}... | custom-call | flops 1073741824 | bytes 4718592 | tf_op jit(solution)/shard_map/pallas_call | solution.py:25
  44.6 1.6 %shard_map.114 = (f32[512,512]{1,0:T(8,128)S(1)}, f32[512,128]{1,0:T(8,128)S(1)}, f32[512,128]{1,0:T(8,128)S(1)}, f32[512,512]{1,0:T(8,128)S(1)}, f32[512,128]{1,0:T(8,128)S(1)}, /*index=5*/f32[512,128]{1,0:T(8,128)S(1)}) custom-call(bf16[512,512]{1,0:T(8,128)(2,1)S(1)} %get-tuple-element., ...), custom_call_target="tpu_custom_call", output_to_operand_aliasing={{0}: (3, {}), {1}: (4, {}), {2}: (5, {}), {3}: (6, {}), {4}... | custom-call | flops 1073741824 | bytes 4718592 | tf_op jit(solution)/shard_map/pallas_call | solution.py:25
  46.2 1.6 %shard_map.115 = (f32[512,512]{1,0:T(8,128)S(1)}, f32[512,128]{1,0:T(8,128)S(1)}, f32[512,128]{1,0:T(8,128)S(1)}, f32[512,512]{1,0:T(8,128)S(1)}, f32[512,128]{1,0:T(8,128)S(1)}, /*index=5*/f32[512,128]{1,0:T(8,128)S(1)}) custom-call(bf16[512,512]{1,0:T(8,128)(2,1)S(1)} %get-tuple-element., ...), custom_call_target="tpu_custom_call", output_to_operand_aliasing={{0}: (3, {}), {1}: (4, {}), {2}: (5, {}), {3}: (6, {}), {4}... | custom-call | flops 1073741824 | bytes 4718592 | tf_op jit(solution)/shard_map/pallas_call | solution.py:25
  47.9 1.6 %shard_map.116 = (f32[512,512]{1,0:T(8,128)S(1)}, f32[512,128]{1,0:T(8,128)S(1)}, f32[512,128]{1,0:T(8,128)S(1)}, f32[512,512]{1,0:T(8,128)S(1)}, f32[512,128]{1,0:T(8,128)S(1)}, /*index=5*/f32[512,128]{1,0:T(8,128)S(1)}) custom-call(bf16[512,512]{1,0:T(8,128)(2,1)S(1)} %get-tuple-element., ...), custom_call_target="tpu_custom_call", output_to_operand_aliasing={{0}: (3, {}), {1}: (4, {}), {2}: (5, {}), {3}: (6, {}), {4}... | custom-call | flops 1073741824 | bytes 4718592 | tf_op jit(solution)/shard_map/pallas_call | solution.py:25
  49.5 1.6 %shard_map.117 = (f32[512,512]{1,0:T(8,128)S(1)}, f32[512,128]{1,0:T(8,128)S(1)}, f32[512,128]{1,0:T(8,128)S(1)}, f32[512,512]{1,0:T(8,128)S(1)}, f32[512,128]{1,0:T(8,128)S(1)}, /*index=5*/f32[512,128]{1,0:T(8,128)S(1)}) custom-call(bf16[512,512]{1,0:T(8,128)(2,1)S(1)} %get-tuple-element., ...), custom_call_target="tpu_custom_call", output_to_operand_aliasing={{0}: (3, {}), {1}: (4, {}), {2}: (5, {}), {3}: (6, {}), {4}... | custom-call | flops 1073741824 | bytes 4718592 | tf_op jit(solution)/shard_map/pallas_call | solution.py:25
  51.2 1.6 %shard_map.118 = (f32[512,512]{1,0:T(8,128)S(1)}, f32[512,128]{1,0:T(8,128)S(1)}, f32[512,128]{1,0:T(8,128)S(1)}, f32[512,640]{1,0:T(8,128)S(1)}) custom-call(bf16[512,512]{1,0:T(8,128)(2,1)S(1)} %get-tuple-element.58.refs_0_.q_ref, bf16[512,512]{1,0:T(8,128)(2,1)S(1)} %collective-permute-done.5.refs_1_, ...), custom_call_target="tpu_custom_call", output_to_operand_aliasing={{0}: (3, {}), {1}: (4, {}), {2}: (5, {})} | custom-call | flops 1073741824 | bytes 4718592 | tf_op jit(solution)/shard_map/pallas_call | solution.py:25
  52.9 0.7 collective-permute-start.4
  54.1 0.9 %shard_map.119 = (f32[512,512]{1,0:T(8,128)S(1)}, f32[512,128]{1,0:T(8,128)S(1)}, f32[512,128]{1,0:T(8,128)S(1)}) custom-call(bf16[512,512]{1,0:T(8,128)(2,1)S(1)} %get-tuple-element.58.refs_0_.q_ref, bf16[512,512]{1,0:T(8,128)(2,1)S(1)} %collective-permute-done.3.refs_1_, ...), custom_call_target="tpu_custom_call", output_to_operand_aliasing={{0}: (2, {}), {1}: (3, {}), {2}: (4, {})} | custom-call | flops 536870912 | bytes 2621440 | tf_op jit(solution)/shard_map/pallas_call | solution.py:25
  55.0 1.7 %collective-permute-done.4.key_ref = bf16[512,512]{1,0:T(8,128)(2,1)S(1)} collective-permute-done((bf16[512,512]{1,0:T(8,128)(2,1)S(1)}, bf16[512,512]{1,0:T(8,128)(2,1)S(1)}, u32[]{:S(2)}, u32[]{:S(2)}) %collective-permute-start.4) | collective-permute-done | bytes 524320 | tf_op jit(solution)/shard_map/ppermute | solution.py:292
  56.7 2.7 %shard_map.121 = (bf16[512,512]{1,0:T(8,128)(2,1)S(1)}, f32[8,128]{1,0:T(8,128)S(1)}, bf16[128,512]{1,0:T(8,128)(2,1)S(1)}, bf16[128,512]{1,0:T(8,128)(2,1)S(1)}) custom-call(s32[3]{0:T(128)S(1)} %add_convert_fusion.flags_ref, bf16[512,512]{1,0:T(8,128)(2,1)S(1)} %get-tuple-element.58.refs_0_.q_ref, bf16[512,512]{1,0:T(8,128)(2,1)S(1)} %collective-permute-done.4.key_ref, ...), custom_call_target="tpu_custom_call" | custom-call | flops 805306368 | bytes 4997132 | tf_op jit(solution)/shard_map/pallas_call | solution.py:25
  59.9 2.5 %collective-permute-start.12 = (bf16[128,512]{1,0:T(8,128)(2,1)S(1)}, bf16[128,512]{1,0:T(8,128)(2,1)S(1)}, u32[]{:S(2)}, u32[]{:S(2)}) collective-permute-start(bf16[128,512]{1,0:T(8,128)(2,1)S(1)} %get-tuple-element.105), channel_id=1, source_target_pairs={{1,2},{3,4},{5,6},{7,8},{9,10},{11,12},{13,14},{2,1},{4,3},{6,5},{... | collective-permute-start | bytes 393224 | tf_op jit(solution)/shard_map/ppermute | solution.py:292
  62.4 15.8 %all_to_all.10.stats_ref = f32[16,8,128]{2,1,0:T(8,128)S(1)} all-to-all(f32[16,8,128]{2,1,0:T(8,128)S(1)} %broadcast_in_dim.7), channel_id=1, replica_groups=mesh['img'=16,'row'=16] {'row'}, dimensions={0} | all-to-all | bytes 131072 | tf_op jit(solution)/shard_map/all_to_all | solution.py:274
  78.2 4.0 %shard_map.122 = bf16[512,512]{1,0:T(8,128)(2,1)} custom-call(s32[3]{0:T(128)S(1)} %add_convert_fusion.flags_ref, bf16[512,512]{1,0:T(8,128)(2,1)S(1)} %get-tuple-element.103.h_ref, bf16[128,512]{1,0:T(8,128)(2,1)S(1)} %collective-permute-done.11.inside_ref, bf16[128,512]{1,0:T(8,128)(2,1)S(1)} %collective-permute-done.12.outside_ref, ...), custom_call_target="tpu_custom_call" | custom-call | flops 2415919104 | bytes 5576716 | tf_op jit(solution)/shard_map/pallas_call | solution.py:25
  (41 shorter events, 1.6 us)
Async XLA Ops:
  0.1 16.4 %collective-permute-start = (bf16[512,512]{1,0:T(8,128)(2,1)}, bf16[512,512]{1,0:T(8,128)(2,1)S(1)}, u32[]{:S(2)}, u32[]{:S(2)}) collective-permute-start(bf16[512,512]{1,0:T(8,128)(2,1)} %bitcast.11), channel_id=1, source_target_pairs={{0,2},{1,15},{2,4},{3,1},{4,6},{5,3},{6,8},{7,5},{8,10},{9,7},{10,... | collective-permute-start | bytes 1572872 | tf_op jit(solution)/shard_map/ppermute | solution.py:292
  6.5 7.3 %collective-permute-start.6 = (bf16[512,512]{1,0:T(8,128)(2,1)}, bf16[512,512]{1,0:T(8,128)(2,1)}, u32[]{:S(2)}, u32[]{:S(2)}) collective-permute-start(bf16[512,512]{1,0:T(8,128)(2,1)} %bitcast.12), channel_id=1, source_target_pairs={{0,1},{1,0},{2,3},{3,2},{4,5},{5,4},{6,7},{7,6},{8,9},{9,8},{10,11... | collective-permute-start | bytes 1572872 | tf_op jit(solution)/shard_map/ppermute | solution.py:292
  6.5 1.1 %copy-start = (bf16[4,128,512]{2,1,0:T(8,128)(2,1)S(1)}, bf16[4,128,512]{2,1,0:T(8,128)(2,1)}, u32[]{:S(2)}) copy-start(bf16[4,128,512]{2,1,0:T(8,128)(2,1)} %param.11) | copy-start | bytes 1572868
  7.6 10.1 %copy-start.4 = (bf16[512,512]{1,0:T(8,128)(2,1)S(1)}, bf16[512,512]{1,0:T(8,128)(2,1)}, u32[]{:S(2)}) copy-start(bf16[512,512]{1,0:T(8,128)(2,1)} %refs_0_.2) | copy-start | bytes 1572868
  9.1 12.5 %all-to-all-start = ((f32[16,8,128]{2,1,0:T(8,128)}), f32[16,8,128]{2,1,0:T(8,128)S(1)}, u32[]{:S(2)}, u32[]{:S(2)}) async-start(f32[16,8,128]{2,1,0:T(8,128)} %broadcast_in_dim.6), calls=%async_computation | async-start | bytes 131072 | tf_op jit(solution)/shard_map/all_to_all | solution.py:274
  13.8 7.8 %copy-start.1 = (bf16[4,128,512]{2,1,0:T(8,128)(2,1)S(1)}, bf16[4,128,512]{2,1,0:T(8,128)(2,1)}, u32[]{:S(2)}) copy-start(bf16[4,128,512]{2,1,0:T(8,128)(2,1)} %param.11) | copy-start | bytes 1572868
  13.8 7.8 %copy-start.2 = (f32[512]{0:T(512)S(1)}, f32[512]{0:T(512)}, u32[]{:S(2)}) copy-start(f32[512]{0:T(512)} %param.12) | copy-start | bytes 6148
  13.8 7.8 %copy-start.3 = (f32[512]{0:T(512)S(1)}, f32[512]{0:T(512)}, u32[]{:S(2)}) copy-start(f32[512]{0:T(512)} %param.13) | copy-start | bytes 6148
  13.8 9.8 %collective-permute-start.7 = (bf16[512,512]{1,0:T(8,128)(2,1)}, bf16[512,512]{1,0:T(8,128)(2,1)S(1)}, u32[]{:S(2)}, u32[]{:S(2)}) collective-permute-start(bf16[512,512]{1,0:T(8,128)(2,1)} %collective-permute-done.6), channel_id=1, source_target_pairs={{0,2},{1,15},{2,4},{3,1},{4,6},{5,3},{6,8},{7,5},{8,10},{9,7},{10,... | collective-permute-start | bytes 1572872 | tf_op jit(solution)/shard_map/ppermute | solution.py:292
  16.5 12.7 %collective-permute-start.1 = (bf16[512,512]{1,0:T(8,128)(2,1)S(1)}, bf16[512,512]{1,0:T(8,128)(2,1)S(1)}, u32[]{:S(2)}, u32[]{:S(2)}) collective-permute-start(bf16[512,512]{1,0:T(8,128)(2,1)S(1)} %collective-permute-done.refs_2_), channel_id=1, source_target_pairs={{0,2},{1,15},{2,4},{3,1},{4,6},{5,3},{6,8},{7,5},{8,10},{9,7},{10,... | collective-permute-start | bytes 1572872 | tf_op jit(solution)/shard_map/ppermute | solution.py:292
  17.6 1.0 %copy-start.5 = (bf16[512,512]{1,0:T(8,128)(2,1)S(1)}, bf16[512,512]{1,0:T(8,128)(2,1)}, u32[]{:S(2)}) copy-start(bf16[512,512]{1,0:T(8,128)(2,1)} %refs_1_.2) | copy-start | bytes 1572868
  23.6 11.2 %collective-permute-start.8 = (bf16[512,512]{1,0:T(8,128)(2,1)S(1)}, bf16[512,512]{1,0:T(8,128)(2,1)S(1)}, u32[]{:S(2)}, u32[]{:S(2)}) collective-permute-start(bf16[512,512]{1,0:T(8,128)(2,1)S(1)} %collective-permute-done.7.refs_2_), channel_id=1, source_target_pairs={{0,2},{1,15},{2,4},{3,1},{4,6},{5,3},{6,8},{7,5},{8,10},{9,7},{10,... | collective-permute-start | bytes 1572872 | tf_op jit(solution)/shard_map/ppermute | solution.py:292
  26.1 11.2 %collective-permute-start.5 = (bf16[512,512]{1,0:T(8,128)(2,1)S(1)}, bf16[512,512]{1,0:T(8,128)(2,1)S(1)}, u32[]{:S(2)}, u32[]{:S(2)}) collective-permute-start(bf16[512,512]{1,0:T(8,128)(2,1)S(1)} %get-tuple-element.58.refs_0_.q_ref), channel_id=1, source_target_pairs={{0,1},{1,0},{2,3},{3,2},{4,5},{5,4},{6,7},{7,6},{8,9},{9,8},{10,11... | collective-permute-start | bytes 1572872 | tf_op jit(solution)/shard_map/ppermute | solution.py:292
  29.2 11.2 %collective-permute-start.2 = (bf16[512,512]{1,0:T(8,128)(2,1)S(1)}, bf16[512,512]{1,0:T(8,128)(2,1)S(1)}, u32[]{:S(2)}, u32[]{:S(2)}) collective-permute-start(bf16[512,512]{1,0:T(8,128)(2,1)S(1)} %collective-permute-done.1.refs_2_), channel_id=1, source_target_pairs={{0,2},{1,15},{2,4},{3,1},{4,6},{5,3},{6,8},{7,5},{8,10},{9,7},{10,... | collective-permute-start | bytes 1572872 | tf_op jit(solution)/shard_map/ppermute | solution.py:292
  34.8 16.3 %collective-permute-start.9 = (bf16[512,512]{1,0:T(8,128)(2,1)S(1)}, bf16[512,512]{1,0:T(8,128)(2,1)S(1)}, u32[]{:S(2)}, u32[]{:S(2)}) collective-permute-start(bf16[512,512]{1,0:T(8,128)(2,1)S(1)} %collective-permute-done.8.refs_2_), channel_id=1, source_target_pairs={{0,2},{1,15},{2,4},{3,1},{4,6},{5,3},{6,8},{7,5},{8,10},{9,7},{10,... | collective-permute-start | bytes 1572872 | tf_op jit(solution)/shard_map/ppermute | solution.py:292
  40.4 12.5 %collective-permute-start.3 = (bf16[512,512]{1,0:T(8,128)(2,1)S(1)}, bf16[512,512]{1,0:T(8,128)(2,1)S(1)}, u32[]{:S(2)}, u32[]{:S(2)}) collective-permute-start(bf16[512,512]{1,0:T(8,128)(2,1)S(1)} %collective-permute-done.2.refs_2_), channel_id=1, source_target_pairs={{0,2},{1,15},{2,4},{3,1},{4,6},{5,3},{6,8},{7,5},{8,10},{9,7},{10,... | collective-permute-start | bytes 1572872 | tf_op jit(solution)/shard_map/ppermute | solution.py:292
  47.8 5.8 %slice-start = ((s8[4718592]{0:T(1024)(128)(4,1)}), s8[4194304]{0:T(1024)(128)(4,1)S(1)}, s32[]{:S(2)}) async-start(s8[4718592]{0:T(1024)(128)(4,1)} %bitcast.19), calls=%async_computation.2 | async-start | bytes 8388608
  49.5 4.1 %slice-start.1 = ((s8[4718592]{0:T(1024)(128)(4,1)}), s8[524288]{0:T(1024)(128)(4,1)S(1)}, s32[]{:S(2)}) async-start(s8[4718592]{0:T(1024)(128)(4,1)} %bitcast.19), calls=%async_computation.3 | async-start | bytes 1048576
  51.1 2.5 %copy-start.6 = (bf16[512,512]{1,0:T(8,128)(2,1)S(1)}, bf16[512,512]{1,0:T(8,128)(2,1)}, u32[]{:S(2)}) copy-start(bf16[512,512]{1,0:T(8,128)(2,1)} %refs_0_.3) | copy-start | bytes 1572868
  51.2 2.4 %copy-start.7 = (bf16[512,512]{1,0:T(8,128)(2,1)S(1)}, bf16[512,512]{1,0:T(8,128)(2,1)}, u32[]{:S(2)}) copy-start(bf16[512,512]{1,0:T(8,128)(2,1)} %refs_1_.3) | copy-start | bytes 1572868
  52.8 3.9 %collective-permute-start.10 = (f32[512,640]{1,0:T(8,128)S(1)}, f32[512,640]{1,0:T(8,128)S(1)}, u32[]{:S(2)}, u32[]{:S(2)}) collective-permute-start(f32[512,640]{1,0:T(8,128)S(1)} %get-tuple-element.101), channel_id=1, source_target_pairs={{0,1},{1,0},{2,3},{3,2},{4,5},{5,4},{6,7},{7,6},{8,9},{9,8},{10,11... | collective-permute-start | bytes 3932168 | tf_op jit(solution)/shard_map/ppermute | solution.py:292
  52.9 3.8 %collective-permute-start.4 = (bf16[512,512]{1,0:T(8,128)(2,1)S(1)}, bf16[512,512]{1,0:T(8,128)(2,1)S(1)}, u32[]{:S(2)}, u32[]{:S(2)}) collective-permute-start(bf16[512,512]{1,0:T(8,128)(2,1)S(1)} %collective-permute-done.3.refs_1_), channel_id=1, source_target_pairs={{0,1},{1,0},{2,3},{3,2},{4,5},{5,4},{6,7},{7,6},{8,9},{9,8},{10,11... | collective-permute-start | bytes 1572872 | tf_op jit(solution)/shard_map/ppermute | solution.py:292
  56.7 21.5 %copy-start.8 = (f32[512]{0:T(512)S(1)}, f32[512]{0:T(512)}, u32[]{:S(2)}) copy-start(f32[512]{0:T(512)} %param.18) | copy-start | bytes 6148
  56.7 21.5 %copy-start.9 = (f32[512]{0:T(512)S(1)}, f32[512]{0:T(512)}, u32[]{:S(2)}) copy-start(f32[512]{0:T(512)} %param.19) | copy-start | bytes 6148
  56.7 21.5 %copy-start.10 = (f32[512]{0:T(512)S(1)}, f32[512]{0:T(512)}, u32[]{:S(2)}) copy-start(f32[512]{0:T(512)} %param.21) | copy-start | bytes 6148
  59.5 18.8 %collective-permute-start.11 = (bf16[128,512]{1,0:T(8,128)(2,1)S(1)}, bf16[128,512]{1,0:T(8,128)(2,1)S(1)}, u32[]{:S(2)}, u32[]{:S(2)}) collective-permute-start(bf16[128,512]{1,0:T(8,128)(2,1)S(1)} %get-tuple-element.104), channel_id=1, source_target_pairs={{0,1},{1,0},{2,3},{3,2},{4,5},{5,4},{6,7},{7,6},{8,9},{9,8},{10,11... | collective-permute-start | bytes 393224 | tf_op jit(solution)/shard_map/ppermute | solution.py:292
  59.9 18.3 %collective-permute-start.12 = (bf16[128,512]{1,0:T(8,128)(2,1)S(1)}, bf16[128,512]{1,0:T(8,128)(2,1)S(1)}, u32[]{:S(2)}, u32[]{:S(2)}) collective-permute-start(bf16[128,512]{1,0:T(8,128)(2,1)S(1)} %get-tuple-element.105), channel_id=1, source_target_pairs={{1,2},{3,4},{5,6},{7,8},{9,10},{11,12},{13,14},{2,1},{4,3},{6,5},{... | collective-permute-start | bytes 393224 | tf_op jit(solution)/shard_map/ppermute | solution.py:292

commit v3 on v2

--- a/solution.py
+++ b/solution.py
@@ -89,16 +89,23 @@
     return call(kernel, out, [VMEM] * len(args), args, AHEAD, 8)
 
 
-def query_kernel(x_ref, stats_ref, gain_ref, shift_ref, wqk_ref, q_ref, coef_ref):
-    scale, shift = affine(stats_ref[...], gain_ref[...], shift_ref[...], x_ref.shape[0])
+def query_kernel(
+    flags_ref, x_ref, far_ref, stats_ref, gain_ref, shift_ref, wqk_ref, q_ref, coef_ref, halo_ref
+):
+    rows = x_ref.shape[0]
+    scale, shift = affine(stats_ref[...], gain_ref[...], shift_ref[...], rows)
     coef_ref[0:1, :] = scale
     coef_ref[1:2, :] = shift
-    normed = (x_ref[...].astype(F32) * scale + shift).astype(BF16)
-    q = jnp.dot(normed, wqk_ref[...], preferred_element_type=F32)
-    q_ref[...] = (q * (scale * (LOG2E / C**0.5))).astype(BF16)
-
-
-BLOCK = 256
+    halo = jnp.where(flags_ref[2] > 0, far_ref[rows - W : rows, :], far_ref[0:W, :])
+    halo_ref[...] = halo
+    for x, at in ((x_ref[...], slice(0, rows)), (halo, slice(rows, rows + W))):
+        normed = (x.astype(F32) * scale + shift).astype(BF16)
+        q = jnp.dot(normed, wqk_ref[...], preferred_element_type=F32)
+        q_ref[at, :] = (q * (scale * (LOG2E / C**0.5))).astype(BF16)
+
+
+BLOCK = 320
+TILE = 256
 
 
 def scores_of(q, keys):
@@ -193,17 +200,18 @@
 
 
 def output_kernel(
-    flags_ref, q_ref, key_ref, acc_ref, top_ref, part_ref, met_ref, x_ref, coef_ref, wvo_ref,
-    hidden_ref, stats_ref, inside_ref, outside_ref,
+    flags_ref, q_ref, key_ref, acc_ref, top_ref, part_ref, met_ref, x_ref, halo_ref, coef_ref,
+    wvo_ref, hidden_ref, stats_ref, inside_ref, outside_ref,
 ):
     keys = [key_ref]
-    rows = q_ref.shape[0]
-    ahead = scores_of(q_ref[0:BLOCK, :], keys)
-    for r in range(0, rows, BLOCK):
-        at = slice(r, r + BLOCK)
+    rows = x_ref.shape[0]
+    half = rows // 2
+    blocks = [slice(0, half), slice(half, rows), slice(rows, rows + W)]
+    ahead = scores_of(q_ref[blocks[0], :], keys)
+    for n, at in enumerate(blocks):
         now = ahead
-        if r + BLOCK < rows:
-            ahead = scores_of(q_ref[r + BLOCK : r + 2 * BLOCK, :], keys)
+        if n + 1 < len(blocks):
+            ahead = scores_of(q_ref[blocks[n + 1], :], keys)
         acc, top, part = absorb(now, keys, (acc_ref[at, :], top_ref[at, :], part_ref[at, :]))
         total = jnp.broadcast_to(jnp.sum(part, axis=1, keepdims=True), top.shape)
         edge = met_ref[at, C : C + LANES]
@@ -214,15 +222,15 @@
         inverse = 1.0 / (total * wa + other_total * wb)
         mixed = acc * wide(wa * inverse) + met_ref[at, 0:C] * wide(wb * inverse)
         normed = (mixed * coef_ref[0:1, :] + coef_ref[1:2, :]).astype(BF16)
-        hidden = x_ref[at, :].astype(F32) + jnp.dot(
-            normed, wvo_ref[...], preferred_element_type=F32
-        )
-        hidden_ref[at, :] = hidden.astype(BF16)
-    first = hidden_ref[0:W, :]
-    last = hidden_ref[rows - W : rows, :]
-    even = flags_ref[2] > 0
-    inside_ref[...] = jnp.where(even, last, first)
-    outside_ref[...] = jnp.where(even, first, last)
+        x = halo_ref[...] if at.start == rows else x_ref[at, :]
+        hidden = x.astype(F32) + jnp.dot(normed, wvo_ref[...], preferred_element_type=F32)
+        if at.start == rows:
+            outside_ref[...] = hidden.astype(BF16)
+        else:
+            hidden_ref[at, :] = hidden.astype(BF16)
+    inside_ref[...] = jnp.where(
+        flags_ref[2] > 0, hidden_ref[rows - W : rows, :], hidden_ref[0:W, :]
+    )
     write_stats(hidden_ref[...].astype(F32), stats_ref)
 
 
@@ -251,20 +259,20 @@
         activate(h_ref[r * W : (r + 1) * W, :], (r + 1) * W, None)
     bottom = jnp.where(even, inside_ref[...], outside_ref[...])
     activate(bottom, rows + W, flags_ref[1] > 0)
-    for r in range(0, rows, BLOCK):
-        for n in range(0, C, BLOCK):
+    for r in range(0, rows, TILE):
+        for n in range(0, C, TILE):
             total = None
             for dy in range(3):
                 for dx, src in enumerate((left_ref, mid_ref, right_ref)):
                     d = jnp.dot(
-                        src[r + dy * W : r + dy * W + BLOCK, :],
-                        w_ref[3 * dy + dx, :, n : n + BLOCK],
+                        src[r + dy * W : r + dy * W + TILE, :],
+                        w_ref[3 * dy + dx, :, n : n + TILE],
                         preferred_element_type=F32,
                     )
                     total = d if total is None else total + d
-            base = h_ref[r : r + BLOCK, n : n + BLOCK].astype(F32)
-            out_ref[r : r + BLOCK, n : n + BLOCK] = (
-                base + (total + bias_ref[:, n : n + BLOCK])
+            base = h_ref[r : r + TILE, n : n + TILE].astype(F32)
+            out_ref[r : r + TILE, n : n + TILE] = (
+                base + (total + bias_ref[:, n : n + TILE])
             ).astype(BF16)
 
 
@@ -305,11 +313,15 @@
             pieces.append(far)
 
     stats = everyone(stats)
-    query, coef = call(
+    query, coef, halo = call(
         query_kernel,
-        [jax.ShapeDtypeStruct((rows, C), BF16), jax.ShapeDtypeStruct((8, C), F32)],
-        [VMEM] * 5,
-        [x, stats, line(attn_gain), line(attn_shift), wqk],
+        [
+            jax.ShapeDtypeStruct((rows + W, C), BF16),
+            jax.ShapeDtypeStruct((8, C), F32),
+            jax.ShapeDtypeStruct((W, C), BF16),
+        ],
+        [SMEM] + [VMEM] * 6,
+        [flags, x, pieces[2], stats, line(attn_gain), line(attn_shift), wqk],
         2 * rows * C * C,
     )
     other = move(query, swap)
@@ -325,14 +337,12 @@
     hidden, tile2, inside, outside = call(
         output_kernel,
         [jax.ShapeDtypeStruct((rows, C), BF16), tile, edge, edge],
-        [SMEM] + [VMEM] * 9,
-        [flags, query, across, *mine, met, x, coef, wvo],
+        [SMEM] + [VMEM] * 10,
+        [flags, query, across, *mine, met, x, halo, coef, wvo],
         6 * rows * C * C,
         20,
     )
-    between = [(i, i + 1) for i in range(1, count - 1, 2)]
     inside = move(inside, swap)
-    outside = move(outside, between + [(b, a) for a, b in between])
     stats2 = everyone(tile2)
     encoded = call(
         conv_kernel,

time: 82.6 us -> 83.3 us (level)
  Pallas kernels: 21 us -> 24.9 us
  starting transfers between devices: 28.7 us -> 26.4 us
  blocking collectives: 15.8 us -> 14.2 us
    pallas_call x14, Pallas kernels: 21 us -> 24.9 us  [call(): pl.pallas_call(kernel, out_shape=outs, in_specs=specs, out_specs=jax.tree...]
    ppermute x13 -> x12, starting transfers between devices: 24.1 us -> 22.4 us  [local(): move = lambda v, to: lax.ppermute(v, 'row', to)]
    all_to_all x1, blocking collectives: 15.8 us -> 14.2 us  [everyone(): lax.all_to_all(copies, 'row', split_axis=0, concat_axis=0, tiled=True)]
    ppermute x13 -> x12, waiting for transfers between devices: 11.2 us -> 12 us  [local(): move = lambda v, to: lax.ppermute(v, 'row', to)]
  transfers between devices with their start and end apart: 14 -> 13, of which waited for: 6 -> 6; matrix products, arithmetic and copies ran while one was open for 1% -> 1% of each run, Pallas kernels for 17% -> 21%
where the time goes in v3:
time: 83.3 us; the launch traced here: 83 us
  starting transfers between devices  26.4 us (32%)
  Pallas kernels  24.9 us (30%)
  waiting for transfers between devices  14.4 us (17%)
  blocking collectives  14.2 us (17%)
  local copies, waits for them, and re-layouts  2.84 us (3%)
    pallas_call x14, Pallas kernels, call(): pl.pallas_call(kernel, out_shape=outs, in_specs=specs, out_specs=jax.tree...  24.9 us
    ppermute x12, starting transfers between devices, local(): move = lambda v, to: lax.ppermute(v, 'row', to)  22.4 us
    all_to_all x1, blocking collectives, everyone(): lax.all_to_all(copies, 'row', split_axis=0, concat_axis=0, tiled=True)  14.2 us
    ppermute x12, waiting for transfers between devices, local(): move = lambda v, to: lax.ppermute(v, 'row', to)  12 us
    all_to_all x1, starting transfers between devices, everyone(): lax.all_to_all(copies, 'row', split_axis=0, concat_axis=0, tiled=True)  4.01 us
    all_to_all x1, waiting for transfers between devices, everyone(): lax.all_to_all(copies, 'row', split_axis=0, concat_axis=0, tiled=True)  2.38 us
    unnamed x26, local copies, waits for them, and re-layouts  2.18 us
  transfers between devices with their start and end apart: 13, of which 6 were waited for; matrix products, arithmetic and copies ran while one was open for 1% of the time, Pallas kernels for 21%

profile of v3, /device:TPU:1, one launch (start us, length us, event | category | flops | bytes accessed | tf_op | source)
XLA Modules:
  0.0 83.0 jit_solution(4587378249333661178)
XLA Ops:
  0.1 3.2 %collective-permute-start = (bf16[512,512]{1,0:T(8,128)(2,1)}, bf16[512,512]{1,0:T(8,128)(2,1)}, u32[]{:S(2)}, u32[]{:S(2)}) collective-permute-start(bf16[512,512]{1,0:T(8,128)(2,1)} %bitcast.11), channel_id=1, source_target_pairs={{0,1},{1,0},{2,3},{3,2},{4,5},{5,4},{6,7},{7,6},{8,9},{9,8},{10,11... | collective-permute-start | bytes 1572872 | tf_op jit(solution)/shard_map/ppermute | solution.py:300
  3.3 3.9 %collective-permute-start.2 = (bf16[512,512]{1,0:T(8,128)(2,1)}, bf16[512,512]{1,0:T(8,128)(2,1)S(1)}, u32[]{:S(2)}, u32[]{:S(2)}) collective-permute-start(bf16[512,512]{1,0:T(8,128)(2,1)} %bitcast.12), channel_id=1, source_target_pairs={{0,2},{1,15},{2,4},{3,1},{4,6},{5,3},{6,8},{7,5},{8,10},{9,7},{10,... | collective-permute-start | bytes 1572872 | tf_op jit(solution)/shard_map/ppermute | solution.py:300
  7.2 1.1 %copy-done = bf16[4,128,512]{2,1,0:T(8,128)(2,1)S(1)} copy-done((bf16[4,128,512]{2,1,0:T(8,128)(2,1)S(1)}, bf16[4,128,512]{2,1,0:T(8,128)(2,1)}, u32[]{:S(2)}) %copy-start) | copy-done | bytes 524312
  8.2 0.9 %shard_map.109 = f32[8,128]{1,0:T(8,128)S(1)} custom-call(bf16[512,512]{1,0:T(8,128)(2,1)S(1)} %bitcast.13), custom_call_target="tpu_custom_call" | custom-call | flops 20000000000 | bytes 524288 | tf_op jit(solution)/shard_map/pallas_call | solution.py:25
  9.1 0.7 broadcast_in_dim.6
  9.8 4.0 %all-to-all-start = ((f32[16,8,128]{2,1,0:T(8,128)}), f32[16,8,128]{2,1,0:T(8,128)S(1)}, u32[]{:S(2)}, u32[]{:S(2)}) async-start(f32[16,8,128]{2,1,0:T(8,128)} %broadcast_in_dim.6), calls=%async_computation | async-start | bytes 131072 | tf_op jit(solution)/shard_map/all_to_all | solution.py:282
  13.8 2.6 %collective-permute-start.1 = (bf16[512,512]{1,0:T(8,128)(2,1)}, bf16[512,512]{1,0:T(8,128)(2,1)S(1)}, u32[]{:S(2)}, u32[]{:S(2)}) collective-permute-start(bf16[512,512]{1,0:T(8,128)(2,1)} %collective-permute-done), channel_id=1, source_target_pairs={{0,2},{1,15},{2,4},{3,1},{4,6},{5,3},{6,8},{7,5},{8,10},{9,7},{10,... | collective-permute-start | bytes 1572872 | tf_op jit(solution)/shard_map/ppermute | solution.py:300
  16.5 1.2 %collective-permute-start.3 = (bf16[512,512]{1,0:T(8,128)(2,1)S(1)}, bf16[512,512]{1,0:T(8,128)(2,1)S(1)}, u32[]{:S(2)}, u32[]{:S(2)}) collective-permute-start(bf16[512,512]{1,0:T(8,128)(2,1)S(1)} %collective-permute-done.2.refs_2_), channel_id=1, source_target_pairs={{0,2},{1,15},{2,4},{3,1},{4,6},{5,3},{6,8},{7,5},{8,10},{9,7},{10,... | collective-permute-start | bytes 1572872 | tf_op jit(solution)/shard_map/ppermute | solution.py:300
  17.7 1.0 %copy-done.5 = bf16[512,512]{1,0:T(8,128)(2,1)S(1)} copy-done((bf16[512,512]{1,0:T(8,128)(2,1)S(1)}, bf16[512,512]{1,0:T(8,128)(2,1)}, u32[]{:S(2)}) %copy-start.5) | copy-done | bytes 524312
  19.2 2.4 %all-to-all-done.stats_ref = f32[16,8,128]{2,1,0:T(8,128)S(1)} async-done(((f32[16,8,128]{2,1,0:T(8,128)}), f32[16,8,128]{2,1,0:T(8,128)S(1)}, u32[]{:S(2)}, u32[]{:S(2)}) %all-to-all-start) | async-done | bytes 65568 | tf_op jit(solution)/shard_map/all_to_all | solution.py:282
  21.6 2.0 %collective-permute-done.1.far_ref.refs_2_ = bf16[512,512]{1,0:T(8,128)(2,1)S(1)} collective-permute-done((bf16[512,512]{1,0:T(8,128)(2,1)}, bf16[512,512]{1,0:T(8,128)(2,1)S(1)}, u32[]{:S(2)}, u32[]{:S(2)}) %collective-permute-start.1) | collective-permute-done | bytes 524320 | tf_op jit(solution)/shard_map/ppermute | solution.py:300
  23.6 1.1 %shard_map.111 = (bf16[640,512]{1,0:T(8,128)(2,1)S(1)}, f32[8,512]{1,0:T(8,128)S(1)}, bf16[128,512]{1,0:T(8,128)(2,1)S(1)}) custom-call(s32[3]{0:T(128)S(1)} %add_convert_fusion.flags_ref, bf16[512,512]{1,0:T(8,128)(2,1)S(1)} %bitcast.14, bf16[512,512]{1,0:T(8,128)(2,1)S(1)} %collective-permute-done.1.far_ref.refs_2_, ...), custom_call_target="tpu_custom_call" | custom-call | flops 268435456 | bytes 1642508 | tf_op jit(solution)/shard_map/pallas_call | solution.py:25
  24.7 2.0 %collective-permute-start.7 = (bf16[640,512]{1,0:T(8,128)(2,1)S(1)}, bf16[640,512]{1,0:T(8,128)(2,1)S(1)}, u32[]{:S(2)}, u32[]{:S(2)}) collective-permute-start(bf16[640,512]{1,0:T(8,128)(2,1)S(1)} %get-tuple-element.59.refs_0_.q_ref), channel_id=1, source_target_pairs={{0,1},{1,0},{2,3},{3,2},{4,5},{5,4},{6,7},{7,6},{8,9},{9,8},{10,11... | collective-permute-start | bytes 1966088 | tf_op jit(solution)/shard_map/ppermute | solution.py:300
  26.7 1.3 %collective-permute-start.8 = (bf16[512,512]{1,0:T(8,128)(2,1)S(1)}, bf16[512,512]{1,0:T(8,128)(2,1)S(1)}, u32[]{:S(2)}, u32[]{:S(2)}) collective-permute-start(bf16[512,512]{1,0:T(8,128)(2,1)S(1)} %collective-permute-done.1.far_ref.refs_2_), channel_id=1, source_target_pairs={{0,2},{1,15},{2,4},{3,1},{4,6},{5,3},{6,8},{7,5},{8,10},{9,7},{10,... | collective-permute-start | bytes 1572872 | tf_op jit(solution)/shard_map/ppermute | solution.py:300
  28.0 1.2 %collective-permute-done.3.refs_2_ = bf16[512,512]{1,0:T(8,128)(2,1)S(1)} collective-permute-done((bf16[512,512]{1,0:T(8,128)(2,1)S(1)}, bf16[512,512]{1,0:T(8,128)(2,1)S(1)}, u32[]{:S(2)}, u32[]{:S(2)}) %collective-permute-start.3) | collective-permute-done | bytes 524320 | tf_op jit(solution)/shard_map/ppermute | solution.py:300
  29.2 2.5 %collective-permute-start.4 = (bf16[512,512]{1,0:T(8,128)(2,1)S(1)}, bf16[512,512]{1,0:T(8,128)(2,1)S(1)}, u32[]{:S(2)}, u32[]{:S(2)}) collective-permute-start(bf16[512,512]{1,0:T(8,128)(2,1)S(1)} %collective-permute-done.3.refs_2_), channel_id=1, source_target_pairs={{0,2},{1,15},{2,4},{3,1},{4,6},{5,3},{6,8},{7,5},{8,10},{9,7},{10,... | collective-permute-start | bytes 1572872 | tf_op jit(solution)/shard_map/ppermute | solution.py:300
  31.8 3.3 %collective-permute-done.8.refs_2_ = bf16[512,512]{1,0:T(8,128)(2,1)S(1)} collective-permute-done((bf16[512,512]{1,0:T(8,128)(2,1)S(1)}, bf16[512,512]{1,0:T(8,128)(2,1)S(1)}, u32[]{:S(2)}, u32[]{:S(2)}) %collective-permute-start.8) | collective-permute-done | bytes 524320 | tf_op jit(solution)/shard_map/ppermute | solution.py:300
  35.1 2.3 %collective-permute-start.9 = (bf16[512,512]{1,0:T(8,128)(2,1)S(1)}, bf16[512,512]{1,0:T(8,128)(2,1)S(1)}, u32[]{:S(2)}, u32[]{:S(2)}) collective-permute-start(bf16[512,512]{1,0:T(8,128)(2,1)S(1)} %collective-permute-done.8.refs_2_), channel_id=1, source_target_pairs={{0,2},{1,15},{2,4},{3,1},{4,6},{5,3},{6,8},{7,5},{8,10},{9,7},{10,... | collective-permute-start | bytes 1572872 | tf_op jit(solution)/shard_map/ppermute | solution.py:300
  37.4 3.3 %collective-permute-done.4.refs_2_ = bf16[512,512]{1,0:T(8,128)(2,1)S(1)} collective-permute-done((bf16[512,512]{1,0:T(8,128)(2,1)S(1)}, bf16[512,512]{1,0:T(8,128)(2,1)S(1)}, u32[]{:S(2)}, u32[]{:S(2)}) %collective-permute-start.4) | collective-permute-done | bytes 524320 | tf_op jit(solution)/shard_map/ppermute | solution.py:300
  40.7 2.3 %collective-permute-start.5 = (bf16[512,512]{1,0:T(8,128)(2,1)S(1)}, bf16[512,512]{1,0:T(8,128)(2,1)S(1)}, u32[]{:S(2)}, u32[]{:S(2)}) collective-permute-start(bf16[512,512]{1,0:T(8,128)(2,1)S(1)} %collective-permute-done.4.refs_2_), channel_id=1, source_target_pairs={{0,2},{1,15},{2,4},{3,1},{4,6},{5,3},{6,8},{7,5},{8,10},{9,7},{10,... | collective-permute-start | bytes 1572872 | tf_op jit(solution)/shard_map/ppermute | solution.py:300
  43.0 1.5 %shard_map.112 = (f32[640,512]{1,0:T(8,128)S(1)}, f32[640,128]{1,0:T(8,128)S(1)}, f32[640,128]{1,0:T(8,128)S(1)}, f32[640,512]{1,0:T(8,128)S(1)}, f32[640,128]{1,0:T(8,128)S(1)}, /*index=5*/f32[640,128]{1,0:T(8,128)S(1)}) custom-call(bf16[640,512]{1,0:T(8,128)(2,1)S(1)} %get-tuple-element.59.refs_0_.q_ref, ...), custom_call_target="tpu_custom_call" | custom-call | flops 1342177280 | bytes 1835008 | tf_op jit(solution)/shard_map/pallas_call | solution.py:25
  44.6 2.1 %shard_map.113 = (f32[640,512]{1,0:T(8,128)S(1)}, f32[640,128]{1,0:T(8,128)S(1)}, f32[640,128]{1,0:T(8,128)S(1)}, f32[640,512]{1,0:T(8,128)S(1)}, f32[640,128]{1,0:T(8,128)S(1)}, /*index=5*/f32[640,128]{1,0:T(8,128)S(1)}) custom-call(bf16[640,512]{1,0:T(8,128)(2,1)S(1)} %get-tuple-element., ...), custom_call_target="tpu_custom_call", output_to_operand_aliasing={{0}: (3, {}), {1}: (4, {}), {2}: (5, {}), {3}: (6, {}), {4}... | custom-call | flops 1342177280 | bytes 5767168 | tf_op jit(solution)/shard_map/pallas_call | solution.py:25
  46.6 2.1 %shard_map.114 = (f32[640,512]{1,0:T(8,128)S(1)}, f32[640,128]{1,0:T(8,128)S(1)}, f32[640,128]{1,0:T(8,128)S(1)}, f32[640,512]{1,0:T(8,128)S(1)}, f32[640,128]{1,0:T(8,128)S(1)}, /*index=5*/f32[640,128]{1,0:T(8,128)S(1)}) custom-call(bf16[640,512]{1,0:T(8,128)(2,1)S(1)} %get-tuple-element., ...), custom_call_target="tpu_custom_call", output_to_operand_aliasing={{0}: (3, {}), {1}: (4, {}), {2}: (5, {}), {3}: (6, {}), {4}... | custom-call | flops 1342177280 | bytes 5767168 | tf_op jit(solution)/shard_map/pallas_call | solution.py:25
  48.7 2.1 %shard_map.115 = (f32[640,512]{1,0:T(8,128)S(1)}, f32[640,128]{1,0:T(8,128)S(1)}, f32[640,128]{1,0:T(8,128)S(1)}, f32[640,512]{1,0:T(8,128)S(1)}, f32[640,128]{1,0:T(8,128)S(1)}, /*index=5*/f32[640,128]{1,0:T(8,128)S(1)}) custom-call(bf16[640,512]{1,0:T(8,128)(2,1)S(1)} %get-tuple-element., ...), custom_call_target="tpu_custom_call", output_to_operand_aliasing={{0}: (3, {}), {1}: (4, {}), {2}: (5, {}), {3}: (6, {}), {4}... | custom-call | flops 1342177280 | bytes 5767168 | tf_op jit(solution)/shard_map/pallas_call | solution.py:25
  50.8 2.1 %shard_map.116 = (f32[640,512]{1,0:T(8,128)S(1)}, f32[640,128]{1,0:T(8,128)S(1)}, f32[640,128]{1,0:T(8,128)S(1)}, f32[640,512]{1,0:T(8,128)S(1)}, f32[640,128]{1,0:T(8,128)S(1)}, /*index=5*/f32[640,128]{1,0:T(8,128)S(1)}) custom-call(bf16[640,512]{1,0:T(8,128)(2,1)S(1)} %get-tuple-element., ...), custom_call_target="tpu_custom_call", output_to_operand_aliasing={{0}: (3, {}), {1}: (4, {}), {2}: (5, {}), {3}: (6, {}), {4}... | custom-call | flops 1342177280 | bytes 5767168 | tf_op jit(solution)/shard_map/pallas_call | solution.py:25
  52.9 2.1 %shard_map.117 = (f32[640,512]{1,0:T(8,128)S(1)}, f32[640,128]{1,0:T(8,128)S(1)}, f32[640,128]{1,0:T(8,128)S(1)}, f32[640,512]{1,0:T(8,128)S(1)}, f32[640,128]{1,0:T(8,128)S(1)}, /*index=5*/f32[640,128]{1,0:T(8,128)S(1)}) custom-call(bf16[640,512]{1,0:T(8,128)(2,1)S(1)} %get-tuple-element., ...), custom_call_target="tpu_custom_call", output_to_operand_aliasing={{0}: (3, {}), {1}: (4, {}), {2}: (5, {}), {3}: (6, {}), {4}... | custom-call | flops 1342177280 | bytes 5767168 | tf_op jit(solution)/shard_map/pallas_call | solution.py:25
  55.0 1.9 %shard_map.118 = (f32[640,512]{1,0:T(8,128)S(1)}, f32[640,128]{1,0:T(8,128)S(1)}, f32[640,128]{1,0:T(8,128)S(1)}, f32[640,640]{1,0:T(8,128)S(1)}) custom-call(bf16[640,512]{1,0:T(8,128)(2,1)S(1)} %get-tuple-element.59.refs_0_.q_ref, bf16[640,512]{1,0:T(8,128)(2,1)S(1)} %collective-permute-done.7.refs_1_, ...), custom_call_target="tpu_custom_call", output_to_operand_aliasing={{0}: (3, {}), {1}: (4, {}), {2}: (5, {})} | custom-call | flops 1342177280 | bytes 5767168 | tf_op jit(solution)/shard_map/pallas_call | solution.py:25
  58.2 1.1 %shard_map.119 = (f32[640,512]{1,0:T(8,128)S(1)}, f32[640,128]{1,0:T(8,128)S(1)}, f32[640,128]{1,0:T(8,128)S(1)}) custom-call(bf16[640,512]{1,0:T(8,128)(2,1)S(1)} %get-tuple-element.59.refs_0_.q_ref, bf16[512,512]{1,0:T(8,128)(2,1)S(1)} %collective-permute-done.5.refs_1_, ...), custom_call_target="tpu_custom_call", output_to_operand_aliasing={{0}: (2, {}), {1}: (3, {}), {2}: (4, {})} | custom-call | flops 671088640 | bytes 3145728 | tf_op jit(solution)/shard_map/pallas_call | solution.py:25
  59.4 2.1 %collective-permute-done.6.key_ref = bf16[512,512]{1,0:T(8,128)(2,1)S(1)} collective-permute-done((bf16[512,512]{1,0:T(8,128)(2,1)S(1)}, bf16[512,512]{1,0:T(8,128)(2,1)S(1)}, u32[]{:S(2)}, u32[]{:S(2)}) %collective-permute-start.6) | collective-permute-done | bytes 524320 | tf_op jit(solution)/shard_map/ppermute | solution.py:300
  61.5 3.1 %shard_map.121 = (bf16[512,512]{1,0:T(8,128)(2,1)S(1)}, f32[8,128]{1,0:T(8,128)S(1)}, bf16[128,512]{1,0:T(8,128)(2,1)S(1)}, bf16[128,512]{1,0:T(8,128)(2,1)S(1)}) custom-call(s32[3]{0:T(128)S(1)} %add_convert_fusion.flags_ref, bf16[640,512]{1,0:T(8,128)(2,1)S(1)} %get-tuple-element.59.refs_0_.q_ref, bf16[512,512]{1,0:T(8,128)(2,1)S(1)} %collective-permute-done.6.key_ref, ...), custom_call_target="tpu_custom_call" | custom-call | flops 805306368 | bytes 5980172 | tf_op jit(solution)/shard_map/pallas_call | solution.py:25
  64.8 14.2 %all_to_all.10.stats_ref = f32[16,8,128]{2,1,0:T(8,128)S(1)} all-to-all(f32[16,8,128]{2,1,0:T(8,128)S(1)} %broadcast_in_dim.7), channel_id=1, replica_groups=mesh['img'=16,'row'=16] {'row'}, dimensions={0} | all-to-all | bytes 131072 | tf_op jit(solution)/shard_map/all_to_all | solution.py:282
  78.9 4.0 %shard_map.122 = bf16[512,512]{1,0:T(8,128)(2,1)} custom-call(s32[3]{0:T(128)S(1)} %add_convert_fusion.flags_ref, bf16[512,512]{1,0:T(8,128)(2,1)S(1)} %get-tuple-element.105.h_ref, bf16[128,512]{1,0:T(8,128)(2,1)S(1)} %collective-permute-done.11.inside_ref, bf16[128,512]{1,0:T(8,128)(2,1)S(1)} %get-tuple-element.107.outside_ref, ...), custom_call_target="tpu_custom_call" | custom-call | flops 2415919104 | bytes 5576716 | tf_op jit(solution)/shard_map/pallas_call | solution.py:25
  (39 shorter events, 2.1 us)
Async XLA Ops:
  0.1 13.7 %collective-permute-start = (bf16[512,512]{1,0:T(8,128)(2,1)}, bf16[512,512]{1,0:T(8,128)(2,1)}, u32[]{:S(2)}, u32[]{:S(2)}) collective-permute-start(bf16[512,512]{1,0:T(8,128)(2,1)} %bitcast.11), channel_id=1, source_target_pairs={{0,1},{1,0},{2,3},{3,2},{4,5},{5,4},{6,7},{7,6},{8,9},{9,8},{10,11... | collective-permute-start | bytes 1572872 | tf_op jit(solution)/shard_map/ppermute | solution.py:300
  3.3 13.2 %collective-permute-start.2 = (bf16[512,512]{1,0:T(8,128)(2,1)}, bf16[512,512]{1,0:T(8,128)(2,1)S(1)}, u32[]{:S(2)}, u32[]{:S(2)}) collective-permute-start(bf16[512,512]{1,0:T(8,128)(2,1)} %bitcast.12), channel_id=1, source_target_pairs={{0,2},{1,15},{2,4},{3,1},{4,6},{5,3},{6,8},{7,5},{8,10},{9,7},{10,... | collective-permute-start | bytes 1572872 | tf_op jit(solution)/shard_map/ppermute | solution.py:300
  7.2 1.1 %copy-start = (bf16[4,128,512]{2,1,0:T(8,128)(2,1)S(1)}, bf16[4,128,512]{2,1,0:T(8,128)(2,1)}, u32[]{:S(2)}) copy-start(bf16[4,128,512]{2,1,0:T(8,128)(2,1)} %param.11) | copy-start | bytes 1572868
  8.2 9.4 %copy-start.4 = (bf16[512,512]{1,0:T(8,128)(2,1)S(1)}, bf16[512,512]{1,0:T(8,128)(2,1)}, u32[]{:S(2)}) copy-start(bf16[512,512]{1,0:T(8,128)(2,1)} %refs_0_.2) | copy-start | bytes 1572868
  9.8 11.8 %all-to-all-start = ((f32[16,8,128]{2,1,0:T(8,128)}), f32[16,8,128]{2,1,0:T(8,128)S(1)}, u32[]{:S(2)}, u32[]{:S(2)}) async-start(f32[16,8,128]{2,1,0:T(8,128)} %broadcast_in_dim.6), calls=%async_computation | async-start | bytes 131072 | tf_op jit(solution)/shard_map/all_to_all | solution.py:282
  13.8 9.8 %copy-start.1 = (bf16[4,128,512]{2,1,0:T(8,128)(2,1)S(1)}, bf16[4,128,512]{2,1,0:T(8,128)(2,1)}, u32[]{:S(2)}) copy-start(bf16[4,128,512]{2,1,0:T(8,128)(2,1)} %param.11) | copy-start | bytes 1572868
  13.8 9.8 %copy-start.2 = (f32[512]{0:T(512)S(1)}, f32[512]{0:T(512)}, u32[]{:S(2)}) copy-start(f32[512]{0:T(512)} %param.12) | copy-start | bytes 6148
  13.8 9.8 %copy-start.3 = (f32[512]{0:T(512)S(1)}, f32[512]{0:T(512)}, u32[]{:S(2)}) copy-start(f32[512]{0:T(512)} %param.13) | copy-start | bytes 6148
  13.8 9.8 %collective-permute-start.1 = (bf16[512,512]{1,0:T(8,128)(2,1)}, bf16[512,512]{1,0:T(8,128)(2,1)S(1)}, u32[]{:S(2)}, u32[]{:S(2)}) collective-permute-start(bf16[512,512]{1,0:T(8,128)(2,1)} %collective-permute-done), channel_id=1, source_target_pairs={{0,2},{1,15},{2,4},{3,1},{4,6},{5,3},{6,8},{7,5},{8,10},{9,7},{10,... | collective-permute-start | bytes 1572872 | tf_op jit(solution)/shard_map/ppermute | solution.py:300
  16.5 12.7 %collective-permute-start.3 = (bf16[512,512]{1,0:T(8,128)(2,1)S(1)}, bf16[512,512]{1,0:T(8,128)(2,1)S(1)}, u32[]{:S(2)}, u32[]{:S(2)}) collective-permute-start(bf16[512,512]{1,0:T(8,128)(2,1)S(1)} %collective-permute-done.2.refs_2_), channel_id=1, source_target_pairs={{0,2},{1,15},{2,4},{3,1},{4,6},{5,3},{6,8},{7,5},{8,10},{9,7},{10,... | collective-permute-start | bytes 1572872 | tf_op jit(solution)/shard_map/ppermute | solution.py:300
  17.7 1.0 %copy-start.5 = (bf16[512,512]{1,0:T(8,128)(2,1)S(1)}, bf16[512,512]{1,0:T(8,128)(2,1)}, u32[]{:S(2)}) copy-start(bf16[512,512]{1,0:T(8,128)(2,1)} %refs_1_.2) | copy-start | bytes 1572868
  24.7 18.3 %collective-permute-start.7 = (bf16[640,512]{1,0:T(8,128)(2,1)S(1)}, bf16[640,512]{1,0:T(8,128)(2,1)S(1)}, u32[]{:S(2)}, u32[]{:S(2)}) collective-permute-start(bf16[640,512]{1,0:T(8,128)(2,1)S(1)} %get-tuple-element.59.refs_0_.q_ref), channel_id=1, source_target_pairs={{0,1},{1,0},{2,3},{3,2},{4,5},{5,4},{6,7},{7,6},{8,9},{9,8},{10,11... | collective-permute-start | bytes 1966088 | tf_op jit(solution)/shard_map/ppermute | solution.py:300
  26.7 8.3 %collective-permute-start.8 = (bf16[512,512]{1,0:T(8,128)(2,1)S(1)}, bf16[512,512]{1,0:T(8,128)(2,1)S(1)}, u32[]{:S(2)}, u32[]{:S(2)}) collective-permute-start(bf16[512,512]{1,0:T(8,128)(2,1)S(1)} %collective-permute-done.1.far_ref.refs_2_), channel_id=1, source_target_pairs={{0,2},{1,15},{2,4},{3,1},{4,6},{5,3},{6,8},{7,5},{8,10},{9,7},{10,... | collective-permute-start | bytes 1572872 | tf_op jit(solution)/shard_map/ppermute | solution.py:300
  29.2 11.4 %collective-permute-start.4 = (bf16[512,512]{1,0:T(8,128)(2,1)S(1)}, bf16[512,512]{1,0:T(8,128)(2,1)S(1)}, u32[]{:S(2)}, u32[]{:S(2)}) collective-permute-start(bf16[512,512]{1,0:T(8,128)(2,1)S(1)} %collective-permute-done.3.refs_2_), channel_id=1, source_target_pairs={{0,2},{1,15},{2,4},{3,1},{4,6},{5,3},{6,8},{7,5},{8,10},{9,7},{10,... | collective-permute-start | bytes 1572872 | tf_op jit(solution)/shard_map/ppermute | solution.py:300
  35.1 19.9 %collective-permute-start.9 = (bf16[512,512]{1,0:T(8,128)(2,1)S(1)}, bf16[512,512]{1,0:T(8,128)(2,1)S(1)}, u32[]{:S(2)}, u32[]{:S(2)}) collective-permute-start(bf16[512,512]{1,0:T(8,128)(2,1)S(1)} %collective-permute-done.8.refs_2_), channel_id=1, source_target_pairs={{0,2},{1,15},{2,4},{3,1},{4,6},{5,3},{6,8},{7,5},{8,10},{9,7},{10,... | collective-permute-start | bytes 1572872 | tf_op jit(solution)/shard_map/ppermute | solution.py:300
  40.7 16.6 %collective-permute-start.5 = (bf16[512,512]{1,0:T(8,128)(2,1)S(1)}, bf16[512,512]{1,0:T(8,128)(2,1)S(1)}, u32[]{:S(2)}, u32[]{:S(2)}) collective-permute-start(bf16[512,512]{1,0:T(8,128)(2,1)S(1)} %collective-permute-done.4.refs_2_), channel_id=1, source_target_pairs={{0,2},{1,15},{2,4},{3,1},{4,6},{5,3},{6,8},{7,5},{8,10},{9,7},{10,... | collective-permute-start | bytes 1572872 | tf_op jit(solution)/shard_map/ppermute | solution.py:300
  50.8 7.0 %slice-start = ((s8[4718592]{0:T(1024)(128)(4,1)}), s8[4194304]{0:T(1024)(128)(4,1)S(1)}, s32[]{:S(2)}) async-start(s8[4718592]{0:T(1024)(128)(4,1)} %bitcast.19), calls=%async_computation.2 | async-start | bytes 8388608
  52.9 4.9 %slice-start.1 = ((s8[4718592]{0:T(1024)(128)(4,1)}), s8[524288]{0:T(1024)(128)(4,1)S(1)}, s32[]{:S(2)}) async-start(s8[4718592]{0:T(1024)(128)(4,1)} %bitcast.19), calls=%async_computation.3 | async-start | bytes 1048576
  55.0 2.8 %copy-start.6 = (bf16[512,512]{1,0:T(8,128)(2,1)S(1)}, bf16[512,512]{1,0:T(8,128)(2,1)}, u32[]{:S(2)}) copy-start(bf16[512,512]{1,0:T(8,128)(2,1)} %refs_0_.3) | copy-start | bytes 1572868
  55.0 2.8 %copy-start.7 = (bf16[512,512]{1,0:T(8,128)(2,1)S(1)}, bf16[512,512]{1,0:T(8,128)(2,1)}, u32[]{:S(2)}) copy-start(bf16[512,512]{1,0:T(8,128)(2,1)} %refs_1_.3) | copy-start | bytes 1572868
  56.9 4.6 %collective-permute-start.10 = (f32[640,640]{1,0:T(8,128)S(1)}, f32[640,640]{1,0:T(8,128)S(1)}, u32[]{:S(2)}, u32[]{:S(2)}) collective-permute-start(f32[640,640]{1,0:T(8,128)S(1)} %get-tuple-element.102), channel_id=1, source_target_pairs={{0,1},{1,0},{2,3},{3,2},{4,5},{5,4},{6,7},{7,6},{8,9},{9,8},{10,11... | collective-permute-start | bytes 4915208 | tf_op jit(solution)/shard_map/ppermute | solution.py:300
  57.3 4.2 %collective-permute-start.6 = (bf16[512,512]{1,0:T(8,128)(2,1)S(1)}, bf16[512,512]{1,0:T(8,128)(2,1)S(1)}, u32[]{:S(2)}, u32[]{:S(2)}) collective-permute-start(bf16[512,512]{1,0:T(8,128)(2,1)S(1)} %collective-permute-done.5.refs_1_), channel_id=1, source_target_pairs={{0,1},{1,0},{2,3},{3,2},{4,5},{5,4},{6,7},{7,6},{8,9},{9,8},{10,11... | collective-permute-start | bytes 1572872 | tf_op jit(solution)/shard_map/ppermute | solution.py:300
  61.5 17.4 %copy-start.8 = (f32[512]{0:T(512)S(1)}, f32[512]{0:T(512)}, u32[]{:S(2)}) copy-start(f32[512]{0:T(512)} %param.18) | copy-start | bytes 6148
  61.5 17.4 %copy-start.9 = (f32[512]{0:T(512)S(1)}, f32[512]{0:T(512)}, u32[]{:S(2)}) copy-start(f32[512]{0:T(512)} %param.19) | copy-start | bytes 6148
  61.5 17.4 %copy-start.10 = (f32[512]{0:T(512)S(1)}, f32[512]{0:T(512)}, u32[]{:S(2)}) copy-start(f32[512]{0:T(512)} %param.21) | copy-start | bytes 6148
  64.6 14.3 %collective-permute-start.11 = (bf16[128,512]{1,0:T(8,128)(2,1)S(1)}, bf16[128,512]{1,0:T(8,128)(2,1)S(1)}, u32[]{:S(2)}, u32[]{:S(2)}) collective-permute-start(bf16[128,512]{1,0:T(8,128)(2,1)S(1)} %get-tuple-element.106), channel_id=1, source_target_pairs={{0,1},{1,0},{2,3},{3,2},{4,5},{5,4},{6,7},{7,6},{8,9},{9,8},{10,11... | collective-permute-start | bytes 393224 | tf_op jit(solution)/shard_map/ppermute | solution.py:300

commit v4 on v3

--- a/solution.py
+++ b/solution.py
@@ -13,7 +13,6 @@
 EPS = 1e-06
 LOG2E = 1.4426950408889634
 VMEM = pl.BlockSpec(memory_space=pltpu.VMEM)
-SMEM = pl.BlockSpec(memory_space=pltpu.SMEM)
 F32 = jnp.float32
 BF16 = jnp.bfloat16
 MIB = 1024 * 1024
@@ -43,18 +42,27 @@
     return v
 
 
-def write_stats(field, out_ref):
-    rows = field.shape[0]
-    share = C // GROUPS
-    mean = group_sum(jnp.broadcast_to(jnp.sum(field, 0, keepdims=True), (8, C))) * (
-        1.0 / (rows * share)
-    )
-    offset = field - mean[0:1]
-    spread = group_sum(jnp.broadcast_to(jnp.sum(offset * offset, 0, keepdims=True), (8, C)))
+def store_stats(mean, spread, out_ref):
     for i in range(C // LANES):
         cut = slice(i * LANES, (i + 1) * LANES)
         out_ref[i : i + 1, :] = mean[0:1, cut]
         out_ref[i + 4 : i + 5, :] = spread[0:1, cut]
+
+
+def field_stats(parts, out_ref):
+    share = C // GROUPS
+    first = jnp.sum(parts[0], 0, keepdims=True) * (1.0 / (parts[0].shape[0] * share))
+    pivot = group_sum(jnp.broadcast_to(first, (8, C)))[0:1]
+    one = two = None
+    for part in parts:
+        offset = part - pivot
+        sums = jnp.sum(offset, 0, keepdims=True), jnp.sum(offset * offset, 0, keepdims=True)
+        one, two = sums if one is None else (one + sums[0], two + sums[1])
+    row = lax.broadcasted_iota(jnp.int32, (8, C), 0)
+    total = group_sum(jnp.where(row == 0, one, two))
+    drift = total[0:1] * (1.0 / (sum(p.shape[0] for p in parts) * share))
+    spread = jnp.maximum(total[1:2] - total[0:1] * drift, 0.0)
+    store_stats(pivot + drift, spread, out_ref)
 
 
 def affine(stats, gain, shift, rows):
@@ -70,8 +78,15 @@
     return scale, shift - flat(mean) * scale
 
 
+def pick(flags_ref, row, yes, no):
+    flag = flags_ref[row : row + 1, :]
+    wanted = jnp.broadcast_to(jnp.concatenate([flag] * (C // LANES), axis=1), yes.shape) > 0.0
+    return jnp.where(wanted, yes, no)
+
+
 def stats_kernel(x_ref, out_ref):
-    write_stats(x_ref[...].astype(F32), out_ref)
+    half = x_ref.shape[0] // 2
+    field_stats([x_ref[:half, :].astype(F32), x_ref[half:, :].astype(F32)], out_ref)
 
 
 def fold_kernel(transposed, left_ref, right_ref, *refs):
@@ -96,7 +111,7 @@
     scale, shift = affine(stats_ref[...], gain_ref[...], shift_ref[...], rows)
     coef_ref[0:1, :] = scale
     coef_ref[1:2, :] = shift
-    halo = jnp.where(flags_ref[2] > 0, far_ref[rows - W : rows, :], far_ref[0:W, :])
+    halo = pick(flags_ref, 2, far_ref[rows - W : rows, :], far_ref[0:W, :])
     halo_ref[...] = halo
     for x, at in ((x_ref[...], slice(0, rows)), (halo, slice(rows, rows + W))):
         normed = (x.astype(F32) * scale + shift).astype(BF16)
@@ -207,6 +222,7 @@
     rows = x_ref.shape[0]
     half = rows // 2
     blocks = [slice(0, half), slice(half, rows), slice(rows, rows + W)]
+    parts = []
     ahead = scores_of(q_ref[blocks[0], :], keys)
     for n, at in enumerate(blocks):
         now = ahead
@@ -228,10 +244,12 @@
             outside_ref[...] = hidden.astype(BF16)
         else:
             hidden_ref[at, :] = hidden.astype(BF16)
-    inside_ref[...] = jnp.where(
-        flags_ref[2] > 0, hidden_ref[rows - W : rows, :], hidden_ref[0:W, :]
+            parts.append(hidden.astype(BF16).astype(F32))
+        if n == 1:
+            field_stats(parts, stats_ref)
+    inside_ref[...] = pick(
+        flags_ref, 2, hidden_ref[rows - W : rows, :], hidden_ref[0:W, :]
     )
-    write_stats(hidden_ref[...].astype(F32), stats_ref)
 
 
 def conv_kernel(
@@ -240,12 +258,13 @@
 ):
     rows = h_ref.shape[0]
     scale, shift = affine(stats_ref[...], gain_ref[...], shift_ref[...], rows)
+    scale, shift = 0.5 * scale, 0.5 * shift
 
     def activate(f, at, keep):
         v = f.astype(F32) * scale + shift
-        v = v / (1.0 + jnp.exp(-v))
+        v = v + v * jnp.tanh(v)
         if keep is not None:
-            v = jnp.where(keep, v, 0.0)
+            v = pick(flags_ref, keep, v, jnp.zeros_like(v))
         column = lax.broadcasted_iota(jnp.int32, v.shape, 0) % W
         mid_ref[at : at + W, :] = v.astype(BF16)
         before = jnp.where(column == 0, 0.0, pltpu.roll(v, 1, 0))
@@ -253,12 +272,11 @@
         after = jnp.where(column == W - 1, 0.0, pltpu.roll(v, W - 1, 0))
         right_ref[at : at + W, :] = after.astype(BF16)
 
-    even = flags_ref[2] > 0
-    activate(jnp.where(even, outside_ref[...], inside_ref[...]), 0, flags_ref[0] > 0)
+    inside, outside = inside_ref[...].astype(F32), outside_ref[...].astype(F32)
+    activate(pick(flags_ref, 2, outside, inside), 0, 0)
     for r in range(rows // W):
         activate(h_ref[r * W : (r + 1) * W, :], (r + 1) * W, None)
-    bottom = jnp.where(even, inside_ref[...], outside_ref[...])
-    activate(bottom, rows + W, flags_ref[1] > 0)
+    activate(pick(flags_ref, 2, inside, outside), rows + W, 1)
     for r in range(0, rows, TILE):
         for n in range(0, C, TILE):
             total = None
@@ -290,7 +308,9 @@
     chips = count // 2
     rows = latent.shape[0] * W
     me = lax.axis_index("row")
-    flags = jnp.stack([me > 0, me < count - 1, me % 2 == 0]).astype(jnp.int32)
+    place = lax.broadcasted_iota(jnp.int32, (8, LANES), 0)
+    holds = [me > 0, me < count - 1, me % 2 == 0]
+    flags = sum(jnp.where((place == i) & h, 1.0, 0.0) for i, h in enumerate(holds))
     latent, flags = lax.optimization_barrier((latent, flags))
     x = latent.reshape(rows, C)
     line = lambda v: v.reshape(1, C)
@@ -320,7 +340,7 @@
             jax.ShapeDtypeStruct((8, C), F32),
             jax.ShapeDtypeStruct((W, C), BF16),
         ],
-        [SMEM] + [VMEM] * 6,
+        [VMEM] * 7,
         [flags, x, pieces[2], stats, line(attn_gain), line(attn_shift), wqk],
         2 * rows * C * C,
     )
@@ -337,7 +357,7 @@
     hidden, tile2, inside, outside = call(
         output_kernel,
         [jax.ShapeDtypeStruct((rows, C), BF16), tile, edge, edge],
-        [SMEM] + [VMEM] * 10,
+        [VMEM] * 11,
         [flags, query, across, *mine, met, x, halo, coef, wvo],
         6 * rows * C * C,
         20,
@@ -347,7 +367,7 @@
     encoded = call(
         conv_kernel,
         jax.ShapeDtypeStruct((rows, C), BF16),
-        [SMEM] + [VMEM] * 8,
+        [VMEM] * 9,
         [
             flags, hidden, inside, outside, stats2, line(conv_gain), line(conv_shift),
             taps, line(conv_bias),

time: 83.3 us -> 81.4 us (0.977)
  Pallas kernels: 24.9 us -> 23 us
    pallas_call x14, Pallas kernels: 24.9 us -> 23 us  [call(): pl.pallas_call(kernel, out_shape=outs, in_specs=specs, out_specs=jax.tree...]
where the time goes in v4:
time: 81.4 us; the launch traced here: 81.1 us
  starting transfers between devices  26.8 us (33%)
  Pallas kernels  23 us (28%)
  waiting for transfers between devices  14.5 us (18%)
  blocking collectives  13.7 us (17%)
  local copies, waits for them, and re-layouts  2.89 us (4%)
    pallas_call x14, Pallas kernels, call(): pl.pallas_call(kernel, out_shape=outs, in_specs=specs, out_specs=jax.tree...  23 us
    ppermute x12, starting transfers between devices, local(): move = lambda v, to: lax.ppermute(v, 'row', to)  22.8 us
    all_to_all x1, blocking collectives, everyone(): lax.all_to_all(copies, 'row', split_axis=0, concat_axis=0, tiled=True)  13.7 us
    ppermute x12, waiting for transfers between devices, local(): move = lambda v, to: lax.ppermute(v, 'row', to)  12.1 us
    all_to_all x1, starting transfers between devices, everyone(): lax.all_to_all(copies, 'row', split_axis=0, concat_axis=0, tiled=True)  4.01 us
    all_to_all x1, waiting for transfers between devices, everyone(): lax.all_to_all(copies, 'row', split_axis=0, concat_axis=0, tiled=True)  2.38 us
    unnamed x26, local copies, waits for them, and re-layouts  2.18 us
  transfers between devices with their start and end apart: 13, of which 6 were waited for; matrix products, arithmetic and copies ran while one was open for 1% of the time, Pallas kernels for 21%

profile of v4, /device:TPU:1, one launch (start us, length us, event | category | flops | bytes accessed | tf_op | source)
XLA Modules:
  0.0 81.1 jit_solution(16583833407463333052)
XLA Ops:
  0.1 3.2 %collective-permute-start = (bf16[512,512]{1,0:T(8,128)(2,1)}, bf16[512,512]{1,0:T(8,128)(2,1)}, u32[]{:S(2)}, u32[]{:S(2)}) collective-permute-start(bf16[512,512]{1,0:T(8,128)(2,1)} %bitcast.8), channel_id=1, source_target_pairs={{0,1},{1,0},{2,3},{3,2},{4,5},{5,4},{6,7},{7,6},{8,9},{9,8},{10,11... | collective-permute-start | bytes 1572872 | tf_op jit(solution)/shard_map/ppermute | solution.py:320
  3.3 3.9 %collective-permute-start.2 = (bf16[512,512]{1,0:T(8,128)(2,1)}, bf16[512,512]{1,0:T(8,128)(2,1)S(1)}, u32[]{:S(2)}, u32[]{:S(2)}) collective-permute-start(bf16[512,512]{1,0:T(8,128)(2,1)} %bitcast.9), channel_id=1, source_target_pairs={{0,2},{1,15},{2,4},{3,1},{4,6},{5,3},{6,8},{7,5},{8,10},{9,7},{10,... | collective-permute-start | bytes 1572872 | tf_op jit(solution)/shard_map/ppermute | solution.py:320
  7.2 1.1 %copy-done = bf16[4,128,512]{2,1,0:T(8,128)(2,1)S(1)} copy-done((bf16[4,128,512]{2,1,0:T(8,128)(2,1)S(1)}, bf16[4,128,512]{2,1,0:T(8,128)(2,1)}, u32[]{:S(2)}) %copy-start) | copy-done | bytes 524312
  8.3 0.9 %shard_map.109 = f32[8,128]{1,0:T(8,128)S(1)} custom-call(bf16[512,512]{1,0:T(8,128)(2,1)S(1)} %bitcast.10), custom_call_target="tpu_custom_call" | custom-call | flops 20000000000 | bytes 524288 | tf_op jit(solution)/shard_map/pallas_call | solution.py:24
  9.1 0.6 broadcast_in_dim.20
  9.8 4.0 %all-to-all-start = ((f32[16,8,128]{2,1,0:T(8,128)}), f32[16,8,128]{2,1,0:T(8,128)S(1)}, u32[]{:S(2)}, u32[]{:S(2)}) async-start(f32[16,8,128]{2,1,0:T(8,128)} %broadcast_in_dim.20), calls=%async_computation | async-start | bytes 131072 | tf_op jit(solution)/shard_map/all_to_all | solution.py:300
  13.8 2.6 %collective-permute-start.1 = (bf16[512,512]{1,0:T(8,128)(2,1)}, bf16[512,512]{1,0:T(8,128)(2,1)S(1)}, u32[]{:S(2)}, u32[]{:S(2)}) collective-permute-start(bf16[512,512]{1,0:T(8,128)(2,1)} %collective-permute-done), channel_id=1, source_target_pairs={{0,2},{1,15},{2,4},{3,1},{4,6},{5,3},{6,8},{7,5},{8,10},{9,7},{10,... | collective-permute-start | bytes 1572872 | tf_op jit(solution)/shard_map/ppermute | solution.py:320
  16.5 1.2 %collective-permute-start.3 = (bf16[512,512]{1,0:T(8,128)(2,1)S(1)}, bf16[512,512]{1,0:T(8,128)(2,1)S(1)}, u32[]{:S(2)}, u32[]{:S(2)}) collective-permute-start(bf16[512,512]{1,0:T(8,128)(2,1)S(1)} %collective-permute-done.2.refs_2_), channel_id=1, source_target_pairs={{0,2},{1,15},{2,4},{3,1},{4,6},{5,3},{6,8},{7,5},{8,10},{9,7},{10,... | collective-permute-start | bytes 1572872 | tf_op jit(solution)/shard_map/ppermute | solution.py:320
  17.7 1.0 %copy-done.5 = bf16[512,512]{1,0:T(8,128)(2,1)S(1)} copy-done((bf16[512,512]{1,0:T(8,128)(2,1)S(1)}, bf16[512,512]{1,0:T(8,128)(2,1)}, u32[]{:S(2)}) %copy-start.5) | copy-done | bytes 524312
  19.2 2.4 %all-to-all-done.stats_ref = f32[16,8,128]{2,1,0:T(8,128)S(1)} async-done(((f32[16,8,128]{2,1,0:T(8,128)}), f32[16,8,128]{2,1,0:T(8,128)S(1)}, u32[]{:S(2)}, u32[]{:S(2)}) %all-to-all-start) | async-done | bytes 65568 | tf_op jit(solution)/shard_map/all_to_all | solution.py:300
  21.6 2.0 %collective-permute-done.1.far_ref.refs_2_ = bf16[512,512]{1,0:T(8,128)(2,1)S(1)} collective-permute-done((bf16[512,512]{1,0:T(8,128)(2,1)}, bf16[512,512]{1,0:T(8,128)(2,1)S(1)}, u32[]{:S(2)}, u32[]{:S(2)}) %collective-permute-start.1) | collective-permute-done | bytes 524320 | tf_op jit(solution)/shard_map/ppermute | solution.py:320
  23.6 0.6 shard_map.111
  24.2 2.0 %collective-permute-start.7 = (bf16[640,512]{1,0:T(8,128)(2,1)S(1)}, bf16[640,512]{1,0:T(8,128)(2,1)S(1)}, u32[]{:S(2)}, u32[]{:S(2)}) collective-permute-start(bf16[640,512]{1,0:T(8,128)(2,1)S(1)} %get-tuple-element.59.refs_0_.q_ref), channel_id=1, source_target_pairs={{0,1},{1,0},{2,3},{3,2},{4,5},{5,4},{6,7},{7,6},{8,9},{9,8},{10,11... | collective-permute-start | bytes 1966088 | tf_op jit(solution)/shard_map/ppermute | solution.py:320
  26.2 1.2 %collective-permute-start.8 = (bf16[512,512]{1,0:T(8,128)(2,1)S(1)}, bf16[512,512]{1,0:T(8,128)(2,1)S(1)}, u32[]{:S(2)}, u32[]{:S(2)}) collective-permute-start(bf16[512,512]{1,0:T(8,128)(2,1)S(1)} %collective-permute-done.1.far_ref.refs_2_), channel_id=1, source_target_pairs={{0,2},{1,15},{2,4},{3,1},{4,6},{5,3},{6,8},{7,5},{8,10},{9,7},{10,... | collective-permute-start | bytes 1572872 | tf_op jit(solution)/shard_map/ppermute | solution.py:320
  27.4 1.8 %collective-permute-done.3.refs_2_ = bf16[512,512]{1,0:T(8,128)(2,1)S(1)} collective-permute-done((bf16[512,512]{1,0:T(8,128)(2,1)S(1)}, bf16[512,512]{1,0:T(8,128)(2,1)S(1)}, u32[]{:S(2)}, u32[]{:S(2)}) %collective-permute-start.3) | collective-permute-done | bytes 524320 | tf_op jit(solution)/shard_map/ppermute | solution.py:320
  29.2 2.5 %collective-permute-start.4 = (bf16[512,512]{1,0:T(8,128)(2,1)S(1)}, bf16[512,512]{1,0:T(8,128)(2,1)S(1)}, u32[]{:S(2)}, u32[]{:S(2)}) collective-permute-start(bf16[512,512]{1,0:T(8,128)(2,1)S(1)} %collective-permute-done.3.refs_2_), channel_id=1, source_target_pairs={{0,2},{1,15},{2,4},{3,1},{4,6},{5,3},{6,8},{7,5},{8,10},{9,7},{10,... | collective-permute-start | bytes 1572872 | tf_op jit(solution)/shard_map/ppermute | solution.py:320
  31.8 3.1 %collective-permute-done.8.refs_2_ = bf16[512,512]{1,0:T(8,128)(2,1)S(1)} collective-permute-done((bf16[512,512]{1,0:T(8,128)(2,1)S(1)}, bf16[512,512]{1,0:T(8,128)(2,1)S(1)}, u32[]{:S(2)}, u32[]{:S(2)}) %collective-permute-start.8) | collective-permute-done | bytes 524320 | tf_op jit(solution)/shard_map/ppermute | solution.py:320
  34.8 2.5 %collective-permute-start.9 = (bf16[512,512]{1,0:T(8,128)(2,1)S(1)}, bf16[512,512]{1,0:T(8,128)(2,1)S(1)}, u32[]{:S(2)}, u32[]{:S(2)}) collective-permute-start(bf16[512,512]{1,0:T(8,128)(2,1)S(1)} %collective-permute-done.8.refs_2_), channel_id=1, source_target_pairs={{0,2},{1,15},{2,4},{3,1},{4,6},{5,3},{6,8},{7,5},{8,10},{9,7},{10,... | collective-permute-start | bytes 1572872 | tf_op jit(solution)/shard_map/ppermute | solution.py:320
  37.4 3.1 %collective-permute-done.4.refs_2_ = bf16[512,512]{1,0:T(8,128)(2,1)S(1)} collective-permute-done((bf16[512,512]{1,0:T(8,128)(2,1)S(1)}, bf16[512,512]{1,0:T(8,128)(2,1)S(1)}, u32[]{:S(2)}, u32[]{:S(2)}) %collective-permute-start.4) | collective-permute-done | bytes 524320 | tf_op jit(solution)/shard_map/ppermute | solution.py:320
  40.5 2.5 %collective-permute-start.5 = (bf16[512,512]{1,0:T(8,128)(2,1)S(1)}, bf16[512,512]{1,0:T(8,128)(2,1)S(1)}, u32[]{:S(2)}, u32[]{:S(2)}) collective-permute-start(bf16[512,512]{1,0:T(8,128)(2,1)S(1)} %collective-permute-done.4.refs_2_), channel_id=1, source_target_pairs={{0,2},{1,15},{2,4},{3,1},{4,6},{5,3},{6,8},{7,5},{8,10},{9,7},{10,... | collective-permute-start | bytes 1572872 | tf_op jit(solution)/shard_map/ppermute | solution.py:320
  43.0 1.6 %shard_map.112 = (f32[640,512]{1,0:T(8,128)S(1)}, f32[640,128]{1,0:T(8,128)S(1)}, f32[640,128]{1,0:T(8,128)S(1)}, f32[640,512]{1,0:T(8,128)S(1)}, f32[640,128]{1,0:T(8,128)S(1)}, /*index=5*/f32[640,128]{1,0:T(8,128)S(1)}) custom-call(bf16[640,512]{1,0:T(8,128)(2,1)S(1)} %get-tuple-element.59.refs_0_.q_ref, ...), custom_call_target="tpu_custom_call" | custom-call | flops 1342177280 | bytes 1835008 | tf_op jit(solution)/shard_map/pallas_call | solution.py:24
  44.6 2.1 %shard_map.113 = (f32[640,512]{1,0:T(8,128)S(1)}, f32[640,128]{1,0:T(8,128)S(1)}, f32[640,128]{1,0:T(8,128)S(1)}, f32[640,512]{1,0:T(8,128)S(1)}, f32[640,128]{1,0:T(8,128)S(1)}, /*index=5*/f32[640,128]{1,0:T(8,128)S(1)}) custom-call(bf16[640,512]{1,0:T(8,128)(2,1)S(1)} %get-tuple-element., ...), custom_call_target="tpu_custom_call", output_to_operand_aliasing={{0}: (3, {}), {1}: (4, {}), {2}: (5, {}), {3}: (6, {}), {4}... | custom-call | flops 1342177280 | bytes 5767168 | tf_op jit(solution)/shard_map/pallas_call | solution.py:24
  46.6 2.1 %shard_map.114 = (f32[640,512]{1,0:T(8,128)S(1)}, f32[640,128]{1,0:T(8,128)S(1)}, f32[640,128]{1,0:T(8,128)S(1)}, f32[640,512]{1,0:T(8,128)S(1)}, f32[640,128]{1,0:T(8,128)S(1)}, /*index=5*/f32[640,128]{1,0:T(8,128)S(1)}) custom-call(bf16[640,512]{1,0:T(8,128)(2,1)S(1)} %get-tuple-element., ...), custom_call_target="tpu_custom_call", output_to_operand_aliasing={{0}: (3, {}), {1}: (4, {}), {2}: (5, {}), {3}: (6, {}), {4}... | custom-call | flops 1342177280 | bytes 5767168 | tf_op jit(solution)/shard_map/pallas_call | solution.py:24
  48.7 2.1 %shard_map.115 = (f32[640,512]{1,0:T(8,128)S(1)}, f32[640,128]{1,0:T(8,128)S(1)}, f32[640,128]{1,0:T(8,128)S(1)}, f32[640,512]{1,0:T(8,128)S(1)}, f32[640,128]{1,0:T(8,128)S(1)}, /*index=5*/f32[640,128]{1,0:T(8,128)S(1)}) custom-call(bf16[640,512]{1,0:T(8,128)(2,1)S(1)} %get-tuple-element., ...), custom_call_target="tpu_custom_call", output_to_operand_aliasing={{0}: (3, {}), {1}: (4, {}), {2}: (5, {}), {3}: (6, {}), {4}... | custom-call | flops 1342177280 | bytes 5767168 | tf_op jit(solution)/shard_map/pallas_call | solution.py:24
  50.8 2.1 %shard_map.116 = (f32[640,512]{1,0:T(8,128)S(1)}, f32[640,128]{1,0:T(8,128)S(1)}, f32[640,128]{1,0:T(8,128)S(1)}, f32[640,512]{1,0:T(8,128)S(1)}, f32[640,128]{1,0:T(8,128)S(1)}, /*index=5*/f32[640,128]{1,0:T(8,128)S(1)}) custom-call(bf16[640,512]{1,0:T(8,128)(2,1)S(1)} %get-tuple-element., ...), custom_call_target="tpu_custom_call", output_to_operand_aliasing={{0}: (3, {}), {1}: (4, {}), {2}: (5, {}), {3}: (6, {}), {4}... | custom-call | flops 1342177280 | bytes 5767168 | tf_op jit(solution)/shard_map/pallas_call | solution.py:24
  52.9 2.1 %shard_map.117 = (f32[640,512]{1,0:T(8,128)S(1)}, f32[640,128]{1,0:T(8,128)S(1)}, f32[640,128]{1,0:T(8,128)S(1)}, f32[640,512]{1,0:T(8,128)S(1)}, f32[640,128]{1,0:T(8,128)S(1)}, /*index=5*/f32[640,128]{1,0:T(8,128)S(1)}) custom-call(bf16[640,512]{1,0:T(8,128)(2,1)S(1)} %get-tuple-element., ...), custom_call_target="tpu_custom_call", output_to_operand_aliasing={{0}: (3, {}), {1}: (4, {}), {2}: (5, {}), {3}: (6, {}), {4}... | custom-call | flops 1342177280 | bytes 5767168 | tf_op jit(solution)/shard_map/pallas_call | solution.py:24
  55.0 1.9 %shard_map.118 = (f32[640,512]{1,0:T(8,128)S(1)}, f32[640,128]{1,0:T(8,128)S(1)}, f32[640,128]{1,0:T(8,128)S(1)}, f32[640,640]{1,0:T(8,128)S(1)}) custom-call(bf16[640,512]{1,0:T(8,128)(2,1)S(1)} %get-tuple-element.59.refs_0_.q_ref, bf16[640,512]{1,0:T(8,128)(2,1)S(1)} %collective-permute-done.7.refs_1_, ...), custom_call_target="tpu_custom_call", output_to_operand_aliasing={{0}: (3, {}), {1}: (4, {}), {2}: (5, {})} | custom-call | flops 1342177280 | bytes 5767168 | tf_op jit(solution)/shard_map/pallas_call | solution.py:24
  58.2 1.1 %shard_map.119 = (f32[640,512]{1,0:T(8,128)S(1)}, f32[640,128]{1,0:T(8,128)S(1)}, f32[640,128]{1,0:T(8,128)S(1)}) custom-call(bf16[640,512]{1,0:T(8,128)(2,1)S(1)} %get-tuple-element.59.refs_0_.q_ref, bf16[512,512]{1,0:T(8,128)(2,1)S(1)} %collective-permute-done.5.refs_1_, ...), custom_call_target="tpu_custom_call", output_to_operand_aliasing={{0}: (2, {}), {1}: (3, {}), {2}: (4, {})} | custom-call | flops 671088640 | bytes 3145728 | tf_op jit(solution)/shard_map/pallas_call | solution.py:24
  59.4 2.1 %collective-permute-done.6.key_ref = bf16[512,512]{1,0:T(8,128)(2,1)S(1)} collective-permute-done((bf16[512,512]{1,0:T(8,128)(2,1)S(1)}, bf16[512,512]{1,0:T(8,128)(2,1)S(1)}, u32[]{:S(2)}, u32[]{:S(2)}) %collective-permute-start.6) | collective-permute-done | bytes 524320 | tf_op jit(solution)/shard_map/ppermute | solution.py:320
  61.5 2.2 %shard_map.121 = (bf16[512,512]{1,0:T(8,128)(2,1)S(1)}, f32[8,128]{1,0:T(8,128)S(1)}, bf16[128,512]{1,0:T(8,128)(2,1)S(1)}, bf16[128,512]{1,0:T(8,128)(2,1)S(1)}) custom-call(f32[8,128]{1,0:T(8,128)S(1)} %iota.13.flags_ref, bf16[640,512]{1,0:T(8,128)(2,1)S(1)} %get-tuple-element.59.refs_0_.q_ref, bf16[512,512]{1,0:T(8,128)(2,1)S(1)} %collective-permute-done.6.key_ref, ...), custom_call_target="tpu_custom_call" | custom-call | flops 805306368 | bytes 5984256 | tf_op jit(solution)/shard_map/pallas_call | solution.py:24
  64.0 13.7 %all_to_all.10.stats_ref = f32[16,8,128]{2,1,0:T(8,128)S(1)} all-to-all(f32[16,8,128]{2,1,0:T(8,128)S(1)} %broadcast_in_dim.21), channel_id=1, replica_groups=mesh['img'=16,'row'=16] {'row'}, dimensions={0} | all-to-all | bytes 131072 | tf_op jit(solution)/shard_map/all_to_all | solution.py:300
  77.7 3.5 %shard_map.122 = bf16[512,512]{1,0:T(8,128)(2,1)} custom-call(f32[8,128]{1,0:T(8,128)S(1)} %iota.13.flags_ref, bf16[512,512]{1,0:T(8,128)(2,1)S(1)} %get-tuple-element.105.h_ref, bf16[128,512]{1,0:T(8,128)(2,1)S(1)} %collective-permute-done.11.inside_ref, bf16[128,512]{1,0:T(8,128)(2,1)S(1)} %get-tuple-element.107.outside_ref, ...), custom_call_target="tpu_custom_call" | custom-call | flops 2415919104 | bytes 5580800 | tf_op jit(solution)/shard_map/pallas_call | solution.py:24
  (40 shorter events, 2.1 us)
Async XLA Ops:
  0.1 13.7 %collective-permute-start = (bf16[512,512]{1,0:T(8,128)(2,1)}, bf16[512,512]{1,0:T(8,128)(2,1)}, u32[]{:S(2)}, u32[]{:S(2)}) collective-permute-start(bf16[512,512]{1,0:T(8,128)(2,1)} %bitcast.8), channel_id=1, source_target_pairs={{0,1},{1,0},{2,3},{3,2},{4,5},{5,4},{6,7},{7,6},{8,9},{9,8},{10,11... | collective-permute-start | bytes 1572872 | tf_op jit(solution)/shard_map/ppermute | solution.py:320
  3.3 13.2 %collective-permute-start.2 = (bf16[512,512]{1,0:T(8,128)(2,1)}, bf16[512,512]{1,0:T(8,128)(2,1)S(1)}, u32[]{:S(2)}, u32[]{:S(2)}) collective-permute-start(bf16[512,512]{1,0:T(8,128)(2,1)} %bitcast.9), channel_id=1, source_target_pairs={{0,2},{1,15},{2,4},{3,1},{4,6},{5,3},{6,8},{7,5},{8,10},{9,7},{10,... | collective-permute-start | bytes 1572872 | tf_op jit(solution)/shard_map/ppermute | solution.py:320
  7.2 1.1 %copy-start = (bf16[4,128,512]{2,1,0:T(8,128)(2,1)S(1)}, bf16[4,128,512]{2,1,0:T(8,128)(2,1)}, u32[]{:S(2)}) copy-start(bf16[4,128,512]{2,1,0:T(8,128)(2,1)} %param.11) | copy-start | bytes 1572868
  8.3 9.4 %copy-start.4 = (bf16[512,512]{1,0:T(8,128)(2,1)S(1)}, bf16[512,512]{1,0:T(8,128)(2,1)}, u32[]{:S(2)}) copy-start(bf16[512,512]{1,0:T(8,128)(2,1)} %refs_0_.2) | copy-start | bytes 1572868
  9.8 11.8 %all-to-all-start = ((f32[16,8,128]{2,1,0:T(8,128)}), f32[16,8,128]{2,1,0:T(8,128)S(1)}, u32[]{:S(2)}, u32[]{:S(2)}) async-start(f32[16,8,128]{2,1,0:T(8,128)} %broadcast_in_dim.20), calls=%async_computation | async-start | bytes 131072 | tf_op jit(solution)/shard_map/all_to_all | solution.py:300
  13.8 9.8 %copy-start.1 = (bf16[4,128,512]{2,1,0:T(8,128)(2,1)S(1)}, bf16[4,128,512]{2,1,0:T(8,128)(2,1)}, u32[]{:S(2)}) copy-start(bf16[4,128,512]{2,1,0:T(8,128)(2,1)} %param.11) | copy-start | bytes 1572868
  13.8 9.8 %copy-start.2 = (f32[512]{0:T(512)S(1)}, f32[512]{0:T(512)}, u32[]{:S(2)}) copy-start(f32[512]{0:T(512)} %param.12) | copy-start | bytes 6148
  13.8 9.8 %copy-start.3 = (f32[512]{0:T(512)S(1)}, f32[512]{0:T(512)}, u32[]{:S(2)}) copy-start(f32[512]{0:T(512)} %param.13) | copy-start | bytes 6148
  13.8 9.8 %collective-permute-start.1 = (bf16[512,512]{1,0:T(8,128)(2,1)}, bf16[512,512]{1,0:T(8,128)(2,1)S(1)}, u32[]{:S(2)}, u32[]{:S(2)}) collective-permute-start(bf16[512,512]{1,0:T(8,128)(2,1)} %collective-permute-done), channel_id=1, source_target_pairs={{0,2},{1,15},{2,4},{3,1},{4,6},{5,3},{6,8},{7,5},{8,10},{9,7},{10,... | collective-permute-start | bytes 1572872 | tf_op jit(solution)/shard_map/ppermute | solution.py:320
  16.5 12.7 %collective-permute-start.3 = (bf16[512,512]{1,0:T(8,128)(2,1)S(1)}, bf16[512,512]{1,0:T(8,128)(2,1)S(1)}, u32[]{:S(2)}, u32[]{:S(2)}) collective-permute-start(bf16[512,512]{1,0:T(8,128)(2,1)S(1)} %collective-permute-done.2.refs_2_), channel_id=1, source_target_pairs={{0,2},{1,15},{2,4},{3,1},{4,6},{5,3},{6,8},{7,5},{8,10},{9,7},{10,... | collective-permute-start | bytes 1572872 | tf_op jit(solution)/shard_map/ppermute | solution.py:320
  17.7 1.0 %copy-start.5 = (bf16[512,512]{1,0:T(8,128)(2,1)S(1)}, bf16[512,512]{1,0:T(8,128)(2,1)}, u32[]{:S(2)}) copy-start(bf16[512,512]{1,0:T(8,128)(2,1)} %refs_1_.2) | copy-start | bytes 1572868
  24.2 18.8 %collective-permute-start.7 = (bf16[640,512]{1,0:T(8,128)(2,1)S(1)}, bf16[640,512]{1,0:T(8,128)(2,1)S(1)}, u32[]{:S(2)}, u32[]{:S(2)}) collective-permute-start(bf16[640,512]{1,0:T(8,128)(2,1)S(1)} %get-tuple-element.59.refs_0_.q_ref), channel_id=1, source_target_pairs={{0,1},{1,0},{2,3},{3,2},{4,5},{5,4},{6,7},{7,6},{8,9},{9,8},{10,11... | collective-permute-start | bytes 1966088 | tf_op jit(solution)/shard_map/ppermute | solution.py:320
  26.2 8.6 %collective-permute-start.8 = (bf16[512,512]{1,0:T(8,128)(2,1)S(1)}, bf16[512,512]{1,0:T(8,128)(2,1)S(1)}, u32[]{:S(2)}, u32[]{:S(2)}) collective-permute-start(bf16[512,512]{1,0:T(8,128)(2,1)S(1)} %collective-permute-done.1.far_ref.refs_2_), channel_id=1, source_target_pairs={{0,2},{1,15},{2,4},{3,1},{4,6},{5,3},{6,8},{7,5},{8,10},{9,7},{10,... | collective-permute-start | bytes 1572872 | tf_op jit(solution)/shard_map/ppermute | solution.py:320
  29.2 11.2 %collective-permute-start.4 = (bf16[512,512]{1,0:T(8,128)(2,1)S(1)}, bf16[512,512]{1,0:T(8,128)(2,1)S(1)}, u32[]{:S(2)}, u32[]{:S(2)}) collective-permute-start(bf16[512,512]{1,0:T(8,128)(2,1)S(1)} %collective-permute-done.3.refs_2_), channel_id=1, source_target_pairs={{0,2},{1,15},{2,4},{3,1},{4,6},{5,3},{6,8},{7,5},{8,10},{9,7},{10,... | collective-permute-start | bytes 1572872 | tf_op jit(solution)/shard_map/ppermute | solution.py:320
  34.8 20.1 %collective-permute-start.9 = (bf16[512,512]{1,0:T(8,128)(2,1)S(1)}, bf16[512,512]{1,0:T(8,128)(2,1)S(1)}, u32[]{:S(2)}, u32[]{:S(2)}) collective-permute-start(bf16[512,512]{1,0:T(8,128)(2,1)S(1)} %collective-permute-done.8.refs_2_), channel_id=1, source_target_pairs={{0,2},{1,15},{2,4},{3,1},{4,6},{5,3},{6,8},{7,5},{8,10},{9,7},{10,... | collective-permute-start | bytes 1572872 | tf_op jit(solution)/shard_map/ppermute | solution.py:320
  40.5 16.8 %collective-permute-start.5 = (bf16[512,512]{1,0:T(8,128)(2,1)S(1)}, bf16[512,512]{1,0:T(8,128)(2,1)S(1)}, u32[]{:S(2)}, u32[]{:S(2)}) collective-permute-start(bf16[512,512]{1,0:T(8,128)(2,1)S(1)} %collective-permute-done.4.refs_2_), channel_id=1, source_target_pairs={{0,2},{1,15},{2,4},{3,1},{4,6},{5,3},{6,8},{7,5},{8,10},{9,7},{10,... | collective-permute-start | bytes 1572872 | tf_op jit(solution)/shard_map/ppermute | solution.py:320
  50.8 7.0 %slice-start = ((s8[4718592]{0:T(1024)(128)(4,1)}), s8[4194304]{0:T(1024)(128)(4,1)S(1)}, s32[]{:S(2)}) async-start(s8[4718592]{0:T(1024)(128)(4,1)} %bitcast.16), calls=%async_computation.2 | async-start | bytes 8388608
  52.9 4.9 %slice-start.1 = ((s8[4718592]{0:T(1024)(128)(4,1)}), s8[524288]{0:T(1024)(128)(4,1)S(1)}, s32[]{:S(2)}) async-start(s8[4718592]{0:T(1024)(128)(4,1)} %bitcast.16), calls=%async_computation.3 | async-start | bytes 1048576
  55.0 2.8 %copy-start.6 = (bf16[512,512]{1,0:T(8,128)(2,1)S(1)}, bf16[512,512]{1,0:T(8,128)(2,1)}, u32[]{:S(2)}) copy-start(bf16[512,512]{1,0:T(8,128)(2,1)} %refs_0_.3) | copy-start | bytes 1572868
  55.0 2.8 %copy-start.7 = (bf16[512,512]{1,0:T(8,128)(2,1)S(1)}, bf16[512,512]{1,0:T(8,128)(2,1)}, u32[]{:S(2)}) copy-start(bf16[512,512]{1,0:T(8,128)(2,1)} %refs_1_.3) | copy-start | bytes 1572868
  56.9 4.6 %collective-permute-start.10 = (f32[640,640]{1,0:T(8,128)S(1)}, f32[640,640]{1,0:T(8,128)S(1)}, u32[]{:S(2)}, u32[]{:S(2)}) collective-permute-start(f32[640,640]{1,0:T(8,128)S(1)} %get-tuple-element.102), channel_id=1, source_target_pairs={{0,1},{1,0},{2,3},{3,2},{4,5},{5,4},{6,7},{7,6},{8,9},{9,8},{10,11... | collective-permute-start | bytes 4915208 | tf_op jit(solution)/shard_map/ppermute | solution.py:320
  57.3 4.2 %collective-permute-start.6 = (bf16[512,512]{1,0:T(8,128)(2,1)S(1)}, bf16[512,512]{1,0:T(8,128)(2,1)S(1)}, u32[]{:S(2)}, u32[]{:S(2)}) collective-permute-start(bf16[512,512]{1,0:T(8,128)(2,1)S(1)} %collective-permute-done.5.refs_1_), channel_id=1, source_target_pairs={{0,1},{1,0},{2,3},{3,2},{4,5},{5,4},{6,7},{7,6},{8,9},{9,8},{10,11... | collective-permute-start | bytes 1572872 | tf_op jit(solution)/shard_map/ppermute | solution.py:320
  61.5 16.2 %copy-start.8 = (f32[512]{0:T(512)S(1)}, f32[512]{0:T(512)}, u32[]{:S(2)}) copy-start(f32[512]{0:T(512)} %param.18) | copy-start | bytes 6148
  61.5 16.2 %copy-start.9 = (f32[512]{0:T(512)S(1)}, f32[512]{0:T(512)}, u32[]{:S(2)}) copy-start(f32[512]{0:T(512)} %param.19) | copy-start | bytes 6148
  61.5 16.2 %copy-start.10 = (f32[512]{0:T(512)S(1)}, f32[512]{0:T(512)}, u32[]{:S(2)}) copy-start(f32[512]{0:T(512)} %param.21) | copy-start | bytes 6148
  63.7 13.9 %collective-permute-start.11 = (bf16[128,512]{1,0:T(8,128)(2,1)S(1)}, bf16[128,512]{1,0:T(8,128)(2,1)S(1)}, u32[]{:S(2)}, u32[]{:S(2)}) collective-permute-start(bf16[128,512]{1,0:T(8,128)(2,1)S(1)} %get-tuple-element.106), channel_id=1, source_target_pairs={{0,1},{1,0},{2,3},{3,2},{4,5},{5,4},{6,7},{7,6},{8,9},{9,8},{10,11... | collective-permute-start | bytes 393224 | tf_op jit(solution)/shard_map/ppermute | solution.py:320

commit v5 on v4

--- a/solution.py
+++ b/solution.py
@@ -325,12 +325,12 @@
     wvo = fold(w_value, w_out, False, taps)
     near, far = x, move(x, swap)
     pieces = [x]
-    for step in range(1, chips // 2 + 1):
+    for _ in range(1, chips // 2):
         near = move(near, ring)
-        pieces.append(near)
-        if step < chips // 2:
-            far = move(far, ring)
-            pieces.append(far)
+        far = move(far, ring)
+        pieces += [near, far]
+    last_a = move(near[: rows // 2], ring)
+    last_b = move(near[rows // 2 :], ring)
 
     stats = everyone(stats)
     query, coef, halo = call(
@@ -346,13 +346,14 @@
     )
     other = move(query, swap)
     state = None
-    *early, late = pieces
-    for n, key in enumerate(early):
-        state = attend([query, other], [key], state, n == len(early) - 1)
+    for n, key in enumerate(pieces):
+        state = attend([query, other], [key], state, n == len(pieces) - 1)
     *mine, theirs = state
     met = move(theirs, swap)
-    across = move(late, swap)
-    mine = attend([query], [late], mine)
+    across_a = move(last_a, swap)
+    mine = attend([query], [last_a], mine)
+    across = move(last_b, swap)
+    mine = attend([query], [across_a, last_b], mine)
     edge = jax.ShapeDtypeStruct((W, C), BF16)
     hidden, tile2, inside, outside = call(
         output_kernel,

time: 81.4 us -> 85.3 us (1.048)
  starting transfers between devices: 26.8 us -> 28.6 us
  local copies, waits for them, and re-layouts: 2.89 us -> 3.92 us
    ppermute x12 -> x14, waiting for transfers between devices: 12.1 us -> 13.7 us  [local(): move = lambda v, to: lax.ppermute(v, 'row', to)]
    all_to_all x1, starting transfers between devices: 4.01 us -> 5.29 us  [everyone(): lax.all_to_all(copies, 'row', split_axis=0, concat_axis=0, tiled=True)]
    all_to_all x1, waiting for transfers between devices: 2.38 us -> 1.35 us  [everyone(): lax.all_to_all(copies, 'row', split_axis=0, concat_axis=0, tiled=True)]
    unnamed x26, local copies, waits for them, and re-layouts: 2.18 us -> 3.17 us
    pallas_call x14 -> x15, Pallas kernels: 23 us -> 23.5 us  [call(): pl.pallas_call(kernel, out_shape=outs, in_specs=specs, out_specs=jax.tree...]
    ppermute x12 -> x14, starting transfers between devices: 22.8 us -> 23.3 us  [local(): move = lambda v, to: lax.ppermute(v, 'row', to)]
  transfers between devices with their start and end apart: 13 -> 15, of which waited for: 6 -> 6; matrix products, arithmetic and copies ran while one was open for 1% -> 1% of each run, Pallas kernels for 21% -> 21%
where the time goes in v5:
time: 85.3 us; the launch traced here: 85 us
  starting transfers between devices  28.6 us (34%)
  Pallas kernels  23.5 us (28%)
  waiting for transfers between devices  15 us (18%)
  blocking collectives  13.7 us (16%)
  local copies, waits for them, and re-layouts  3.92 us (5%)
    pallas_call x15, Pallas kernels, call(): pl.pallas_call(kernel, out_shape=outs, in_specs=specs, out_specs=jax.tree...  23.5 us
    ppermute x14, starting transfers between devices, local(): move = lambda v, to: lax.ppermute(v, 'row', to)  23.3 us
    all_to_all x1, blocking collectives, everyone(): lax.all_to_all(copies, 'row', split_axis=0, concat_axis=0, tiled=True)  13.7 us
    ppermute x14, waiting for transfers between devices, local(): move = lambda v, to: lax.ppermute(v, 'row', to)  13.7 us
    all_to_all x1, starting transfers between devices, everyone(): lax.all_to_all(copies, 'row', split_axis=0, concat_axis=0, tiled=True)  5.29 us
    unnamed x26, local copies, waits for them, and re-layouts  3.17 us
  transfers between devices with their start and end apart: 15, of which 6 were waited for; matrix products, arithmetic and copies ran while one was open for 1% of the time, Pallas kernels for 21%

profile of v5, /device:TPU:1, one launch (start us, length us, event | category | flops | bytes accessed | tf_op | source)
XLA Modules:
  0.0 85.0 jit_solution(17048073311460728034)
XLA Ops:
  0.1 6.4 %collective-permute-start.2 = (bf16[512,512]{1,0:T(8,128)(2,1)}, bf16[512,512]{1,0:T(8,128)(2,1)S(1)}, u32[]{:S(2)}, u32[]{:S(2)}) collective-permute-start(bf16[512,512]{1,0:T(8,128)(2,1)} %bitcast.8), channel_id=1, source_target_pairs={{0,2},{1,15},{2,4},{3,1},{4,6},{5,3},{6,8},{7,5},{8,10},{9,7},{10,... | collective-permute-start | bytes 1572872 | tf_op jit(solution)/shard_map/ppermute | solution.py:320
  6.5 6.4 %collective-permute-done.2.refs_2_ = bf16[512,512]{1,0:T(8,128)(2,1)S(1)} collective-permute-done((bf16[512,512]{1,0:T(8,128)(2,1)}, bf16[512,512]{1,0:T(8,128)(2,1)S(1)}, u32[]{:S(2)}, u32[]{:S(2)}) %collective-permute-start.2) | collective-permute-done | bytes 524320 | tf_op jit(solution)/shard_map/ppermute | solution.py:320
  12.9 3.0 %collective-permute-start.3 = (bf16[512,512]{1,0:T(8,128)(2,1)S(1)}, bf16[512,512]{1,0:T(8,128)(2,1)S(1)}, u32[]{:S(2)}, u32[]{:S(2)}) collective-permute-start(bf16[512,512]{1,0:T(8,128)(2,1)S(1)} %collective-permute-done.2.refs_2_), channel_id=1, source_target_pairs={{0,2},{1,15},{2,4},{3,1},{4,6},{5,3},{6,8},{7,5},{8,10},{9,7},{10,... | collective-permute-start | bytes 1572872 | tf_op jit(solution)/shard_map/ppermute | solution.py:320
  15.9 1.0 %copy-done = bf16[4,128,512]{2,1,0:T(8,128)(2,1)S(1)} copy-done((bf16[4,128,512]{2,1,0:T(8,128)(2,1)S(1)}, bf16[4,128,512]{2,1,0:T(8,128)(2,1)}, u32[]{:S(2)}) %copy-start) | copy-done | bytes 524312
  17.0 0.9 %shard_map.109 = f32[8,128]{1,0:T(8,128)S(1)} custom-call(bf16[512,512]{1,0:T(8,128)(2,1)S(1)} %bitcast.10), custom_call_target="tpu_custom_call" | custom-call | flops 20000000000 | bytes 524288 | tf_op jit(solution)/shard_map/pallas_call | solution.py:24
  17.9 0.6 broadcast_in_dim.20
  18.5 5.3 %all-to-all-start = ((f32[16,8,128]{2,1,0:T(8,128)}), f32[16,8,128]{2,1,0:T(8,128)S(1)}, u32[]{:S(2)}, u32[]{:S(2)}) async-start(f32[16,8,128]{2,1,0:T(8,128)} %broadcast_in_dim.20), calls=%async_computation | async-start | bytes 131072 | tf_op jit(solution)/shard_map/all_to_all | solution.py:300
  23.8 2.6 %collective-permute-start.1 = (bf16[512,512]{1,0:T(8,128)(2,1)}, bf16[512,512]{1,0:T(8,128)(2,1)S(1)}, u32[]{:S(2)}, u32[]{:S(2)}) collective-permute-start(bf16[512,512]{1,0:T(8,128)(2,1)} %collective-permute-done), channel_id=1, source_target_pairs={{0,2},{1,15},{2,4},{3,1},{4,6},{5,3},{6,8},{7,5},{8,10},{9,7},{10,... | collective-permute-start | bytes 1572872 | tf_op jit(solution)/shard_map/ppermute | solution.py:320
  26.5 1.2 %collective-permute-start.4 = (bf16[512,512]{1,0:T(8,128)(2,1)S(1)}, bf16[512,512]{1,0:T(8,128)(2,1)S(1)}, u32[]{:S(2)}, u32[]{:S(2)}) collective-permute-start(bf16[512,512]{1,0:T(8,128)(2,1)S(1)} %collective-permute-done.3.refs_2_), channel_id=1, source_target_pairs={{0,2},{1,15},{2,4},{3,1},{4,6},{5,3},{6,8},{7,5},{8,10},{9,7},{10,... | collective-permute-start | bytes 1572872 | tf_op jit(solution)/shard_map/ppermute | solution.py:320
  27.7 1.0 %copy-done.4 = bf16[512,512]{1,0:T(8,128)(2,1)S(1)} copy-done((bf16[512,512]{1,0:T(8,128)(2,1)S(1)}, bf16[512,512]{1,0:T(8,128)(2,1)}, u32[]{:S(2)}) %copy-start.4) | copy-done | bytes 524312
  28.7 1.0 %copy-done.5 = bf16[512,512]{1,0:T(8,128)(2,1)S(1)} copy-done((bf16[512,512]{1,0:T(8,128)(2,1)S(1)}, bf16[512,512]{1,0:T(8,128)(2,1)}, u32[]{:S(2)}) %copy-start.5) | copy-done | bytes 524312
  30.2 1.3 %all-to-all-done.stats_ref = f32[16,8,128]{2,1,0:T(8,128)S(1)} async-done(((f32[16,8,128]{2,1,0:T(8,128)}), f32[16,8,128]{2,1,0:T(8,128)S(1)}, u32[]{:S(2)}, u32[]{:S(2)}) %all-to-all-start) | async-done | bytes 65568 | tf_op jit(solution)/shard_map/all_to_all | solution.py:300
  31.6 2.0 %collective-permute-done.1.far_ref.refs_2_ = bf16[512,512]{1,0:T(8,128)(2,1)S(1)} collective-permute-done((bf16[512,512]{1,0:T(8,128)(2,1)}, bf16[512,512]{1,0:T(8,128)(2,1)S(1)}, u32[]{:S(2)}, u32[]{:S(2)}) %collective-permute-start.1) | collective-permute-done | bytes 524320 | tf_op jit(solution)/shard_map/ppermute | solution.py:320
  34.2 2.0 %collective-permute-start.9 = (bf16[640,512]{1,0:T(8,128)(2,1)S(1)}, bf16[640,512]{1,0:T(8,128)(2,1)S(1)}, u32[]{:S(2)}, u32[]{:S(2)}) collective-permute-start(bf16[640,512]{1,0:T(8,128)(2,1)S(1)} %get-tuple-element.62.refs_0_.q_ref), channel_id=1, source_target_pairs={{0,1},{1,0},{2,3},{3,2},{4,5},{5,4},{6,7},{7,6},{8,9},{9,8},{10,11... | collective-permute-start | bytes 1966088 | tf_op jit(solution)/shard_map/ppermute | solution.py:320
  36.2 1.3 %collective-permute-start.10 = (bf16[512,512]{1,0:T(8,128)(2,1)S(1)}, bf16[512,512]{1,0:T(8,128)(2,1)S(1)}, u32[]{:S(2)}, u32[]{:S(2)}) collective-permute-start(bf16[512,512]{1,0:T(8,128)(2,1)S(1)} %collective-permute-done.1.far_ref.refs_2_), channel_id=1, source_target_pairs={{0,2},{1,15},{2,4},{3,1},{4,6},{5,3},{6,8},{7,5},{8,10},{9,7},{10,... | collective-permute-start | bytes 1572872 | tf_op jit(solution)/shard_map/ppermute | solution.py:320
  37.5 1.8 %collective-permute-done.4.refs_2_ = bf16[512,512]{1,0:T(8,128)(2,1)S(1)} collective-permute-done((bf16[512,512]{1,0:T(8,128)(2,1)S(1)}, bf16[512,512]{1,0:T(8,128)(2,1)S(1)}, u32[]{:S(2)}, u32[]{:S(2)}) %collective-permute-start.4) | collective-permute-done | bytes 524320 | tf_op jit(solution)/shard_map/ppermute | solution.py:320
  39.3 2.6 %collective-permute-start.7 = (bf16[256,512]{1,0:T(8,128)(2,1)S(1)}, bf16[256,512]{1,0:T(8,128)(2,1)S(1)}, u32[]{:S(2)}, u32[]{:S(2)}) collective-permute-start(bf16[256,512]{1,0:T(8,128)(2,1)S(1)} %get-tuple-element.115), channel_id=1, source_target_pairs={{0,2},{1,15},{2,4},{3,1},{4,6},{5,3},{6,8},{7,5},{8,10},{9,7},{10,... | collective-permute-start | bytes 786440 | tf_op jit(solution)/shard_map/ppermute | solution.py:320
  42.1 2.7 %collective-permute-done.10.refs_2_ = bf16[512,512]{1,0:T(8,128)(2,1)S(1)} collective-permute-done((bf16[512,512]{1,0:T(8,128)(2,1)S(1)}, bf16[512,512]{1,0:T(8,128)(2,1)S(1)}, u32[]{:S(2)}, u32[]{:S(2)}) %collective-permute-start.10) | collective-permute-done | bytes 524320 | tf_op jit(solution)/shard_map/ppermute | solution.py:320
  44.8 2.5 %collective-permute-start.11 = (bf16[512,512]{1,0:T(8,128)(2,1)S(1)}, bf16[512,512]{1,0:T(8,128)(2,1)S(1)}, u32[]{:S(2)}, u32[]{:S(2)}) collective-permute-start(bf16[512,512]{1,0:T(8,128)(2,1)S(1)} %collective-permute-done.10.refs_2_), channel_id=1, source_target_pairs={{0,2},{1,15},{2,4},{3,1},{4,6},{5,3},{6,8},{7,5},{8,10},{9,7},{10,... | collective-permute-start | bytes 1572872 | tf_op jit(solution)/shard_map/ppermute | solution.py:320
  47.4 1.6 %shard_map.112 = (f32[640,512]{1,0:T(8,128)S(1)}, f32[640,128]{1,0:T(8,128)S(1)}, f32[640,128]{1,0:T(8,128)S(1)}, f32[640,512]{1,0:T(8,128)S(1)}, f32[640,128]{1,0:T(8,128)S(1)}, /*index=5*/f32[640,128]{1,0:T(8,128)S(1)}) custom-call(bf16[640,512]{1,0:T(8,128)(2,1)S(1)} %get-tuple-element.62.refs_0_.q_ref, ...), custom_call_target="tpu_custom_call" | custom-call | flops 1342177280 | bytes 1835008 | tf_op jit(solution)/shard_map/pallas_call | solution.py:24
  48.9 2.0 %shard_map.113 = (f32[640,512]{1,0:T(8,128)S(1)}, f32[640,128]{1,0:T(8,128)S(1)}, f32[640,128]{1,0:T(8,128)S(1)}, f32[640,512]{1,0:T(8,128)S(1)}, f32[640,128]{1,0:T(8,128)S(1)}, /*index=5*/f32[640,128]{1,0:T(8,128)S(1)}) custom-call(bf16[640,512]{1,0:T(8,128)(2,1)S(1)} %get-tuple-element., ...), custom_call_target="tpu_custom_call", output_to_operand_aliasing={{0}: (3, {}), {1}: (4, {}), {2}: (5, {}), {3}: (6, {}), {4}... | custom-call | flops 1342177280 | bytes 5767168 | tf_op jit(solution)/shard_map/pallas_call | solution.py:24
  51.0 2.0 %shard_map.114 = (f32[640,512]{1,0:T(8,128)S(1)}, f32[640,128]{1,0:T(8,128)S(1)}, f32[640,128]{1,0:T(8,128)S(1)}, f32[640,512]{1,0:T(8,128)S(1)}, f32[640,128]{1,0:T(8,128)S(1)}, /*index=5*/f32[640,128]{1,0:T(8,128)S(1)}) custom-call(bf16[640,512]{1,0:T(8,128)(2,1)S(1)} %get-tuple-element., ...), custom_call_target="tpu_custom_call", output_to_operand_aliasing={{0}: (3, {}), {1}: (4, {}), {2}: (5, {}), {3}: (6, {}), {4}... | custom-call | flops 1342177280 | bytes 5767168 | tf_op jit(solution)/shard_map/pallas_call | solution.py:24
  53.0 2.0 %shard_map.115 = (f32[640,512]{1,0:T(8,128)S(1)}, f32[640,128]{1,0:T(8,128)S(1)}, f32[640,128]{1,0:T(8,128)S(1)}, f32[640,512]{1,0:T(8,128)S(1)}, f32[640,128]{1,0:T(8,128)S(1)}, /*index=5*/f32[640,128]{1,0:T(8,128)S(1)}) custom-call(bf16[640,512]{1,0:T(8,128)(2,1)S(1)} %get-tuple-element., ...), custom_call_target="tpu_custom_call", output_to_operand_aliasing={{0}: (3, {}), {1}: (4, {}), {2}: (5, {}), {3}: (6, {}), {4}... | custom-call | flops 1342177280 | bytes 5767168 | tf_op jit(solution)/shard_map/pallas_call | solution.py:24
  55.1 2.0 %shard_map.116 = (f32[640,512]{1,0:T(8,128)S(1)}, f32[640,128]{1,0:T(8,128)S(1)}, f32[640,128]{1,0:T(8,128)S(1)}, f32[640,512]{1,0:T(8,128)S(1)}, f32[640,128]{1,0:T(8,128)S(1)}, /*index=5*/f32[640,128]{1,0:T(8,128)S(1)}) custom-call(bf16[640,512]{1,0:T(8,128)(2,1)S(1)} %get-tuple-element., ...), custom_call_target="tpu_custom_call", output_to_operand_aliasing={{0}: (3, {}), {1}: (4, {}), {2}: (5, {}), {3}: (6, {}), {4}... | custom-call | flops 1342177280 | bytes 5767168 | tf_op jit(solution)/shard_map/pallas_call | solution.py:24
  57.2 2.0 %shard_map.117 = (f32[640,512]{1,0:T(8,128)S(1)}, f32[640,128]{1,0:T(8,128)S(1)}, f32[640,128]{1,0:T(8,128)S(1)}, f32[640,512]{1,0:T(8,128)S(1)}, f32[640,128]{1,0:T(8,128)S(1)}, /*index=5*/f32[640,128]{1,0:T(8,128)S(1)}) custom-call(bf16[640,512]{1,0:T(8,128)(2,1)S(1)} %get-tuple-element., ...), custom_call_target="tpu_custom_call", output_to_operand_aliasing={{0}: (3, {}), {1}: (4, {}), {2}: (5, {}), {3}: (6, {}), {4}... | custom-call | flops 1342177280 | bytes 5767168 | tf_op jit(solution)/shard_map/pallas_call | solution.py:24
  59.8 1.9 %shard_map.118 = (f32[640,512]{1,0:T(8,128)S(1)}, f32[640,128]{1,0:T(8,128)S(1)}, f32[640,128]{1,0:T(8,128)S(1)}, f32[640,640]{1,0:T(8,128)S(1)}) custom-call(bf16[640,512]{1,0:T(8,128)(2,1)S(1)} %get-tuple-element.62.refs_0_.q_ref, bf16[640,512]{1,0:T(8,128)(2,1)S(1)} %collective-permute-done.9.refs_1_, ...), custom_call_target="tpu_custom_call", output_to_operand_aliasing={{0}: (3, {}), {1}: (4, {}), {2}: (5, {})} | custom-call | flops 1342177280 | bytes 5767168 | tf_op jit(solution)/shard_map/pallas_call | solution.py:24
  62.6 0.9 %shard_map.119 = (f32[640,512]{1,0:T(8,128)S(1)}, f32[640,128]{1,0:T(8,128)S(1)}, f32[640,128]{1,0:T(8,128)S(1)}) custom-call(bf16[640,512]{1,0:T(8,128)(2,1)S(1)} %get-tuple-element.62.refs_0_.q_ref, bf16[256,512]{1,0:T(8,128)(2,1)S(1)} %collective-permute-done.7.refs_1_, ...), custom_call_target="tpu_custom_call", output_to_operand_aliasing={{0}: (2, {}), {1}: (3, {}), {2}: (4, {})} | custom-call | flops 335544320 | bytes 2883584 | tf_op jit(solution)/shard_map/pallas_call | solution.py:24
  63.6 1.1 %shard_map.120 = (f32[640,512]{1,0:T(8,128)S(1)}, f32[640,128]{1,0:T(8,128)S(1)}, f32[640,128]{1,0:T(8,128)S(1)}) custom-call(bf16[640,512]{1,0:T(8,128)(2,1)S(1)} %get-tuple-element.62.refs_0_.q_ref, bf16[256,512]{1,0:T(8,128)(2,1)S(1)} %collective-permute-done.8.refs_1_, ...), custom_call_target="tpu_custom_call", output_to_operand_aliasing={{0}: (3, {}), {1}: (4, {}), {2}: (5, {})} | custom-call | flops 671088640 | bytes 3145728 | tf_op jit(solution)/shard_map/pallas_call | solution.py:24
  64.7 0.7 collective-permute-done.12.met_ref
  65.4 2.0 %shard_map.122 = (bf16[512,512]{1,0:T(8,128)(2,1)S(1)}, f32[8,128]{1,0:T(8,128)S(1)}, bf16[128,512]{1,0:T(8,128)(2,1)S(1)}, bf16[128,512]{1,0:T(8,128)(2,1)S(1)}) custom-call(f32[8,128]{1,0:T(8,128)S(1)} %iota.13.flags_ref, bf16[640,512]{1,0:T(8,128)(2,1)S(1)} %get-tuple-element.62.refs_0_.q_ref, bf16[256,512]{1,0:T(8,128)(2,1)S(1)} %collective-permute-done.6.key_ref, ...), custom_call_target="tpu_custom_call" | custom-call | flops 805306368 | bytes 5722112 | tf_op jit(solution)/shard_map/pallas_call | solution.py:24
  67.8 13.7 %all_to_all.10.stats_ref = f32[16,8,128]{2,1,0:T(8,128)S(1)} all-to-all(f32[16,8,128]{2,1,0:T(8,128)S(1)} %broadcast_in_dim.21), channel_id=1, replica_groups=mesh['img'=16,'row'=16] {'row'}, dimensions={0} | all-to-all | bytes 131072 | tf_op jit(solution)/shard_map/all_to_all | solution.py:300
  81.5 3.5 %shard_map.123 = bf16[512,512]{1,0:T(8,128)(2,1)} custom-call(f32[8,128]{1,0:T(8,128)S(1)} %iota.13.flags_ref, bf16[512,512]{1,0:T(8,128)(2,1)S(1)} %get-tuple-element.111.h_ref, bf16[128,512]{1,0:T(8,128)(2,1)S(1)} %collective-permute-done.13.inside_ref, bf16[128,512]{1,0:T(8,128)(2,1)S(1)} %get-tuple-element.113.outside_ref, ...), custom_call_target="tpu_custom_call" | custom-call | flops 2415919104 | bytes 5580800 | tf_op jit(solution)/shard_map/pallas_call | solution.py:24
  (46 shorter events, 3.3 us)
Async XLA Ops:
  0.1 12.9 %collective-permute-start.2 = (bf16[512,512]{1,0:T(8,128)(2,1)}, bf16[512,512]{1,0:T(8,128)(2,1)S(1)}, u32[]{:S(2)}, u32[]{:S(2)}) collective-permute-start(bf16[512,512]{1,0:T(8,128)(2,1)} %bitcast.8), channel_id=1, source_target_pairs={{0,2},{1,15},{2,4},{3,1},{4,6},{5,3},{6,8},{7,5},{8,10},{9,7},{10,... | collective-permute-start | bytes 1572872 | tf_op jit(solution)/shard_map/ppermute | solution.py:320
  6.5 17.3 %collective-permute-start = (bf16[512,512]{1,0:T(8,128)(2,1)}, bf16[512,512]{1,0:T(8,128)(2,1)}, u32[]{:S(2)}, u32[]{:S(2)}) collective-permute-start(bf16[512,512]{1,0:T(8,128)(2,1)} %bitcast.9), channel_id=1, source_target_pairs={{0,1},{1,0},{2,3},{3,2},{4,5},{5,4},{6,7},{7,6},{8,9},{9,8},{10,11... | collective-permute-start | bytes 1572872 | tf_op jit(solution)/shard_map/ppermute | solution.py:320
  12.9 13.5 %collective-permute-start.3 = (bf16[512,512]{1,0:T(8,128)(2,1)S(1)}, bf16[512,512]{1,0:T(8,128)(2,1)S(1)}, u32[]{:S(2)}, u32[]{:S(2)}) collective-permute-start(bf16[512,512]{1,0:T(8,128)(2,1)S(1)} %collective-permute-done.2.refs_2_), channel_id=1, source_target_pairs={{0,2},{1,15},{2,4},{3,1},{4,6},{5,3},{6,8},{7,5},{8,10},{9,7},{10,... | collective-permute-start | bytes 1572872 | tf_op jit(solution)/shard_map/ppermute | solution.py:320
  15.9 1.0 %copy-start = (bf16[4,128,512]{2,1,0:T(8,128)(2,1)S(1)}, bf16[4,128,512]{2,1,0:T(8,128)(2,1)}, u32[]{:S(2)}) copy-start(bf16[4,128,512]{2,1,0:T(8,128)(2,1)} %param.11) | copy-start | bytes 1572868
  18.5 13.1 %all-to-all-start = ((f32[16,8,128]{2,1,0:T(8,128)}), f32[16,8,128]{2,1,0:T(8,128)S(1)}, u32[]{:S(2)}, u32[]{:S(2)}) async-start(f32[16,8,128]{2,1,0:T(8,128)} %broadcast_in_dim.20), calls=%async_computation | async-start | bytes 131072 | tf_op jit(solution)/shard_map/all_to_all | solution.py:300
  23.8 9.8 %copy-start.1 = (bf16[4,128,512]{2,1,0:T(8,128)(2,1)S(1)}, bf16[4,128,512]{2,1,0:T(8,128)(2,1)}, u32[]{:S(2)}) copy-start(bf16[4,128,512]{2,1,0:T(8,128)(2,1)} %param.11) | copy-start | bytes 1572868
  23.8 9.8 %copy-start.2 = (f32[512]{0:T(512)S(1)}, f32[512]{0:T(512)}, u32[]{:S(2)}) copy-start(f32[512]{0:T(512)} %param.12) | copy-start | bytes 6148
  23.8 9.8 %copy-start.3 = (f32[512]{0:T(512)S(1)}, f32[512]{0:T(512)}, u32[]{:S(2)}) copy-start(f32[512]{0:T(512)} %param.13) | copy-start | bytes 6148
  23.8 9.8 %collective-permute-start.1 = (bf16[512,512]{1,0:T(8,128)(2,1)}, bf16[512,512]{1,0:T(8,128)(2,1)S(1)}, u32[]{:S(2)}, u32[]{:S(2)}) collective-permute-start(bf16[512,512]{1,0:T(8,128)(2,1)} %collective-permute-done), channel_id=1, source_target_pairs={{0,2},{1,15},{2,4},{3,1},{4,6},{5,3},{6,8},{7,5},{8,10},{9,7},{10,... | collective-permute-start | bytes 1572872 | tf_op jit(solution)/shard_map/ppermute | solution.py:320
  26.5 12.7 %collective-permute-start.4 = (bf16[512,512]{1,0:T(8,128)(2,1)S(1)}, bf16[512,512]{1,0:T(8,128)(2,1)S(1)}, u32[]{:S(2)}, u32[]{:S(2)}) collective-permute-start(bf16[512,512]{1,0:T(8,128)(2,1)S(1)} %collective-permute-done.3.refs_2_), channel_id=1, source_target_pairs={{0,2},{1,15},{2,4},{3,1},{4,6},{5,3},{6,8},{7,5},{8,10},{9,7},{10,... | collective-permute-start | bytes 1572872 | tf_op jit(solution)/shard_map/ppermute | solution.py:320
  27.7 1.0 %copy-start.4 = (bf16[512,512]{1,0:T(8,128)(2,1)S(1)}, bf16[512,512]{1,0:T(8,128)(2,1)}, u32[]{:S(2)}) copy-start(bf16[512,512]{1,0:T(8,128)(2,1)} %refs_0_.2) | copy-start | bytes 1572868
  28.7 1.0 %copy-start.5 = (bf16[512,512]{1,0:T(8,128)(2,1)S(1)}, bf16[512,512]{1,0:T(8,128)(2,1)}, u32[]{:S(2)}) copy-start(bf16[512,512]{1,0:T(8,128)(2,1)} %refs_1_.2) | copy-start | bytes 1572868
  34.2 13.2 %collective-permute-start.9 = (bf16[640,512]{1,0:T(8,128)(2,1)S(1)}, bf16[640,512]{1,0:T(8,128)(2,1)S(1)}, u32[]{:S(2)}, u32[]{:S(2)}) collective-permute-start(bf16[640,512]{1,0:T(8,128)(2,1)S(1)} %get-tuple-element.62.refs_0_.q_ref), channel_id=1, source_target_pairs={{0,1},{1,0},{2,3},{3,2},{4,5},{5,4},{6,7},{7,6},{8,9},{9,8},{10,11... | collective-permute-start | bytes 1966088 | tf_op jit(solution)/shard_map/ppermute | solution.py:320
  36.2 8.7 %collective-permute-start.10 = (bf16[512,512]{1,0:T(8,128)(2,1)S(1)}, bf16[512,512]{1,0:T(8,128)(2,1)S(1)}, u32[]{:S(2)}, u32[]{:S(2)}) collective-permute-start(bf16[512,512]{1,0:T(8,128)(2,1)S(1)} %collective-permute-done.1.far_ref.refs_2_), channel_id=1, source_target_pairs={{0,2},{1,15},{2,4},{3,1},{4,6},{5,3},{6,8},{7,5},{8,10},{9,7},{10,... | collective-permute-start | bytes 1572872 | tf_op jit(solution)/shard_map/ppermute | solution.py:320
  39.3 20.0 %collective-permute-start.7 = (bf16[256,512]{1,0:T(8,128)(2,1)S(1)}, bf16[256,512]{1,0:T(8,128)(2,1)S(1)}, u32[]{:S(2)}, u32[]{:S(2)}) collective-permute-start(bf16[256,512]{1,0:T(8,128)(2,1)S(1)} %get-tuple-element.115), channel_id=1, source_target_pairs={{0,2},{1,15},{2,4},{3,1},{4,6},{5,3},{6,8},{7,5},{8,10},{9,7},{10,... | collective-permute-start | bytes 786440 | tf_op jit(solution)/shard_map/ppermute | solution.py:320
  41.9 17.5 %collective-permute-start.5 = (bf16[256,512]{1,0:T(8,128)(2,1)S(1)}, bf16[256,512]{1,0:T(8,128)(2,1)S(1)}, u32[]{:S(2)}, u32[]{:S(2)}) collective-permute-start(bf16[256,512]{1,0:T(8,128)(2,1)S(1)} %get-tuple-element.116), channel_id=1, source_target_pairs={{0,2},{1,15},{2,4},{3,1},{4,6},{5,3},{6,8},{7,5},{8,10},{9,7},{10,... | collective-permute-start | bytes 786440 | tf_op jit(solution)/shard_map/ppermute | solution.py:320
  44.8 15.0 %collective-permute-start.11 = (bf16[512,512]{1,0:T(8,128)(2,1)S(1)}, bf16[512,512]{1,0:T(8,128)(2,1)S(1)}, u32[]{:S(2)}, u32[]{:S(2)}) collective-permute-start(bf16[512,512]{1,0:T(8,128)(2,1)S(1)} %collective-permute-done.10.refs_2_), channel_id=1, source_target_pairs={{0,2},{1,15},{2,4},{3,1},{4,6},{5,3},{6,8},{7,5},{8,10},{9,7},{10,... | collective-permute-start | bytes 1572872 | tf_op jit(solution)/shard_map/ppermute | solution.py:320
  55.1 7.1 %slice-start = ((s8[4718592]{0:T(1024)(128)(4,1)}), s8[4194304]{0:T(1024)(128)(4,1)S(1)}, s32[]{:S(2)}) async-start(s8[4718592]{0:T(1024)(128)(4,1)} %bitcast.16), calls=%async_computation.2 | async-start | bytes 8388608
  57.2 5.0 %slice-start.1 = ((s8[4718592]{0:T(1024)(128)(4,1)}), s8[524288]{0:T(1024)(128)(4,1)S(1)}, s32[]{:S(2)}) async-start(s8[4718592]{0:T(1024)(128)(4,1)} %bitcast.16), calls=%async_computation.3 | async-start | bytes 1048576
  59.2 4.3 %collective-permute-start.8 = (bf16[256,512]{1,0:T(8,128)(2,1)S(1)}, bf16[256,512]{1,0:T(8,128)(2,1)S(1)}, u32[]{:S(2)}, u32[]{:S(2)}) collective-permute-start(bf16[256,512]{1,0:T(8,128)(2,1)S(1)} %collective-permute-done.7.refs_1_), channel_id=1, source_target_pairs={{0,1},{1,0},{2,3},{3,2},{4,5},{5,4},{6,7},{7,6},{8,9},{9,8},{10,11... | collective-permute-start | bytes 786440 | tf_op jit(solution)/shard_map/ppermute | solution.py:320
  59.3 5.3 %collective-permute-start.6 = (bf16[256,512]{1,0:T(8,128)(2,1)S(1)}, bf16[256,512]{1,0:T(8,128)(2,1)S(1)}, u32[]{:S(2)}, u32[]{:S(2)}) collective-permute-start(bf16[256,512]{1,0:T(8,128)(2,1)S(1)} %collective-permute-done.5.refs_2_), channel_id=1, source_target_pairs={{0,1},{1,0},{2,3},{3,2},{4,5},{5,4},{6,7},{7,6},{8,9},{9,8},{10,11... | collective-permute-start | bytes 786440 | tf_op jit(solution)/shard_map/ppermute | solution.py:320
  59.8 2.3 %copy-start.6 = (bf16[512,512]{1,0:T(8,128)(2,1)S(1)}, bf16[512,512]{1,0:T(8,128)(2,1)}, u32[]{:S(2)}) copy-start(bf16[512,512]{1,0:T(8,128)(2,1)} %refs_0_.3) | copy-start | bytes 1572868
  59.8 2.3 %copy-start.7 = (bf16[512,512]{1,0:T(8,128)(2,1)S(1)}, bf16[512,512]{1,0:T(8,128)(2,1)}, u32[]{:S(2)}) copy-start(bf16[512,512]{1,0:T(8,128)(2,1)} %refs_1_.3) | copy-start | bytes 1572868
  61.8 3.6 %collective-permute-start.12 = (f32[640,640]{1,0:T(8,128)S(1)}, f32[640,640]{1,0:T(8,128)S(1)}, u32[]{:S(2)}, u32[]{:S(2)}) collective-permute-start(f32[640,640]{1,0:T(8,128)S(1)} %get-tuple-element.108), channel_id=1, source_target_pairs={{0,1},{1,0},{2,3},{3,2},{4,5},{5,4},{6,7},{7,6},{8,9},{9,8},{10,11... | collective-permute-start | bytes 4915208 | tf_op jit(solution)/shard_map/ppermute | solution.py:320
  65.4 16.2 %copy-start.8 = (f32[512]{0:T(512)S(1)}, f32[512]{0:T(512)}, u32[]{:S(2)}) copy-start(f32[512]{0:T(512)} %param.18) | copy-start | bytes 6148
  65.4 16.2 %copy-start.9 = (f32[512]{0:T(512)S(1)}, f32[512]{0:T(512)}, u32[]{:S(2)}) copy-start(f32[512]{0:T(512)} %param.19) | copy-start | bytes 6148
  65.4 16.2 %copy-start.10 = (f32[512]{0:T(512)S(1)}, f32[512]{0:T(512)}, u32[]{:S(2)}) copy-start(f32[512]{0:T(512)} %param.21) | copy-start | bytes 6148
  67.4 14.1 %collective-permute-start.13 = (bf16[128,512]{1,0:T(8,128)(2,1)S(1)}, bf16[128,512]{1,0:T(8,128)(2,1)S(1)}, u32[]{:S(2)}, u32[]{:S(2)}) collective-permute-start(bf16[128,512]{1,0:T(8,128)(2,1)S(1)} %get-tuple-element.112), channel_id=1, source_target_pairs={{0,1},{1,0},{2,3},{3,2},{4,5},{5,4},{6,7},{7,6},{8,9},{9,8},{10,11... | collective-permute-start | bytes 393224 | tf_op jit(solution)/shard_map/ppermute | solution.py:320
